TPU v7x, 8 devices: a whole 2x2x1 slice. The times are simulated.
8 devices in a mesh: dp: 1 (over z), tx: 2 (over y), ty: 4 (over x, core).
Axes of the slice: x: 2, y: 2, z: 1, core: 2. Of those that a mesh axis runs over, the one named last changes fastest.
Arguments:
- residual: float32 [512, 2560], P('dp', 'tx')
- norm_w: float32 [2, 2560], P(None, 'tx')
- w_in: bfloat16 [2, 2560, 2, 5120], P(None, 'tx', None, 'ty')
- conv_w: float32 [2, 5120, 4], P(None, 'ty')
- conv_b: float32 [2, 5120], P(None, 'ty')
- w_x: bfloat16 [2, 5120, 192], P(None, 'ty')
- w_dt: bfloat16 [2, 160, 5120], P(None, None, 'ty')
- dt_bias: float32 [2, 5120], P(None, 'ty')
- a_log: float32 [2, 5120, 16], P(None, 'ty')
- d_skip: float32 [2, 5120], P(None, 'ty')
- w_out: bfloat16 [2, 5120, 2560], P(None, 'ty', 'tx')
- conv_state: bfloat16 [2, 512, 5120, 3], P(None, ('dp', 'tx'), 'ty')
- ssm_state: float32 [2, 512, 5120, 16], P(None, ('dp', 'tx'), 'ty')
Outputs:
- output 1: float32 [512, 2560], P('dp', 'tx')
- output 2: bfloat16 [2, 512, 5120, 3], P(None, ('dp', 'tx'), 'ty')
- output 3: float32 [2, 512, 5120, 16], P(None, ('dp', 'tx'), 'ty')
All inputs are finite; a program needn't handle non-finite values.
Results may differ from a plain program's by a relative error of at most 0.0142533.
Values are sent between devices in bfloat16 or wider.
A program may use at most 1 GiB of HBM per device.

v0:
```python
import jax
import jax.numpy as jnp
from jax import lax
from jax.sharding import PartitionSpec as P

NORM_EPS = 1e-5
INNER_EPS = 1e-6


def unit_rms(vec):
    return vec * lax.rsqrt(jnp.mean(vec * vec, axis=-1, keepdims=True) + INNER_EPS)


def channel_update(x_branch, z_branch, conv_prev, ssm_prev, conv_w, conv_b, w_x, w_dt, dt_bias, a_log, d_skip, reduce_fn):
    n_rank = w_dt.shape[0]
    n_state = a_log.shape[-1]
    window = jnp.concatenate([conv_prev, x_branch[:, :, None]], axis=-1)
    conv_val = jnp.sum(window.astype(jnp.float32) * conv_w, axis=-1) + conv_b
    x_conv = jax.nn.silu(conv_val).astype(jnp.bfloat16)
    x_dbl = reduce_fn(jnp.dot(x_conv, w_x, preferred_element_type=jnp.float32))
    dt_low = unit_rms(x_dbl[:, :n_rank])
    b_mat = unit_rms(x_dbl[:, n_rank:n_rank + n_state])
    c_mat = unit_rms(x_dbl[:, n_rank + n_state:])
    delta = jax.nn.softplus(jnp.dot(dt_low.astype(jnp.bfloat16), w_dt, preferred_element_type=jnp.float32) + dt_bias)
    x_float = x_conv.astype(jnp.float32)
    decay = jnp.exp(delta[:, :, None] * -jnp.exp(a_log))
    ssm_new = decay * ssm_prev + (delta * x_float)[:, :, None] * b_mat[:, None, :]
    state_val = jnp.sum(ssm_new * c_mat[:, None, :], axis=-1)
    gated = ((state_val + d_skip * x_float) * jax.nn.silu(z_branch.astype(jnp.float32))).astype(jnp.bfloat16)
    return gated, window[:, :, 1:], ssm_new


def solution(mesh):
    n_dmod = mesh.shape["tx"]

    def sum_over_ty(part_sum):
        return lax.psum(part_sum.astype(jnp.bfloat16), "ty").astype(jnp.float32)

    def local_step(residual, norm_w, w_in, conv_w, conv_b, w_x, w_dt, dt_bias, a_log, d_skip, w_out, conv_state, ssm_state):
        d_model = residual.shape[1] * n_dmod
        conv_list = []
        ssm_list = []
        for layer_idx in range(norm_w.shape[0]):
            sq_part = jnp.sum(residual * residual, axis=-1, keepdims=True)
            sq_total = lax.psum(sq_part, "tx")
            normed = (residual * lax.rsqrt(sq_total / d_model + NORM_EPS) * norm_w[layer_idx]).astype(jnp.bfloat16)
            proj_part = jnp.einsum("bd,dke->bke", normed, w_in[layer_idx], preferred_element_type=jnp.float32)
            proj_in = lax.psum_scatter(proj_part.astype(jnp.bfloat16), "tx", scatter_dimension=0, tiled=True)
            gated, conv_new, ssm_new = channel_update(proj_in[:, 0, :], proj_in[:, 1, :], conv_state[layer_idx], ssm_state[layer_idx], conv_w[layer_idx], conv_b[layer_idx], w_x[layer_idx], w_dt[layer_idx], dt_bias[layer_idx], a_log[layer_idx], d_skip[layer_idx], sum_over_ty)
            gated_rows = lax.all_gather(gated, "tx", axis=0, tiled=True)
            out_part = jnp.dot(gated_rows, w_out[layer_idx], preferred_element_type=jnp.float32)
            residual = residual + sum_over_ty(out_part)
            conv_list.append(conv_new)
            ssm_list.append(ssm_new)
        return residual, jnp.stack(conv_list), jnp.stack(ssm_list)

    cache_spec = P(None, ("dp", "tx"), "ty", None)
    in_specs = (P("dp", "tx"), P(None, "tx"), P(None, "tx", None, "ty"), P(None, "ty", None), P(None, "ty"), P(None, "ty", None), P(None, None, "ty"), P(None, "ty"), P(None, "ty", None), P(None, "ty"), P(None, "ty", "tx"), cache_spec, cache_spec)
    out_specs = (P("dp", "tx"), cache_spec, cache_spec)
    return jax.shard_map(local_step, mesh=mesh, in_specs=in_specs, out_specs=out_specs, check_vma=False)
```

profile of v0, /device:TPU:0, one launch (start us, length us, event | category | flops | bytes accessed | tf_op | source)
XLA Modules:
  0.0 373.4 jit_solution(7130820632059308490)
XLA Ops:
  7.2 0.0 reduce-scatter.3.cloned.1.call-start
  7.2 2.0 multiply_reduce_fusion.3
  9.2 6.3 %psum.42 = f32[512,1]{0,1:T(1,128)S(1)} all-reduce(f32[512,1]{0,1:T(1,128)S(1)} %bitcast.97), channel_id=1, replica_groups=mesh['dp'=1,'tx'=2,'ty'=4] {'tx'}, use_global_device_ids=true, to_apply=%region_1.0 | all-reduce | flops 512 | bytes 4096 | tf_op jit(solution)/shard_map/psum | solution.py:45
  15.5 0.6 slice_reduce_fusion.7
  16.1 11.6 %fusion.56 = (bf16[1,1280,2,1280]{3,2,1,0:T(2,128)(2,1)S(1)}, bf16[1,1280,2,1280]{3,2,1,0:T(2,128)(2,1)}) fusion(bf16[2,1280,2,1280]{3,2,1,0:T(2,128)(2,1)} %param.15), kind=kLoop, calls=%fused_computation.126 | loop fusion | bytes 26214400 | tf_op jit(solution)/shard_map/slice | solution.py:47
  27.8 4.9 %fusion.8 = bf16[512,2,1280]{2,0,1:T(8,128)(2,1)} fusion(bf16[1,1280,2,1280]{3,2,1,0:T(2,128)(2,1)S(1)} %get-tuple-element.17, f32[512,1280]{1,0:T(8,128)S(1)} %copy-done, f32[1280]{0:T(1024)S(1)} %get-tuple-element.13, f32[512]{0:T(512)S(1)} %bitcast.98), kind=kOutput, calls=%fused_computation.20 | convolution fusion | flops 3358720000 | bytes 11803648 | tf_op jit(solution)/shard_map/bd,dke->bke/dot_general | solution.py:47
  32.7 0.0 reduce-scatter.3.cloned.1.call-update
  32.8 0.0 all-reduce.5.cloned.1.call-start
  32.8 0.6 copy-done.22
  33.5 0.6 slice_reduce_fusion.1
  34.1 0.7 negate_bitcast_fusion
  34.8 4.3 %slice_bitcast_fusion = (bf16[256,1280,3]{1,0,2:T(8,128)(2,1)}, bf16[256,1280,3]{1,0,2:T(8,128)(2,1)}) fusion(bf16[2,256,1280,3]{2,1,3,0:T(8,128)(2,1)} %param.24), kind=kLoop, calls=%fused_computation.48 | loop fusion | bytes 7864320 | tf_op jit(solution)/shard_map/squeeze | solution.py:49
  39.1 30.1 %reduce-scatter.3.cloned.1.call-done = bf16[256,2,1280]{2,0,1:T(8,128)(2,1)} async-done(((bf16[512,2,1280]{2,0,1:T(8,128)(2,1)}), bf16[256,2,1280]{2,0,1:T(8,128)(2,1)}) %reduce-scatter.3.cloned.1.call-update) | async-done | bytes 1310736 | tf_op jit(solution)/shard_map/reduce_scatter | solution.py:48
  69.2 1.1 slice_bitcast_fusion.5
  70.3 2.3 multiply_reduce_fusion.1
  72.6 1.0 copy-done.4
  73.6 0.4 multiply_convert_fusion.3
  74.1 0.8 copy-done.15
  74.9 1.0 convolution_convert_fusion.1
  75.9 0.0 all-reduce.5.cloned.1.call-update
  76.0 0.0 all-gather.3.cloned.1.call-start
  76.0 0.6 slice_reduce_fusion
  76.6 25.5 %all-reduce.5.cloned.1.call-done = bf16[256,192]{0,1:T(8,128)(2,1)} async-done(((bf16[256,192]{0,1:T(8,128)(2,1)}), bf16[256,192]{0,1:T(8,128)(2,1)}) %all-reduce.5.cloned.1.call-update) | async-done | bytes 98320 | tf_op jit(solution)/shard_map/psum | solution.py:37
  102.2 0.9 convert_element_type.83
  103.2 0.6 slice_multiply_fusion.3
  103.8 0.8 copy.25
  104.6 0.8 copy.26
  105.4 2.3 convert_multiply_fusion.5
  107.8 17.1 %fusion.5 = f32[256,1280]{1,0:T(8,128)S(1)} fusion(f32[2,256,1280,16]{2,3,1,0:T(8,128)} %param.25, f32[256,16]{1,0:T(8,128)S(1)} %copy-done.17, f32[256,16]{1,0:T(8,128)S(1)} %copy.25, f32[256,1280]{1,0:T(8,128)S(1)} %get-tuple-element.29, f32[1280,16]{0,1:T(8,128)S(1)} %copy-done.13, f32[256,1280]{1,0:T(8,128)S(1)} %get-tuple-element.30), kind=kLoop, calls=%fused_computation.8 | loop fusion | flops 31129600 | bytes 25018368 | tf_op jit(solution)/shard_map/reduce_sum | solution.py:28
  124.9 1.7 fusion.28
  126.6 0.0 all-gather.3.cloned.1.call-update
  126.6 0.0 all-reduce.7.cloned.1.call-start
  126.7 21.2 %all-gather.3.cloned.1.call-done = bf16[512,1280]{1,0:T(8,128)(2,1)} async-done(((bf16[256,1280]{1,0:T(8,128)(2,1)}), bf16[512,1280]{1,0:T(8,128)(2,1)}) %all-gather.3.cloned.1.call-update) | async-done | bytes 1310736 | tf_op jit(solution)/shard_map/all_gather | solution.py:50
  147.9 5.2 %fusion.16 = bf16[512,1280]{1,0:T(8,128)(2,1)} fusion(bf16[512,1280]{1,0:T(8,128)(2,1)} %all-gather.3.cloned.1.call-done, bf16[2,1280,1280]{2,1,0:T(8,128)(2,1)} %param.23), kind=kOutput, calls=%fused_computation.32 | convolution fusion | flops 1678376960 | bytes 5898240 | tf_op jit(solution)/shard_map/dot_general | solution.py:51
  153.2 0.0 reduce-scatter.5.cloned.1.call-start
  153.2 33.8 %all-reduce.7.cloned.1.call-done = bf16[512,1280]{1,0:T(8,128)(2,1)} async-done(((bf16[512,1280]{1,0:T(8,128)(2,1)}), bf16[512,1280]{1,0:T(8,128)(2,1)}) %all-reduce.7.cloned.1.call-update) | async-done | bytes 1310736 | tf_op jit(solution)/shard_map/psum | solution.py:37
  187.1 1.7 multiply_reduce_fusion.2
  188.8 5.1 %psum.45 = f32[512,1]{0,1:T(1,128)S(1)} all-reduce(f32[512,1]{0,1:T(1,128)S(1)} %bitcast.96), channel_id=1, replica_groups=mesh['dp'=1,'tx'=2,'ty'=4] {'tx'}, use_global_device_ids=true, to_apply=%region_11.12 | all-reduce | flops 512 | bytes 4096 | tf_op jit(solution)/shard_map/psum | solution.py:45
  193.9 8.4 %fusion.9 = bf16[512,2,1280]{2,0,1:T(8,128)(2,1)} fusion(bf16[1,1280,2,1280]{3,2,1,0:T(2,128)(2,1)} %get-tuple-element.18, f32[1280]{0:T(1024)S(1)} %copy-done.26, f32[512]{0:T(512)S(1)} %bitcast.99, f32[512,1280]{1,0:T(8,128)S(1)} %copy-done, bf16[512,1280]{1,0:T(8,128)(2,1)} %all-reduce.7.cloned.1.call-done), kind=kOutput, calls=%fused_computation.21 | convolution fusion | flops 3360030720 | bytes 13114368 | tf_op jit(solution)/shard_map/bd,dke->bke/dot_general | solution.py:47
  202.4 0.0 all-reduce.9.cloned.1.call-start
  202.4 2.8 fusion.25
  205.2 32.1 %reduce-scatter.5.cloned.1.call-done = bf16[256,2,1280]{2,0,1:T(8,128)(2,1)} async-done(((bf16[512,2,1280]{2,0,1:T(8,128)(2,1)}), bf16[256,2,1280]{2,0,1:T(8,128)(2,1)}) %reduce-scatter.5.cloned.1.call-update) | async-done | bytes 1310736 | tf_op jit(solution)/shard_map/reduce_scatter | solution.py:48
  237.3 1.1 slice_bitcast_fusion.3
  238.4 2.9 fusion.23
  241.3 0.5 multiply_reduce_fusion
  241.9 1.0 copy-done.2
  242.9 0.4 multiply_convert_fusion.2
  243.4 0.9 copy-done.16
  244.2 1.0 convolution_convert_fusion
  245.3 0.0 all-gather.5.cloned.1.call-start
  245.3 4.4 %pad_maximum_fusion.1 = bf16[2,256,1280,3]{2,1,3,0:T(8,128)(2,1)} fusion(bf16[1,256,1280,3]{2,1,3,0:T(8,128)(2,1)} %fusion.23, bf16[1,256,1280,3]{2,1,3,0:T(8,128)(2,1)} %fusion.25), kind=kLoop, calls=%fused_computation.17 | loop fusion | flops 1966080 | bytes 7864320 | tf_op jit(solution)/shard_map/stack | solution.py:55
  249.8 21.7 %all-reduce.9.cloned.1.call-done = bf16[256,192]{0,1:T(8,128)(2,1)} async-done(((bf16[256,192]{0,1:T(8,128)(2,1)}), bf16[256,192]{0,1:T(8,128)(2,1)}) %all-reduce.9.cloned.1.call-update) | async-done | bytes 98320 | tf_op jit(solution)/shard_map/psum | solution.py:37
  271.5 0.9 convert_element_type.96
  272.5 0.1 copy.28
  272.6 0.1 copy.29
  272.7 2.2 convert_multiply_fusion.3
  275.0 17.1 %fusion.2 = f32[256,1280]{1,0:T(8,128)S(1)} fusion(f32[2,256,1280,16]{2,3,1,0:T(8,128)} %param.25, f32[256,16]{1,0:T(8,128)S(1)} %copy.29, f32[256,16]{1,0:T(8,128)S(1)} %copy.28, f32[256,1280]{1,0:T(8,128)S(1)} %get-tuple-element.31, f32[1280,16]{0,1:T(8,128)S(1)} %get-tuple-element.25, f32[256,1280]{1,0:T(8,128)S(1)} %get-tuple-element.32), kind=kLoop, calls=%fused_computation.4 | loop fusion | flops 31129600 | bytes 25018368 | tf_op jit(solution)/shard_map/reduce_sum | solution.py:28
  292.2 1.7 fusion.31
  293.9 0.3 all-reduce.11.cloned.1.call-start
  294.2 29.7 %multiply_add_fusion.1 = (f32[1,256,1280,16]{2,3,1,0:T(8,128)}, f32[1,256,1280,16]{2,3,1,0:T(8,128)}) fusion(f32[2,256,1280,16]{2,3,1,0:T(8,128)} %param.25, f32[256,16]{1,0:T(8,128)S(1)} %copy.25, f32[256,1280]{1,0:T(8,128)} %copy-done.6, f32[1280,16]{0,1:T(8,128)S(1)} %copy-done.14, f32[256,1280]{1,0:T(8,128)} %copy-done.7, f32[256,16]{1,0:T(8,128)S(1)} %copy.28, ...), kind=kLoop, calls=%fused_computation.10 | loop fusion | flops 41943040 | bytes 89325568 | tf_op jit(solution)/shard_map/add | solution.py:27
  323.9 5.2 %fusion.19 = bf16[512,1280]{1,0:T(8,128)(2,1)} fusion(bf16[512,1280]{1,0:T(8,128)(2,1)} %all-gather.5.cloned.1.call-done, bf16[2,1280,1280]{2,1,0:T(8,128)(2,1)} %param.23), kind=kOutput, calls=%fused_computation.33 | convolution fusion | flops 1678376960 | bytes 5898240 | tf_op jit(solution)/shard_map/dot_general | solution.py:51
  329.2 29.1 %pad_maximum_fusion = f32[2,256,1280,16]{2,3,1,0:T(8,128)} fusion(f32[1,256,1280,16]{2,3,1,0:T(8,128)} %get-tuple-element.16, f32[1,256,1280,16]{2,3,1,0:T(8,128)} %get-tuple-element.15), kind=kLoop, calls=%fused_computation | loop fusion | flops 10485760 | bytes 83886080 | tf_op jit(solution)/shard_map/stack | solution.py:55
  358.2 4.8 %all-reduce.11.cloned.1.call-done = bf16[512,1280]{1,0:T(8,128)(2,1)} async-done(((bf16[512,1280]{1,0:T(8,128)(2,1)}), bf16[512,1280]{1,0:T(8,128)(2,1)}) %all-reduce.11.cloned.1.call-update) | async-done | bytes 1310736 | tf_op jit(solution)/shard_map/psum | solution.py:37
  363.0 3.5 convert_add_fusion
  (73 shorter events, 0.4 us)
Async XLA Ops:
  7.2 8.3 %copy-start.21 = (f32[2,1280]{1,0:T(2,128)S(1)}, f32[2,1280]{1,0:T(2,128)}, u32[]{:S(2)}) copy-start(f32[2,1280]{1,0:T(2,128)} %param.14) | copy-start | bytes 30724
  7.2 62.0 %reduce-scatter.3.cloned.1.call-start = ((), (), s32[]{:S(2)}) async-start(), calls=%async_computation.2 | async-start | bytes 3932160 | tf_op jit(solution)/shard_map/reduce_scatter | solution.py:48
  16.1 11.6 %copy-start = (f32[512,1280]{1,0:T(8,128)S(1)}, f32[512,1280]{1,0:T(8,128)}, u32[]{:S(2)}) copy-start(f32[512,1280]{1,0:T(8,128)} %param.13) | copy-start | bytes 7864324
  32.7 0.7 copy-start.22
  32.7 0.7 copy-start.23
  32.7 1.4 copy-start.19
  32.7 1.4 copy-start.18
  32.8 69.4 %all-reduce.5.cloned.1.call-start = ((), (), s32[]{:S(2)}) async-start(), calls=%async_computation.3 | async-start | bytes 196608 | tf_op jit(solution)/shard_map/psum | solution.py:37
  72.6 1.1 copy-start.4
  72.6 2.3 copy-start.27
  72.6 3.4 copy-start.24
  74.1 0.8 copy-start.15
  76.0 72.0 %all-gather.3.cloned.1.call-start = ((), (), s32[]{:S(2)}) async-start(), calls=%async_computation.4 | async-start | bytes 1966080 | tf_op jit(solution)/shard_map/all_gather | solution.py:50
  103.1 0.7 copy-start.12
  105.4 2.4 copy-start.13
  105.4 2.4 copy-start.17
  107.7 17.2 %copy-start.6 = (f32[256,1280]{1,0:T(8,128)}, f32[256,1280]{1,0:T(8,128)S(1)}, u32[]{:S(2)}) copy-start(f32[256,1280]{1,0:T(8,128)S(1)} %get-tuple-element.29) | copy-start | bytes 3932164
  107.7 17.2 %copy-start.7 = (f32[256,1280]{1,0:T(8,128)}, f32[256,1280]{1,0:T(8,128)S(1)}, u32[]{:S(2)}) copy-start(f32[256,1280]{1,0:T(8,128)S(1)} %get-tuple-element.30) | copy-start | bytes 3932164
  107.8 17.1 %copy-start.5 = (f32[256,1280]{1,0:T(8,128)S(1)}, f32[256,1280]{1,0:T(8,128)}, u32[]{:S(2)}) copy-start(f32[256,1280]{1,0:T(8,128)} %copy-done.4) | copy-start | bytes 3932164
  107.8 17.1 %copy-start.10 = (bf16[256,2,1280]{2,0,1:T(8,128)(2,1)S(1)}, bf16[256,2,1280]{2,0,1:T(8,128)(2,1)}, u32[]{:S(2)}) copy-start(bf16[256,2,1280]{2,0,1:T(8,128)(2,1)} %reduce-scatter.3.cloned.1.call-done) | copy-start | bytes 3932164
  107.8 17.1 %copy-start.20 = (f32[1280]{0:T(1024)S(1)}, f32[1280]{0:T(1024)}, u32[]{:S(2)}) copy-start(f32[1280]{0:T(1024)} %get-tuple-element.8) | copy-start | bytes 15364
  126.6 60.4 %all-reduce.7.cloned.1.call-start = ((), (), s32[]{:S(2)}) async-start(), calls=%async_computation.5 | async-start | bytes 2621440 | tf_op jit(solution)/shard_map/psum | solution.py:37
  153.2 40.7 %copy-start.26 = (f32[1280]{0:T(1024)S(1)}, f32[1280]{0:T(1024)}, u32[]{:S(2)}) copy-start(f32[1280]{0:T(1024)} %get-tuple-element.14) | copy-start | bytes 15364
  153.2 84.1 %reduce-scatter.5.cloned.1.call-start = ((), (), s32[]{:S(2)}) async-start(), calls=%async_computation.6 | async-start | bytes 3932160 | tf_op jit(solution)/shard_map/reduce_scatter | solution.py:48
  202.4 69.1 %all-reduce.9.cloned.1.call-start = ((), (), s32[]{:S(2)}) async-start(), calls=%async_computation.7 | async-start | bytes 196608 | tf_op jit(solution)/shard_map/psum | solution.py:37
  238.4 2.9 copy-start.1
  241.9 1.1 copy-start.2
  241.9 2.4 copy-start.28
  243.4 0.9 copy-start.16
  245.3 27.4 %copy-start.25 = (f32[1280]{0:T(1024)S(1)}, f32[1280]{0:T(1024)}, u32[]{:S(2)}) copy-start(f32[1280]{0:T(1024)} %get-tuple-element.9) | copy-start | bytes 15364
  245.3 78.6 %all-gather.5.cloned.1.call-start = ((), (), s32[]{:S(2)}) async-start(), calls=%async_computation.8 | async-start | bytes 1966080 | tf_op jit(solution)/shard_map/all_gather | solution.py:50
  275.0 17.2 %copy-start.8 = (f32[256,1280]{1,0:T(8,128)}, f32[256,1280]{1,0:T(8,128)S(1)}, u32[]{:S(2)}) copy-start(f32[256,1280]{1,0:T(8,128)S(1)} %get-tuple-element.31) | copy-start | bytes 3932164
  275.0 17.2 %copy-start.9 = (f32[256,1280]{1,0:T(8,128)}, f32[256,1280]{1,0:T(8,128)S(1)}, u32[]{:S(2)}) copy-start(f32[256,1280]{1,0:T(8,128)S(1)} %get-tuple-element.32) | copy-start | bytes 3932164
  275.0 17.2 %copy-start.3 = (f32[256,1280]{1,0:T(8,128)S(1)}, f32[256,1280]{1,0:T(8,128)}, u32[]{:S(2)}) copy-start(f32[256,1280]{1,0:T(8,128)} %copy-done.2) | copy-start | bytes 3932164
  275.0 17.2 %copy-start.11 = (bf16[256,2,1280]{2,0,1:T(8,128)(2,1)S(1)}, bf16[256,2,1280]{2,0,1:T(8,128)(2,1)}, u32[]{:S(2)}) copy-start(bf16[256,2,1280]{2,0,1:T(8,128)(2,1)} %reduce-scatter.5.cloned.1.call-done) | copy-start | bytes 3932164
  292.1 2.0 copy-start.14
  293.9 69.1 %all-reduce.11.cloned.1.call-start = ((), (), s32[]{:S(2)}) async-start(), calls=%async_computation.9 | async-start | bytes 2621440 | tf_op jit(solution)/shard_map/psum | solution.py:37
Sparse Core Ops, SparseCore 0:
  32.9 36.2 reduce-scatter.2
  76.1 26.0 all-reduce.4
  126.8 21.1 all-gather.2
  153.3 33.7 all-reduce.6
  202.5 34.7 reduce-scatter.4
  245.4 26.0 all-reduce.8
  294.0 21.1 all-gather.4
  329.3 33.7 all-reduce.10
where the time goes:
time: 374 us; the launch traced here: 373 us
  waiting for transfers between devices  169 us (45%)
  other arithmetic  121 us (32%)
  matrix products  30.5 us (8%)
  local copies, waits for them, and re-layouts  26.4 us (7%)
  between operations  14.6 us (4%)
  blocking collectives  11.4 us (3%)
    psum x4, waiting for transfers between devices, sum_over_ty(): return lax.psum(part_sum.astype(jnp.bfloat16), 'ty').astype(jnp.float32)  85.9 us
    reduce_scatter x2, waiting for transfers between devices, local_step(): lax.psum_scatter(proj_part.astype(jnp.bfloat16), 'tx', scatter_dimension=...  62.2 us
    another operation x4, other arithmetic, local_step(): return (residual, jnp.stack(conv_list), jnp.stack(ssm_list))  39.2 us
    reduce_sum x2, other arithmetic, channel_update(): state_val = jnp.sum(ssm_new * c_mat[:, None, :], axis=-1)  34.2 us
    add x1, other arithmetic, channel_update(): decay * ssm_prev + (delta * x_float)[:, :, None] * b_mat[:, None, :]  29.7 us
    all_gather x2, waiting for transfers between devices, local_step(): gated_rows = lax.all_gather(gated, 'tx', axis=0, tiled=True)  21.2 us
    dot_general x2, matrix products, local_step(): jnp.einsum('bd,dke->bke', normed, w_in[layer_idx], preferred_element_type...  13.4 us
    slice x1, local copies, waits for them, and re-layouts, local_step(): w_in[layer_idx]  11.6 us
  transfers between devices with their start and end apart: 8, of which 7 were waited for; matrix products, arithmetic and copies ran while one was open for 19% of the time, Pallas kernels for 0%

commit v1 on v0

v1 whole, which is shorter than its diff:
```python
import functools
import jax
import jax.numpy as jnp
from jax import lax
from jax.experimental import pallas as pl
from jax.experimental.pallas import tpu as pltpu
from jax.sharding import PartitionSpec as P

NORM_EPS = 1e-5
INNER_EPS = 1e-6
LOG2E = 1.4426950408889634
N_CHUNK = 4
BF = jnp.bfloat16
F32 = jnp.float32
MESH = pl.DeviceIdType.MESH


def step_kernel(dims, res_hbm, norm_w, w_in_hbm, conv_w, conv_b, w_x, w_dt, dt_bias, a_log, d_skip, w_out_hbm, conv_hbm, ssm_hbm,
                r_ref, conv_out, ssm_out,
                w_in, w_out, a_neg, ssm_buf, conv_buf, h_buf, u_own, z_buf, x_buf, dt_buf, dtx_buf, y_buf, b_bc, c_bc, o_buf,
                st_send, st_recv, u_send, u_recv, p_own, p_send, p_recv, g_all, cr_send, cr_recv, xs_send, xs_recv, ag_send, ag_recv,
                in_sem, ssm_in_sem, ssm_out_sem, conv_in_sem, conv_out_sem,
                st_s, st_r, u_s, u_r, p_s, p_r, g_s, g_r, cr_s, cr_r, xs_s, xs_r, ag_s, ag_r):
    n_layer, rows, d_loc, e_loc, n_state, n_rank, d_model = dims
    half = rows // 2
    n_chunk = N_CHUNK
    blk = half // n_chunk
    total = n_layer * n_chunk
    tx = lax.axis_index("tx")
    ty = lax.axis_index("ty")
    core = lax.rem(ty, 2)
    chip = lax.div(ty, 2)
    y_peer = {"tx": 1 - tx, "ty": ty}
    core_peer = {"tx": tx, "ty": chip * 2 + (1 - core)}
    x_peer = {"tx": tx, "ty": (1 - chip) * 2 + core}
    d_peer = {"tx": tx, "ty": (1 - chip) * 2 + (1 - core)}

    def layer_of(i):
        return lax.div(i, n_chunk)

    def chunk_of(i):
        return lax.rem(i, n_chunk)

    def part_rows(i, part):
        side = jnp.where(part == 0, tx, 1 - tx)
        return pl.multiple_of(side * half + chunk_of(i) * blk, blk)

    def remote(src, dst, s_sem, r_sem, dev):
        return pltpu.make_async_remote_copy(src_ref=src, dst_ref=dst, send_sem=s_sem, recv_sem=r_sem, device_id=dev, device_id_type=MESH)

    def st_copy(i):
        return remote(st_send.at[i], st_recv.at[i], st_s.at[i], st_r.at[i], y_peer)

    def u_copy(i, k):
        s = lax.rem(i, 2)
        return remote(u_send.at[s, k], u_recv.at[i, k], u_s.at[s, k], u_r.at[i, k], y_peer)

    def p_copy(i, q):
        s = lax.rem(i, 2)
        dev = (core_peer, x_peer, d_peer)[q]
        return remote(p_send.at[s], p_recv.at[i, q], p_s.at[s, q], p_r.at[i, q], dev)

    def g_copy(i):
        return remote(g_all.at[i, pl.ds(0, blk)], g_all.at[i, pl.ds(blk, blk)], g_s.at[i], g_r.at[i], y_peer)

    def cr_copy(i):
        return remote(cr_send.at[i], cr_recv.at[i], cr_s.at[i], cr_r.at[i], core_peer)

    def xs_copy(i):
        return remote(xs_send.at[i], xs_recv.at[i], xs_s.at[i], xs_r.at[i], x_peer)

    def ag_copy(i):
        return remote(ag_send.at[i], ag_recv.at[i], ag_s.at[i], ag_r.at[i], core_peer)

    def cache_rows(i):
        return pl.ds(pl.multiple_of(chunk_of(i) * blk, blk), blk)

    def ssm_load(i):
        s = lax.rem(i, 2)
        return pltpu.make_async_copy(ssm_hbm.at[layer_of(i), cache_rows(i)], ssm_buf.at[s], ssm_in_sem.at[s])

    def ssm_store(i):
        s = lax.rem(i, 2)
        return pltpu.make_async_copy(ssm_buf.at[s], ssm_out.at[layer_of(i), cache_rows(i)], ssm_out_sem.at[s])

    def conv_load(i):
        s = lax.rem(i, 2)
        return pltpu.make_async_copy(conv_hbm.at[layer_of(i), :, cache_rows(i)], conv_buf.at[s, pl.ds(0, 3)], conv_in_sem.at[s])

    def conv_store(i):
        s = lax.rem(i, 2)
        return pltpu.make_async_copy(conv_buf.at[s, pl.ds(1, 3)], conv_out.at[layer_of(i), :, cache_rows(i)], conv_out_sem.at[s])

    res_load = pltpu.make_async_copy(res_hbm, r_ref, in_sem.at[0])
    w_in_load = [pltpu.make_async_copy(w_in_hbm.at[l], w_in.at[l], in_sem.at[1 + l]) for l in range(n_layer)]
    w_out_load = pltpu.make_async_copy(w_out_hbm, w_out, in_sem.at[1 + n_layer])

    res_load.start()
    w_in_load[0].start()

    barrier = pltpu.get_barrier_semaphore()
    for dev in (y_peer, core_peer, x_peer, d_peer):
        pl.semaphore_signal(barrier, inc=1, device_id=dev, device_id_type=MESH)
    pl.semaphore_wait(barrier, 4)

    def eye():
        n = 2 * blk
        return lax.broadcasted_iota(jnp.int32, (n, n), 0) == lax.broadcasted_iota(jnp.int32, (n, n), 1)

    def phase_a(i):
        sums = []
        for part in range(2):
            val = r_ref[pl.ds(part_rows(i, part), blk), :]
            sums.append(jnp.sum(val * val, axis=1, keepdims=True))
        col = jnp.concatenate(sums, axis=0)
        row = jnp.sum(jnp.where(eye(), col, 0.0), axis=0, keepdims=True)
        st_send[i] = jnp.broadcast_to(row, (8, 2 * blk))
        st_copy(i).start()

    def phase_b(i):
        l = layer_of(i)
        s = lax.rem(i, 2)
        st_copy(i).wait_recv()
        sq = st_send[i] + pltpu.roll(st_recv[i], blk, 1)
        inv = lax.rsqrt(sq / d_model + NORM_EPS)
        col = jnp.sum(jnp.where(eye(), jnp.broadcast_to(inv[0:1], (2 * blk, 2 * blk)), 0.0), axis=1, keepdims=True)
        nw = norm_w[l]
        for part in range(2):
            base = part_rows(i, part)
            for q in range(blk // 16):
                lo = part * blk + q * 16
                val = r_ref[pl.ds(base + q * 16, 16), :]
                h_buf[lo:lo + 16, :] = (val * col[lo:lo + 16] * nw).astype(BF)

        @pl.when(i >= 2)
        def _():
            for k in range(2):
                u_copy(i - 2, k).wait_send()

        for k in range(2):
            def tile(t, carry):
                cols = pl.ds(pl.multiple_of(t * 256, 256), 256)
                u = jnp.dot(h_buf[...], w_in[l, k, :, cols], preferred_element_type=F32)
                u_own[s, k, :, cols] = u[:blk]
                u_send[s, k, :, cols] = u[blk:].astype(BF)
                return carry
            lax.fori_loop(0, e_loc // 256, tile, 0)
            u_copy(i, k).start()

    def phase_c(i):
        l = layer_of(i)
        s = lax.rem(i, 2)

        @pl.when(i >= 1)
        def _():
            conv_store(i - 1).wait()

            @pl.when(i + 1 < total)
            def _():
                conv_load(i + 1).start()

        conv_load(i).wait()
        u_copy(i, 0).wait_recv()
        cb = conv_b[l]

        def rows16(q, carry):
            rws = pl.ds(pl.multiple_of(q * 16, 16), 16)
            xi = (u_own[s, 0, rws, :] + u_recv[i, 0, rws, :].astype(F32)).astype(BF)
            conv_buf[s, 3, rws, :] = xi
            acc = conv_buf[s, 0, rws, :].astype(F32) * conv_w[l, 0:1, :]
            acc = acc + conv_buf[s, 1, rws, :].astype(F32) * conv_w[l, 1:2, :]
            acc = acc + conv_buf[s, 2, rws, :].astype(F32) * conv_w[l, 2:3, :]
            acc = acc + xi.astype(F32) * conv_w[l, 3:4, :]
            acc = acc + cb
            x_buf[rws, :] = (acc * jax.nn.sigmoid(acc)).astype(BF)
            return carry
        lax.fori_loop(0, blk // 16, rows16, 0)
        conv_store(i).start()

        @pl.when(i >= 2)
        def _():
            for q in range(3):
                p_copy(i - 2, q).wait_send()

        pt = lax.dot_general(w_x[l], x_buf[...], (((1,), (1,)), ((), ())), preferred_element_type=F32)
        pt = jnp.concatenate([pt, pt], axis=1)
        p_own[...] = pt
        p_send[s] = pt.astype(BF)
        for q in range(3):
            p_copy(i, q).start()

        u_copy(i, 1).wait_recv()

        def zrows(q, carry):
            rws = pl.ds(pl.multiple_of(q * 16, 16), 16)
            z = (u_own[s, 1, rws, :] + u_recv[i, 1, rws, :].astype(F32)).astype(BF).astype(F32)
            z_buf[rws, :] = z * jax.nn.sigmoid(z)
            return carry
        lax.fori_loop(0, blk // 16, zrows, 0)

    def phase_d(i):
        l = layer_of(i)
        s = lax.rem(i, 2)
        for q in range(3):
            p_copy(i, q).wait_recv()
        pt = p_own[...]
        for q in range(3):
            pt = pt + p_recv[i, q].astype(F32)

        def unit(v):
            return v * lax.rsqrt(jnp.mean(v * v, axis=0, keepdims=True) + INNER_EPS)
        low = unit(pt[:n_rank]).astype(BF)
        bt = unit(pt[n_rank:n_rank + n_state])
        ct = unit(pt[n_rank + n_state:])
        for b in range(blk):
            b_bc[b] = jnp.broadcast_to(bt[:, b:b + 1], (n_state, 128))
            c_bc[b] = jnp.broadcast_to(ct[:, b:b + 1], (n_state, 128))

        def dt_tile(t, carry):
            cols = pl.ds(pl.multiple_of(t * 256, 256), 256)
            v = lax.dot_general(low, w_dt[l, :, cols], (((0,), (0,)), ((), ())), preferred_element_type=F32)[:blk]
            v = v + dt_bias[l, :, cols]
            dt = jnp.maximum(v, 0.0) + jnp.log1p(jnp.exp(-jnp.abs(v)))
            dt_buf[:, cols] = dt
            dtx_buf[:, cols] = dt * x_buf[:, cols].astype(F32)
            return carry
        lax.fori_loop(0, e_loc // 256, dt_tile, 0)
        ssm_load(i).wait()

        def group(g, carry):
            rws = pl.ds(pl.multiple_of(g * 8, 8), 8)
            for j in range(e_loc // 128):
                cols = slice(j * 128, (j + 1) * 128)
                dt8 = dt_buf[rws, cols]
                dx8 = dtx_buf[rws, cols]
                a = a_neg[l, :, cols]
                decay = jnp.exp2(dt8[:, None, :] * a[None])
                new = decay * ssm_buf[s, rws, :, cols] + dx8[:, None, :] * b_bc[rws]
                ssm_buf[s, rws, :, cols] = new
                y_buf[rws, cols] = jnp.sum(new * c_bc[rws], axis=1)
            return carry
        lax.fori_loop(0, blk // 8, group, 0)
        ssm_store(i).start()
        ds = d_skip[l]

        def gate(q, carry):
            rws = pl.ds(pl.multiple_of(q * 16, 16), 16)
            g_all[i, rws, :] = ((y_buf[rws, :] + ds * x_buf[rws, :].astype(F32)) * z_buf[rws, :]).astype(BF)
            return carry
        lax.fori_loop(0, blk // 16, gate, 0)
        g_copy(i).start()

    def phase_e(i):
        l = layer_of(i)
        g_copy(i).wait_recv()

        def tile(t, carry):
            cols = pl.ds(pl.multiple_of(t * 256, 256), 256)
            o_buf[:, cols] = jnp.dot(g_all[i], w_out[l, :, cols], preferred_element_type=F32)
            return carry
        lax.fori_loop(0, d_loc // 256, tile, 0)
        other = pl.multiple_of((1 - core) * blk, blk)
        cr_send[i] = o_buf[pl.ds(other, blk), :].astype(BF)
        cr_copy(i).start()

    def phase_f(i):
        cr_copy(i).wait_recv()
        mine = pl.multiple_of(core * blk, blk)
        xs_send[i] = (o_buf[pl.ds(mine, blk), :] + cr_recv[i].astype(F32)).astype(BF)
        xs_copy(i).start()

    def phase_g(i):
        xs_copy(i).wait_recv()
        tot = (xs_send[i].astype(F32) + xs_recv[i].astype(F32)).astype(BF)
        ag_send[i] = tot
        ag_copy(i).start()
        rws = pl.ds(part_rows(i, core), blk)
        r_ref[rws, :] = r_ref[rws, :] + tot.astype(F32)

    def phase_h(i):
        ag_copy(i).wait_recv()
        rws = pl.ds(part_rows(i, 1 - core), blk)
        r_ref[rws, :] = r_ref[rws, :] + ag_recv[i].astype(F32)

        @pl.when(i + n_chunk < total)
        def _():
            phase_a(i + n_chunk)

    for l in range(n_layer):
        a_neg[l] = jnp.exp(a_log[l]) * (-LOG2E)
    res_load.wait()

    def first_a(i, carry):
        phase_a(i)
        return carry
    lax.fori_loop(0, n_chunk, first_a, 0)
    w_in_load[0].wait()

    def run(phase, i, extra=None):
        ok = (i >= 0) & (i < total)

        @pl.when(ok)
        def _():
            phase(i)

    def step(s, carry):
        @pl.when(s == n_chunk)
        def _():
            w_in_load[1].wait()
        run(phase_b, s)

        @pl.when(s == 0)
        def _():
            conv_load(0).start()
            conv_load(1).start()
            ssm_load(0).start()
            ssm_load(1).start()
            w_out_load.start()
            w_in_load[1].start()

        @pl.when((s >= 2) & (s - 2 < total))
        def _():
            ssm_store(s - 2 - 0).wait()

            @pl.when(s < total)
            def _():
                ssm_load(s).start()
        run(phase_c, s - 1)

        @pl.when(s == 2)
        def _():
            w_out_load.wait()
        run(phase_e, s - 2)
        run(phase_g, s - 3)
        run(phase_f, s - 2)
        run(phase_h, s - 3)
        run(phase_d, s - 1)
        return carry
    lax.fori_loop(0, total + 3, step, 0)

    conv_store(total - 1).wait()
    for i in range(total - 2, total):
        for k in range(2):
            u_copy(i, k).wait_send()
        for q in range(3):
            p_copy(i, q).wait_send()

    def drain(i, carry):
        st_copy(i).wait_send()
        g_copy(i).wait_send()
        cr_copy(i).wait_send()
        xs_copy(i).wait_send()
        ag_copy(i).wait_send()
        return carry
    lax.fori_loop(0, total, drain, 0)


def solution(mesh):
    def local_step(residual, norm_w, w_in, conv_w, conv_b, w_x, w_dt, dt_bias, a_log, d_skip, w_out, conv_state, ssm_state):
        n_layer = norm_w.shape[0]
        rows, d_loc = residual.shape
        e_loc = w_x.shape[1]
        n_state = a_log.shape[-1]
        n_rank = w_dt.shape[1]
        n_proj = w_x.shape[2]
        d_model = d_loc * mesh.shape["tx"]
        total = n_layer * N_CHUNK
        blk = rows // 2 // N_CHUNK
        dims = (n_layer, rows, d_loc, e_loc, n_state, n_rank, d_model)
        w_in_t = jnp.transpose(w_in, (0, 2, 1, 3))
        conv_t = jnp.transpose(conv_state, (0, 3, 1, 2))
        ssm_t = jnp.transpose(ssm_state, (0, 1, 3, 2))
        args = (residual, norm_w[:, None, :], w_in_t, jnp.transpose(conv_w, (0, 2, 1)), conv_b[:, None, :], jnp.transpose(w_x, (0, 2, 1)), w_dt, dt_bias[:, None, :], jnp.transpose(a_log, (0, 2, 1)), d_skip[:, None, :], w_out, conv_t, ssm_t)
        hbm = pl.BlockSpec(memory_space=pl.ANY)
        vmem = pl.BlockSpec(memory_space=pltpu.VMEM)
        in_specs = [hbm, vmem, hbm, vmem, vmem, vmem, vmem, vmem, vmem, vmem, hbm, hbm, hbm]
        dma = pltpu.SemaphoreType.DMA
        scratch = [
            pltpu.VMEM((n_layer, 2, d_loc, e_loc), BF),
            pltpu.VMEM((n_layer, e_loc, d_loc), BF),
            pltpu.VMEM((n_layer, n_state, e_loc), F32),
            pltpu.VMEM((2, blk, n_state, e_loc), F32),
            pltpu.VMEM((2, 4, blk, e_loc), BF),
            pltpu.VMEM((2 * blk, d_loc), BF),
            pltpu.VMEM((2, 2, blk, e_loc), F32),
            pltpu.VMEM((blk, e_loc), F32),
            pltpu.VMEM((blk, e_loc), BF),
            pltpu.VMEM((blk, e_loc), F32),
            pltpu.VMEM((blk, e_loc), F32),
            pltpu.VMEM((blk, e_loc), F32),
            pltpu.VMEM((blk, n_state, 128), F32),
            pltpu.VMEM((blk, n_state, 128), F32),
            pltpu.VMEM((2 * blk, d_loc), F32),
            pltpu.VMEM((total, 8, 2 * blk), F32),
            pltpu.VMEM((total, 8, 2 * blk), F32),
            pltpu.VMEM((2, 2, blk, e_loc), BF),
            pltpu.VMEM((total, 2, blk, e_loc), BF),
            pltpu.VMEM((n_proj, 2 * blk), F32),
            pltpu.VMEM((2, n_proj, 2 * blk), BF),
            pltpu.VMEM((total, 3, n_proj, 2 * blk), BF),
            pltpu.VMEM((total, 2 * blk, e_loc), BF),
        ] + [pltpu.VMEM((total, blk, d_loc), BF)] * 6 + [
            dma((2 + n_layer,)), dma((2,)), dma((2,)), dma((2,)), dma((2,)),
            dma((total,)), dma((total,)), dma((2, 2)), dma((total, 2)), dma((2, 3)), dma((total, 3)),
            dma((total,)), dma((total,)), dma((total,)), dma((total,)), dma((total,)), dma((total,)), dma((total,)), dma((total,)),
        ]
        out = pl.pallas_call(
            functools.partial(step_kernel, dims),
            out_shape=(jax.ShapeDtypeStruct((rows, d_loc), F32), jax.ShapeDtypeStruct(conv_t.shape, BF), jax.ShapeDtypeStruct(ssm_t.shape, F32)),
            in_specs=in_specs,
            out_specs=(vmem, hbm, hbm),
            scratch_shapes=scratch,
            compiler_params=pltpu.CompilerParams(collective_id=0, has_side_effects=True, vmem_limit_bytes=67043328),
            name="mamba_step",
        )(*args)
        return out[0], jnp.transpose(out[1], (0, 2, 3, 1)), jnp.transpose(out[2], (0, 1, 3, 2))

    cache_spec = P(None, ("dp", "tx"), "ty", None)
    in_specs = (P("dp", "tx"), P(None, "tx"), P(None, "tx", None, "ty"), P(None, "ty", None), P(None, "ty"), P(None, "ty", None), P(None, None, "ty"), P(None, "ty"), P(None, "ty", None), P(None, "ty"), P(None, "ty", "tx"), cache_spec, cache_spec)
    out_specs = (P("dp", "tx"), cache_spec, cache_spec)
    return jax.shard_map(local_step, mesh=mesh, in_specs=in_specs, out_specs=out_specs, check_vma=False)
```

time: 374 us -> 180 us (0.48)
  waiting for transfers between devices: 169 us -> 0 us
  Pallas kernels: 0 us -> 127 us
  other arithmetic: 121 us -> 0 us
  matrix products: 30.5 us -> 0 us
  local copies, waits for them, and re-layouts: 26.4 us -> 52.1 us
  between operations: 14.6 us -> 0.65 us
  blocking collectives: 11.4 us -> 0 us
    pallas_call x0 -> x1, Pallas kernels: none -> 127 us  [local_step(): pl.pallas_call(functools.partial(step_kernel, dims), out_shape=(jax.Shape...]
    psum x4 -> x0, waiting for transfers between devices: 85.9 us -> none  [sum_over_ty(): return lax.psum(part_sum.astype(jnp.bfloat16), 'ty').astype(jnp.float32)]
    reduce_scatter x2 -> x0, waiting for transfers between devices: 62.2 us -> none  [local_step(): lax.psum_scatter(proj_part.astype(jnp.bfloat16), 'tx', scatter_dimension=...]
    unnamed x58 -> x6, local copies, waits for them, and re-layouts: 4.49 us -> 46.8 us
    reduce_sum x10 -> x0, other arithmetic: 40.8 us -> none  [the longest x2 34.2 us: channel_update(): state_val = jnp.sum(ssm_new * c_mat[:, None, :], axis=-1)]
    another operation x4 -> x0, other arithmetic: 39.2 us -> none  [local_step(): return (residual, jnp.stack(conv_list), jnp.stack(ssm_list))]
    add x2 -> x0, other arithmetic: 33.3 us -> none  [the longest x1 29.7 us: channel_update(): decay * ssm_prev + (delta * x_float)[:, :, None] * b_mat[:, None, :]]
    dot_general x8 -> x0, matrix products: 30.5 us -> none  [the longest x2 13.4 us: local_step(): jnp.einsum('bd,dke->bke', normed, w_in[layer_idx], preferred_element_type...]
  transfers between devices with their start and end apart: 8 -> 0, of which waited for: 7 -> 0; matrix products, arithmetic and copies ran while one was open for 19% -> 0% of each run, Pallas kernels for 0% -> 0%
where the time goes in v1:
time: 180 us; the launch traced here: 179 us
  Pallas kernels  127 us (71%)
  local copies, waits for them, and re-layouts  52.1 us (29%)
    pallas_call x1, Pallas kernels, local_step(): pl.pallas_call(functools.partial(step_kernel, dims), out_shape=(jax.Shape...  127 us
    unnamed x6, local copies, waits for them, and re-layouts  46.8 us

profile of v1, /device:TPU:0, one launch (start us, length us, event | category | flops | bytes accessed | tf_op | source)
XLA Modules:
  0.0 179.4 jit_solution(10705661195145248174)
XLA Ops:
  0.6 1.3 broadcast_in_dim.12.norm_w
  1.9 1.3 broadcast_in_dim.13.conv_b
  3.2 1.3 broadcast_in_dim.14.dt_bias
  4.5 1.3 broadcast_in_dim.15.d_skip
  5.8 12.5 %copy.18 = bf16[2,1280,2,1280]{3,1,2,0:T(8,128)(2,1)} copy(bf16[2,1280,2,1280]{3,2,1,0:T(2,128)(2,1)} %param.15) | data formatting | bytes 26214400 | tf_op args[2]
  18.3 126.7 %mamba_step.1 = (f32[512,1280]{1,0:T(8,128)}, bf16[2,3,256,1280]{3,2,1,0:T(8,128)(2,1)}, f32[2,256,16,1280]{3,2,1,0:T(8,128)}) custom-call(f32[512,1280]{1,0:T(8,128)} %res_hbm.1, f32[2,1,1280]{2,1,0:T(1,128)} %broadcast_in_dim.12.norm_w, bf16[2,2,1280,1280]{3,2,1,0:T(8,128)(2,1)} %bitcast.10, f32[2,4,1280]{2,1,0:T(4,128)} %bitcast.17, ...), custom_call_target="tpu_custom_call" | custom-call | tf_op jit(solution)/shard_map/mamba_step/pallas_call | solution.py:407
  145.0 0.0 copy-start
  145.0 3.6 %copy.22 = f32[512,1280]{1,0:T(8,128)} copy(f32[512,1280]{1,0:T(8,128)} %get-tuple-element.12) | data formatting | bytes 5242880
  148.6 0.0 copy-done
  148.6 1.9 %copy.23 = bf16[2,256,1280,3]{2,1,3,0:T(8,128)(2,1)} copy(bf16[2,256,1280,3]{2,1,3,0:T(8,128)(2,1)S(1)} %bitcast.14) | data formatting | bytes 7864320
  150.5 28.9 %copy.24 = f32[2,256,1280,16]{2,3,1,0:T(8,128)} copy(f32[2,256,1280,16]{2,3,1,0:T(8,128)} %bitcast.11) | data formatting | bytes 83886080
Async XLA Ops:
  145.0 3.6 %copy-start = (bf16[2,3,256,1280]{3,2,1,0:T(8,128)(2,1)S(1)}, bf16[2,3,256,1280]{3,2,1,0:T(8,128)(2,1)}, u32[]{:S(2)}) copy-start(bf16[2,3,256,1280]{3,2,1,0:T(8,128)(2,1)} %get-tuple-element.7) | copy-start | bytes 11796484

commit v2 on v1

--- a/solution.py
+++ b/solution.py
@@ -6,6 +6,7 @@
 from jax.experimental.pallas import tpu as pltpu
 from jax.sharding import PartitionSpec as P
 
+
 NORM_EPS = 1e-5
 INNER_EPS = 1e-6
 LOG2E = 1.4426950408889634
@@ -15,11 +16,11 @@
 MESH = pl.DeviceIdType.MESH
 
 
-def step_kernel(dims, res_hbm, norm_w, w_in_hbm, conv_w, conv_b, w_x, w_dt, dt_bias, a_log, d_skip, w_out_hbm, conv_hbm, ssm_hbm,
-                r_ref, conv_out, ssm_out,
-                w_in, w_out, a_neg, ssm_buf, conv_buf, h_buf, u_own, z_buf, x_buf, dt_buf, dtx_buf, y_buf, b_bc, c_bc, o_buf,
+def step_kernel(dims, res_hbm, norm_w_in, w_in_hbm, conv_w, conv_b_in, w_x, w_dt, dt_bias_in, a_log, d_skip_in, w_out_hbm, conv_hbm, ssm_hbm,
+                r_ref, bt_out, g_out, dt_out, x_out, xi_out,
+                norm_w, conv_b, dt_bias, d_skip, w_in, w_out, a_neg, ssm_buf, conv_buf, h_buf, u_own, z_buf, x_buf, low_buf, dt_buf, dtx_buf, b_bc, c_bc, o_buf,
                 st_send, st_recv, u_send, u_recv, p_own, p_send, p_recv, g_all, cr_send, cr_recv, xs_send, xs_recv, ag_send, ag_recv,
-                in_sem, ssm_in_sem, ssm_out_sem, conv_in_sem, conv_out_sem,
+                in_sem, ssm_in_sem, conv_in_sem, dt_sem, x_sem, xi_sem, go_sem,
                 st_s, st_r, u_s, u_r, p_s, p_r, g_s, g_r, cr_s, cr_r, xs_s, xs_r, ag_s, ag_r):
     n_layer, rows, d_loc, e_loc, n_state, n_rank, d_model = dims
     half = rows // 2
@@ -79,17 +80,22 @@
         s = lax.rem(i, 2)
         return pltpu.make_async_copy(ssm_hbm.at[layer_of(i), cache_rows(i)], ssm_buf.at[s], ssm_in_sem.at[s])
 
-    def ssm_store(i):
-        s = lax.rem(i, 2)
-        return pltpu.make_async_copy(ssm_buf.at[s], ssm_out.at[layer_of(i), cache_rows(i)], ssm_out_sem.at[s])
-
     def conv_load(i):
         s = lax.rem(i, 2)
         return pltpu.make_async_copy(conv_hbm.at[layer_of(i), :, cache_rows(i)], conv_buf.at[s, pl.ds(0, 3)], conv_in_sem.at[s])
 
-    def conv_store(i):
-        s = lax.rem(i, 2)
-        return pltpu.make_async_copy(conv_buf.at[s, pl.ds(1, 3)], conv_out.at[layer_of(i), :, cache_rows(i)], conv_out_sem.at[s])
+    def dt_store(i):
+        return pltpu.make_async_copy(dt_buf, dt_out.at[layer_of(i), cache_rows(i)], dt_sem)
+
+    def x_store(i):
+        return pltpu.make_async_copy(x_buf, x_out.at[layer_of(i), cache_rows(i)], x_sem)
+
+    def xi_store(i):
+        s = lax.rem(i, 2)
+        return pltpu.make_async_copy(conv_buf.at[s, 3], xi_out.at[layer_of(i), cache_rows(i)], xi_sem.at[s])
+
+    def g_store(i):
+        return pltpu.make_async_copy(g_all.at[i, pl.ds(0, blk)], g_out.at[cache_rows(i)], go_sem.at[chunk_of(i)])
 
     res_load = pltpu.make_async_copy(res_hbm, r_ref, in_sem.at[0])
     w_in_load = [pltpu.make_async_copy(w_in_hbm.at[l], w_in.at[l], in_sem.at[1 + l]) for l in range(n_layer)]
@@ -144,6 +150,7 @@
                 u_own[s, k, :, cols] = u[:blk]
                 u_send[s, k, :, cols] = u[blk:].astype(BF)
                 return carry
+
             lax.fori_loop(0, e_loc // 256, tile, 0)
             u_copy(i, k).start()
 
@@ -153,7 +160,8 @@
 
         @pl.when(i >= 1)
         def _():
-            conv_store(i - 1).wait()
+            xi_store(i - 1).wait()
+            x_store(i - 1).wait()
 
             @pl.when(i + 1 < total)
             def _():
@@ -174,8 +182,10 @@
             acc = acc + cb
             x_buf[rws, :] = (acc * jax.nn.sigmoid(acc)).astype(BF)
             return carry
+
         lax.fori_loop(0, blk // 16, rows16, 0)
-        conv_store(i).start()
+        xi_store(i).start()
+        x_store(i).start()
 
         @pl.when(i >= 2)
         def _():
@@ -196,6 +206,7 @@
             z = (u_own[s, 1, rws, :] + u_recv[i, 1, rws, :].astype(F32)).astype(BF).astype(F32)
             z_buf[rws, :] = z * jax.nn.sigmoid(z)
             return carry
+
         lax.fori_loop(0, blk // 16, zrows, 0)
 
     def phase_d(i):
@@ -209,46 +220,57 @@
 
         def unit(v):
             return v * lax.rsqrt(jnp.mean(v * v, axis=0, keepdims=True) + INNER_EPS)
-        low = unit(pt[:n_rank]).astype(BF)
+
+        low_buf[...] = jnp.transpose(unit(pt[:n_rank]))[:blk].astype(BF)
         bt = unit(pt[n_rank:n_rank + n_state])
         ct = unit(pt[n_rank + n_state:])
+        bt_out[i, 0] = bt
+        bt_out[i, 1] = pltpu.roll(bt, 2 * blk - blk // 2, 1)
         for b in range(blk):
             b_bc[b] = jnp.broadcast_to(bt[:, b:b + 1], (n_state, 128))
             c_bc[b] = jnp.broadcast_to(ct[:, b:b + 1], (n_state, 128))
 
+        @pl.when(i >= 1)
+        def _():
+            dt_store(i - 1).wait()
+
         def dt_tile(t, carry):
             cols = pl.ds(pl.multiple_of(t * 256, 256), 256)
-            v = lax.dot_general(low, w_dt[l, :, cols], (((0,), (0,)), ((), ())), preferred_element_type=F32)[:blk]
+            v = jnp.dot(low_buf[...], w_dt[l, :, cols], preferred_element_type=F32)
             v = v + dt_bias[l, :, cols]
             dt = jnp.maximum(v, 0.0) + jnp.log1p(jnp.exp(-jnp.abs(v)))
             dt_buf[:, cols] = dt
             dtx_buf[:, cols] = dt * x_buf[:, cols].astype(F32)
             return carry
+
         lax.fori_loop(0, e_loc // 256, dt_tile, 0)
+        dt_store(i).start()
         ssm_load(i).wait()
 
         def group(g, carry):
-            rws = pl.ds(pl.multiple_of(g * 8, 8), 8)
             for j in range(e_loc // 128):
                 cols = slice(j * 128, (j + 1) * 128)
-                dt8 = dt_buf[rws, cols]
-                dx8 = dtx_buf[rws, cols]
                 a = a_neg[l, :, cols]
-                decay = jnp.exp2(dt8[:, None, :] * a[None])
-                new = decay * ssm_buf[s, rws, :, cols] + dx8[:, None, :] * b_bc[rws]
-                ssm_buf[s, rws, :, cols] = new
-                y_buf[rws, cols] = jnp.sum(new * c_bc[rws], axis=1)
+                out = []
+                for p in range(2):
+                    rws = pl.ds(pl.multiple_of(g * 16 + p * 8, 8), 8)
+                    decay = jnp.exp2(dt_buf[rws, cols][:, None, :] * a[None])
+                    new = decay * ssm_buf[s, rws, :, cols] + dtx_buf[rws, cols][:, None, :] * b_bc[rws]
+                    out.append(jnp.sum(new * c_bc[rws], axis=1))
+                rws = pl.ds(pl.multiple_of(g * 16, 16), 16)
+                y = jnp.concatenate(out, axis=0) + d_skip[l, :, cols] * x_buf[rws, cols].astype(F32)
+                g_all[i, rws, cols] = (y * z_buf[rws, cols]).astype(BF)
             return carry
-        lax.fori_loop(0, blk // 8, group, 0)
-        ssm_store(i).start()
-        ds = d_skip[l]
-
-        def gate(q, carry):
-            rws = pl.ds(pl.multiple_of(q * 16, 16), 16)
-            g_all[i, rws, :] = ((y_buf[rws, :] + ds * x_buf[rws, :].astype(F32)) * z_buf[rws, :]).astype(BF)
-            return carry
-        lax.fori_loop(0, blk // 16, gate, 0)
-        g_copy(i).start()
+
+        lax.fori_loop(0, blk // 16, group, 0)
+
+        @pl.when(i < total - n_chunk)
+        def _():
+            g_copy(i).start()
+
+        @pl.when(i >= total - n_chunk)
+        def _():
+            g_store(i).start()
 
     def phase_e(i):
         l = layer_of(i)
@@ -258,6 +280,7 @@
             cols = pl.ds(pl.multiple_of(t * 256, 256), 256)
             o_buf[:, cols] = jnp.dot(g_all[i], w_out[l, :, cols], preferred_element_type=F32)
             return carry
+
         lax.fori_loop(0, d_loc // 256, tile, 0)
         other = pl.multiple_of((1 - core) * blk, blk)
         cr_send[i] = o_buf[pl.ds(other, blk), :].astype(BF)
@@ -287,17 +310,20 @@
             phase_a(i + n_chunk)
 
     for l in range(n_layer):
+        for vec, src in ((norm_w, norm_w_in), (conv_b, conv_b_in), (dt_bias, dt_bias_in), (d_skip, d_skip_in)):
+            vec[l] = src[l:l + 1, :]
         a_neg[l] = jnp.exp(a_log[l]) * (-LOG2E)
     res_load.wait()
 
     def first_a(i, carry):
         phase_a(i)
         return carry
+
     lax.fori_loop(0, n_chunk, first_a, 0)
     w_in_load[0].wait()
 
-    def run(phase, i, extra=None):
-        ok = (i >= 0) & (i < total)
+    def run(phase, i, stop=total):
+        ok = (i >= 0) & (i < stop)
 
         @pl.when(ok)
         def _():
@@ -307,6 +333,7 @@
         @pl.when(s == n_chunk)
         def _():
             w_in_load[1].wait()
+
         run(phase_b, s)
 
         @pl.when(s == 0)
@@ -318,27 +345,28 @@
             w_out_load.start()
             w_in_load[1].start()
 
-        @pl.when((s >= 2) & (s - 2 < total))
-        def _():
-            ssm_store(s - 2 - 0).wait()
-
-            @pl.when(s < total)
-            def _():
-                ssm_load(s).start()
+        @pl.when((s >= 2) & (s < total))
+        def _():
+            ssm_load(s).start()
+
         run(phase_c, s - 1)
 
         @pl.when(s == 2)
         def _():
             w_out_load.wait()
-        run(phase_e, s - 2)
-        run(phase_g, s - 3)
-        run(phase_f, s - 2)
-        run(phase_h, s - 3)
+
+        run(phase_e, s - 2, total - n_chunk)
+        run(phase_g, s - 3, total - n_chunk)
+        run(phase_f, s - 2, total - n_chunk)
+        run(phase_h, s - 3, total - n_chunk)
         run(phase_d, s - 1)
         return carry
-    lax.fori_loop(0, total + 3, step, 0)
-
-    conv_store(total - 1).wait()
+
+    lax.fori_loop(0, total + 1, step, 0)
+
+    xi_store(total - 1).wait()
+    x_store(total - 1).wait()
+    dt_store(total - 1).wait()
     for i in range(total - 2, total):
         for k in range(2):
             u_copy(i, k).wait_send()
@@ -347,12 +375,92 @@
 
     def drain(i, carry):
         st_copy(i).wait_send()
+        st_copy(i + n_chunk).wait_send()
         g_copy(i).wait_send()
         cr_copy(i).wait_send()
         xs_copy(i).wait_send()
         ag_copy(i).wait_send()
+        g_store(i + total - n_chunk).wait()
         return carry
-    lax.fori_loop(0, total, drain, 0)
+
+    lax.fori_loop(0, n_chunk, drain, 0)
+
+
+def state_kernel(n_carry, blk, ssm_in, dt, x, bt, a_log, conv_in, xi, *refs):
+    ssm_out, conv_out, a_neg, b_bc = refs[n_carry:]
+    n_state, e_loc = a_log.shape[1:]
+
+    @pl.when(pl.program_id(0) == 0)
+    def _():
+        a_neg[...] = jnp.exp(a_log[0]) * (-LOG2E)
+
+    for b in range(blk):
+        b_bc[b] = jnp.broadcast_to(bt[0, 0, :, b:b + 1], (n_state, 128))
+    conv_out[0, 0] = conv_in[0, 1]
+    conv_out[0, 1] = conv_in[0, 2]
+    conv_out[0, 2] = xi[0]
+
+    def group(g, carry):
+        rws16 = pl.ds(pl.multiple_of(g * 16, 16), 16)
+        for j in range(e_loc // 128):
+            cols = slice(j * 128, (j + 1) * 128)
+            a = a_neg[:, cols]
+            dtx = dt[0, rws16, cols] * x[0, rws16, cols].astype(F32)
+            for p in range(2):
+                rws = pl.ds(pl.multiple_of(g * 16 + p * 8, 8), 8)
+                decay = jnp.exp2(dt[0, rws, cols][:, None, :] * a[None])
+                ssm_out[0, rws, :, cols] = decay * ssm_in[0, rws, :, cols] + dtx[p * 8:p * 8 + 8][:, None, :] * b_bc[rws]
+        return carry
+
+    lax.fori_loop(0, blk // 16, group, 0)
+
+
+def state_pass(l, ssm_t, dt, x, bt, a_log_t, conv_t, xi, carried):
+    _, half, n_state, e_loc = ssm_t.shape
+    blk = 32
+    per = half // N_CHUNK // blk
+
+    def rows_spec(*tail):
+        return pl.BlockSpec((1, blk) + tail, lambda g: (l, g) + (0,) * len(tail))
+
+    conv_spec = pl.BlockSpec((1, 3, blk, e_loc), lambda g: (l, 0, g, 0))
+    in_specs = [rows_spec(n_state, e_loc), rows_spec(e_loc), rows_spec(e_loc),
+                pl.BlockSpec((1, 1, n_state, 128), lambda g: (l * N_CHUNK + g // per, g % per, 0, 0)),
+                pl.BlockSpec((1, n_state, e_loc), lambda g: (l, 0, 0)), conv_spec, rows_spec(e_loc)]
+    in_specs += [pl.BlockSpec(memory_space=pl.ANY)] * len(carried)
+    n_elem = half * n_state * e_loc
+    return pl.pallas_call(
+        functools.partial(state_kernel, len(carried), blk),
+        grid=(half // blk,),
+        out_shape=(jax.ShapeDtypeStruct(ssm_t.shape, F32), jax.ShapeDtypeStruct(conv_t.shape, BF)),
+        in_specs=in_specs,
+        out_specs=(rows_spec(n_state, e_loc), conv_spec),
+        scratch_shapes=[pltpu.VMEM((n_state, e_loc), F32), pltpu.VMEM((blk, n_state, 128), F32)],
+        input_output_aliases={7 + k: k for k in range(len(carried))},
+        compiler_params=pltpu.CompilerParams(vmem_limit_bytes=67043328),
+        cost_estimate=pl.CostEstimate(flops=n_elem * 1000, bytes_accessed=n_elem * 8, transcendentals=n_elem),
+    )(ssm_t, dt, x, bt, a_log_t, conv_t, xi, *carried)
+
+
+def out_kernel(g_ref, w_ref, o_ref):
+    def tile(t, carry):
+        cols = pl.ds(pl.multiple_of(t * 256, 256), 256)
+        o_ref[:, cols] = jnp.dot(g_ref[...], w_ref[0, :, cols], preferred_element_type=F32)
+        return carry
+
+    lax.fori_loop(0, w_ref.shape[2] // 256, tile, 0)
+
+
+def out_proj(g, w_out, l):
+    return pl.pallas_call(
+        out_kernel,
+        grid=(1,),
+        out_shape=jax.ShapeDtypeStruct((g.shape[0], w_out.shape[2]), F32),
+        in_specs=[pl.BlockSpec(g.shape, lambda q: (0, 0)), pl.BlockSpec((1,) + w_out.shape[1:], lambda q: (l, 0, 0))],
+        out_specs=pl.BlockSpec((g.shape[0], w_out.shape[2]), lambda q: (0, 0)),
+        compiler_params=pltpu.CompilerParams(vmem_limit_bytes=67043328),
+        name="out_proj",
+    )(g, w_out)
 
 
 def solution(mesh):
@@ -370,12 +478,13 @@
         w_in_t = jnp.transpose(w_in, (0, 2, 1, 3))
         conv_t = jnp.transpose(conv_state, (0, 3, 1, 2))
         ssm_t = jnp.transpose(ssm_state, (0, 1, 3, 2))
-        args = (residual, norm_w[:, None, :], w_in_t, jnp.transpose(conv_w, (0, 2, 1)), conv_b[:, None, :], jnp.transpose(w_x, (0, 2, 1)), w_dt, dt_bias[:, None, :], jnp.transpose(a_log, (0, 2, 1)), d_skip[:, None, :], w_out, conv_t, ssm_t)
+        a_log_t = jnp.transpose(a_log, (0, 2, 1))
+        args = (residual, norm_w, w_in_t, jnp.transpose(conv_w, (0, 2, 1)), conv_b, jnp.transpose(w_x, (0, 2, 1)), w_dt, dt_bias, a_log_t, d_skip, w_out, conv_t, ssm_t)
         hbm = pl.BlockSpec(memory_space=pl.ANY)
         vmem = pl.BlockSpec(memory_space=pltpu.VMEM)
         in_specs = [hbm, vmem, hbm, vmem, vmem, vmem, vmem, vmem, vmem, vmem, hbm, hbm, hbm]
         dma = pltpu.SemaphoreType.DMA
-        scratch = [
+        scratch = [pltpu.VMEM((n_layer, 1, d_loc), F32)] + [pltpu.VMEM((n_layer, 1, e_loc), F32)] * 3 + [
             pltpu.VMEM((n_layer, 2, d_loc, e_loc), BF),
             pltpu.VMEM((n_layer, e_loc, d_loc), BF),
             pltpu.VMEM((n_layer, n_state, e_loc), F32),
@@ -385,7 +494,7 @@
             pltpu.VMEM((2, 2, blk, e_loc), F32),
             pltpu.VMEM((blk, e_loc), F32),
             pltpu.VMEM((blk, e_loc), BF),
-            pltpu.VMEM((blk, e_loc), F32),
+            pltpu.VMEM((blk, n_rank), BF),
             pltpu.VMEM((blk, e_loc), F32),
             pltpu.VMEM((blk, e_loc), F32),
             pltpu.VMEM((blk, n_state, 128), F32),
@@ -400,20 +509,40 @@
             pltpu.VMEM((total, 3, n_proj, 2 * blk), BF),
             pltpu.VMEM((total, 2 * blk, e_loc), BF),
         ] + [pltpu.VMEM((total, blk, d_loc), BF)] * 6 + [
-            dma((2 + n_layer,)), dma((2,)), dma((2,)), dma((2,)), dma((2,)),
+            dma((2 + n_layer,)), dma((2,)), dma((2,)), dma(()), dma(()), dma((2,)), dma((N_CHUNK,)),
             dma((total,)), dma((total,)), dma((2, 2)), dma((total, 2)), dma((2, 3)), dma((total, 3)),
             dma((total,)), dma((total,)), dma((total,)), dma((total,)), dma((total,)), dma((total,)), dma((total,)), dma((total,)),
         ]
-        out = pl.pallas_call(
+        half = rows // 2
+        r_mid, bt, g_own, dt, x_act, xi = pl.pallas_call(
             functools.partial(step_kernel, dims),
-            out_shape=(jax.ShapeDtypeStruct((rows, d_loc), F32), jax.ShapeDtypeStruct(conv_t.shape, BF), jax.ShapeDtypeStruct(ssm_t.shape, F32)),
+            out_shape=(jax.ShapeDtypeStruct((rows, d_loc), F32), jax.ShapeDtypeStruct((total, 2, n_state, 128), F32), jax.ShapeDtypeStruct((half, e_loc), BF),
+                       jax.ShapeDtypeStruct((n_layer, half, e_loc), F32), jax.ShapeDtypeStruct((n_layer, half, e_loc), BF), jax.ShapeDtypeStruct((n_layer, half, e_loc), BF)),
             in_specs=in_specs,
-            out_specs=(vmem, hbm, hbm),
+            out_specs=(vmem, vmem, hbm, hbm, hbm, hbm),
             scratch_shapes=scratch,
             compiler_params=pltpu.CompilerParams(collective_id=0, has_side_effects=True, vmem_limit_bytes=67043328),
             name="mamba_step",
         )(*args)
-        return out[0], jnp.transpose(out[1], (0, 2, 3, 1)), jnp.transpose(out[2], (0, 1, 3, 2))
+
+        core = lax.rem(lax.axis_index("ty"), 2)
+        tx = lax.axis_index("tx")
+        core_swap = [(0, 1), (1, 0), (2, 3), (3, 2)]
+        g_peer = lax.ppermute(g_own, "tx", [(0, 1), (1, 0)])
+        caches = state_pass(0, ssm_t, dt, x_act, bt, a_log_t, conv_t, xi, ())
+        o_own = out_proj(g_own, w_out, n_layer - 1)
+        o_peer = out_proj(g_peer, w_out, n_layer - 1)
+        kept = jnp.where(core == 0, o_own, o_peer)
+        sent = jnp.where(core == 0, o_peer, o_own).astype(BF)
+        part = (kept + lax.ppermute(sent, "ty", core_swap).astype(F32)).astype(BF)
+        other = lax.ppermute(part, "ty", [(0, 2), (2, 0), (1, 3), (3, 1)])
+        caches = state_pass(1, ssm_t, dt, x_act, bt, a_log_t, conv_t, xi, caches)
+        tot = (part.astype(F32) + other.astype(F32)).astype(BF)
+        tot_peer = lax.ppermute(tot, "ty", core_swap)
+        first = jnp.where(core == tx, tot, tot_peer)
+        second = jnp.where(core == tx, tot_peer, tot)
+        r_out = r_mid + jnp.concatenate([first, second], axis=0).astype(F32)
+        return r_out, jnp.transpose(caches[1], (0, 2, 3, 1)), jnp.transpose(caches[0], (0, 1, 3, 2))
 
     cache_spec = P(None, ("dp", "tx"), "ty", None)
     in_specs = (P("dp", "tx"), P(None, "tx"), P(None, "tx", None, "ty"), P(None, "ty", None), P(None, "ty"), P(None, "ty", None), P(None, None, "ty"), P(None, "ty"), P(None, "ty", None), P(None, "ty"), P(None, "ty", "tx"), cache_spec, cache_spec)

time: 180 us -> 207 us (1.15)
  local copies, waits for them, and re-layouts: 52.1 us -> 13.1 us
  waiting for transfers between devices: 0 us -> 30.1 us
  Pallas kernels: 127 us -> 156 us
  other arithmetic: 0 us -> 6.06 us
    pallas_call x0 -> x4, Pallas kernels: none -> 49 us  [the longest x2 39.1 us: state_pass(): pl.pallas_call(functools.partial(state_kernel, len(carried), blk), grid=(...]
    unnamed x6 -> x7, local copies, waits for them, and re-layouts: 46.8 us -> 13.1 us
    ppermute x0 -> x4, waiting for transfers between devices: none -> 30.1 us  [the longest x1 16.1 us: local_step(): other = lax.ppermute(part, 'ty', [(0, 2), (2, 0), (1, 3), (3, 1)])]
    pallas_call x1, Pallas kernels: 127 us -> 107 us  [local_step(): pl.pallas_call(functools.partial(step_kernel, dims), out_shape=(jax.Shape...]
    broadcast_in_dim x4 -> x0, local copies, waits for them, and re-layouts: 5.22 us -> none  [the longest x1 1.31 us: local_step(): norm_w[:, None, :]]
    convert_element_type x0 -> x3, other arithmetic: none -> 2.8 us  [the longest x1 1.59 us: local_step(): sent = jnp.where(core == 0, o_peer, o_own).astype(BF)]
  transfers between devices with their start and end apart: 0 -> 4, of which waited for: 0 -> 3; matrix products, arithmetic and copies ran while one was open for 0% -> 0% of each run, Pallas kernels for 0% -> 21%
where the time goes in v2:
time: 207 us
  Pallas kernels  156 us (75%)
  waiting for transfers between devices  30.1 us (15%)
  local copies, waits for them, and re-layouts  13.1 us (6%)
  other arithmetic  6.06 us (3%)
    pallas_call x1, Pallas kernels, local_step(): pl.pallas_call(functools.partial(step_kernel, dims), out_shape=(jax.Shape...  107 us
    pallas_call x2, Pallas kernels, state_pass(): pl.pallas_call(functools.partial(state_kernel, len(carried), blk), grid=(...  39.1 us
    ppermute x1, waiting for transfers between devices, local_step(): other = lax.ppermute(part, 'ty', [(0, 2), (2, 0), (1, 3), (3, 1)])  16.1 us
    unnamed x7, local copies, waits for them, and re-layouts  13.1 us
    ppermute x1, waiting for transfers between devices, local_step(): g_peer = lax.ppermute(g_own, 'tx', [(0, 1), (1, 0)])  11.9 us
    pallas_call x2, Pallas kernels, out_proj(): pl.pallas_call(out_kernel, grid=(1,), out_shape=jax.ShapeDtypeStruct((g.s...  9.81 us
  transfers between devices with their start and end apart: 4, of which 3 were waited for; matrix products, arithmetic and copies ran while one was open for 0% of the time, Pallas kernels for 21%

profile of v2, /device:TPU:0, one launch (start us, length us, event | category | flops | bytes accessed | tf_op | source)
XLA Modules:
  0.0 207.2 jit_solution(9937637811666063704)
XLA Ops:
  0.6 12.5 %copy.20 = bf16[2,1280,2,1280]{3,1,2,0:T(8,128)(2,1)} copy(bf16[2,1280,2,1280]{3,2,1,0:T(2,128)(2,1)} %param.15) | data formatting | bytes 26214400 | tf_op args[2]
  13.1 107.3 %mamba_step.1 = (f32[512,1280]{1,0:T(8,128)}, f32[8,2,16,128]{3,2,1,0:T(8,128)}, bf16[256,1280]{1,0:T(8,128)(2,1)}, f32[2,256,1280]{2,1,0:T(8,128)}, bf16[2,256,...) custom-call(f32[512,1280]{1,0:T(8,128)} %res_hbm.1, f32[2,1280]{1,0:T(2,128)} %norm_w_in.1, ...), custom_call_target="tpu_custom_call" | custom-call | tf_op jit(solution)/shard_map/mamba_step/pallas_call | solution.py:517
  120.5 0.3 collective-permute-start
  120.8 4.9 %out_proj.2 = f32[256,1280]{1,0:T(8,128)} custom-call(bf16[256,1280]{1,0:T(8,128)(2,1)} %get-tuple-element.14.g_ref, bf16[2,1280,1280]{2,1,0:T(8,128)(2,1)} %w_ref.3), custom_call_target="tpu_custom_call" | custom-call | tf_op jit(solution)/shard_map/out_proj/pallas_call | solution.py:455
  125.7 11.9 %collective-permute-done.g_ref = bf16[256,1280]{1,0:T(8,128)(2,1)} collective-permute-done((bf16[256,1280]{1,0:T(8,128)(2,1)}, bf16[256,1280]{1,0:T(8,128)(2,1)}, u32[]{:S(2)}, u32[]{:S(2)}) %collective-permute-start) | collective-permute-done | bytes 655392 | tf_op jit(solution)/shard_map/ppermute | solution.py:531
  137.5 4.9 %out_proj.3 = f32[256,1280]{1,0:T(8,128)} custom-call(bf16[256,1280]{1,0:T(8,128)(2,1)} %collective-permute-done.g_ref, bf16[2,1280,1280]{2,1,0:T(8,128)(2,1)} %w_ref.3), custom_call_target="tpu_custom_call" | custom-call | tf_op jit(solution)/shard_map/out_proj/pallas_call | solution.py:455
  142.5 0.0 copy-start
  142.5 0.0 copy-start.1
  142.5 1.6 select_convert_fusion
  144.0 0.0 collective-permute-start.1
  144.1 2.1 %collective-permute-done.1 = bf16[256,1280]{1,0:T(8,128)(2,1)S(1)} collective-permute-done((bf16[256,1280]{1,0:T(8,128)(2,1)S(1)}, bf16[256,1280]{1,0:T(8,128)(2,1)S(1)}, u32[]{:S(2)}, u32[]{:S(2)}) %collective-permute-start.1) | collective-permute-done | bytes 655392 | tf_op jit(solution)/shard_map/ppermute | solution.py:537
  146.2 0.0 copy-done
  146.2 0.0 copy-done.1
  146.2 0.2 add_convert_fusion.1
  146.4 0.7 collective-permute-start.2
  147.1 16.1 %collective-permute-done.2 = bf16[256,1280]{1,0:T(8,128)(2,1)S(1)} collective-permute-done((bf16[256,1280]{1,0:T(8,128)(2,1)S(1)}, bf16[256,1280]{1,0:T(8,128)(2,1)S(1)}, u32[]{:S(2)}, u32[]{:S(2)}) %collective-permute-start.2) | collective-permute-done | bytes 655392 | tf_op jit(solution)/shard_map/ppermute | solution.py:538
  163.2 1.0 add_convert_fusion
  164.2 0.0 collective-permute-start.3
  164.2 19.6 %shard_map.148 = (f32[2,256,16,1280]{3,2,1,0:T(8,128)}, bf16[2,3,256,1280]{3,2,1,0:T(8,128)(2,1)}) custom-call(f32[2,256,16,1280]{3,2,1,0:T(8,128)} %bitcast.11, f32[2,256,1280]{2,1,0:T(8,128)} %get-tuple-element.15.dt, bf16[2,256,1280]{2,1,0:T(8,128)(2,1)} %get-tuple-element.16.x, f32[8,2,16,128]{3,2,1,0:T(8,128)} %get-tuple-element.17.bt, ...), custom_call_target="tpu_custom_call" | custom-call | flops 5242880000 | bytes 41943040 | tf_op jit(solution)/shard_map/pallas_call | solution.py:432
  183.8 19.6 %shard_map.149 = (f32[2,256,16,1280]{3,2,1,0:T(8,128)}, bf16[2,3,256,1280]{3,2,1,0:T(8,128)(2,1)}) custom-call(f32[2,256,16,1280]{3,2,1,0:T(8,128)} %bitcast.12, f32[2,256,1280]{2,1,0:T(8,128)} %get-tuple-element.15.dt, bf16[2,256,1280]{2,1,0:T(8,128)(2,1)} %get-tuple-element.16.x, ...), custom_call_target="tpu_custom_call", output_to_operand_aliasing={{0}: (7, {}), {1}: (8, {})} | custom-call | flops 5242880000 | bytes 41943040 | tf_op jit(solution)/shard_map/pallas_call | solution.py:432
  203.3 0.0 copy-start.2
  203.3 0.0 collective-permute-done.3
  203.3 1.5 broadcast_select_fusion.1
  204.9 0.6 copy-done.2
  205.5 1.7 convert_add_fusion
Async XLA Ops:
  120.5 17.1 %collective-permute-start = (bf16[256,1280]{1,0:T(8,128)(2,1)}, bf16[256,1280]{1,0:T(8,128)(2,1)}, u32[]{:S(2)}, u32[]{:S(2)}) collective-permute-start(bf16[256,1280]{1,0:T(8,128)(2,1)} %get-tuple-element.14.g_ref), channel_id=1, source_target_pairs={{0,4},{4,0},{1,5},{5,1},{2,6},{6,2},{3,7},{7,3}} | collective-permute-start | bytes 1966088 | tf_op jit(solution)/shard_map/ppermute | solution.py:531
  142.5 3.7 %copy-start = (f32[256,1280]{1,0:T(8,128)S(1)}, f32[256,1280]{1,0:T(8,128)}, u32[]{:S(2)}) copy-start(f32[256,1280]{1,0:T(8,128)} %out_proj.2) | copy-start | bytes 3932164
  142.5 3.7 %copy-start.1 = (f32[256,1280]{1,0:T(8,128)S(1)}, f32[256,1280]{1,0:T(8,128)}, u32[]{:S(2)}) copy-start(f32[256,1280]{1,0:T(8,128)} %out_proj.3) | copy-start | bytes 3932164
  144.0 2.1 %collective-permute-start.1 = (bf16[256,1280]{1,0:T(8,128)(2,1)S(1)}, bf16[256,1280]{1,0:T(8,128)(2,1)S(1)}, u32[]{:S(2)}, u32[]{:S(2)}) collective-permute-start(bf16[256,1280]{1,0:T(8,128)(2,1)S(1)} %select_convert_fusion), channel_id=1, source_target_pairs={{0,1},{1,0},{2,3},{3,2},{4,5},{5,4},{6,7},{7,6}} | collective-permute-start | bytes 1966088 | tf_op jit(solution)/shard_map/ppermute | solution.py:537
  146.4 16.8 %collective-permute-start.2 = (bf16[256,1280]{1,0:T(8,128)(2,1)S(1)}, bf16[256,1280]{1,0:T(8,128)(2,1)S(1)}, u32[]{:S(2)}, u32[]{:S(2)}) collective-permute-start(bf16[256,1280]{1,0:T(8,128)(2,1)S(1)} %add_convert_fusion.1), channel_id=1, source_target_pairs={{0,2},{2,0},{1,3},{3,1},{4,6},{6,4},{5,7},{7,5}} | collective-permute-start | bytes 1966088 | tf_op jit(solution)/shard_map/ppermute | solution.py:538
  164.2 39.1 %collective-permute-start.3 = (bf16[256,1280]{1,0:T(8,128)(2,1)}, bf16[256,1280]{1,0:T(8,128)(2,1)}, u32[]{:S(2)}, u32[]{:S(2)}) collective-permute-start(bf16[256,1280]{1,0:T(8,128)(2,1)} %add_convert_fusion), channel_id=1, source_target_pairs={{0,1},{1,0},{2,3},{3,2},{4,5},{5,4},{6,7},{7,6}} | collective-permute-start | bytes 1966088 | tf_op jit(solution)/shard_map/ppermute | solution.py:541
  203.3 2.1 %copy-start.2 = (f32[512,1280]{1,0:T(8,128)S(1)}, f32[512,1280]{1,0:T(8,128)}, u32[]{:S(2)}) copy-start(f32[512,1280]{1,0:T(8,128)} %get-tuple-element.13) | copy-start | bytes 7864324

commit v3 on v2

--- a/solution.py
+++ b/solution.py
@@ -17,16 +17,17 @@
 
 
 def step_kernel(dims, res_hbm, norm_w_in, w_in_hbm, conv_w, conv_b_in, w_x, w_dt, dt_bias_in, a_log, d_skip_in, w_out_hbm, conv_hbm, ssm_hbm,
-                r_ref, bt_out, g_out, dt_out, x_out, xi_out,
-                norm_w, conv_b, dt_bias, d_skip, w_in, w_out, a_neg, ssm_buf, conv_buf, h_buf, u_own, z_buf, x_buf, low_buf, dt_buf, dtx_buf, b_bc, c_bc, o_buf,
-                st_send, st_recv, u_send, u_recv, p_own, p_send, p_recv, g_all, cr_send, cr_recv, xs_send, xs_recv, ag_send, ag_recv,
-                in_sem, ssm_in_sem, conv_in_sem, dt_sem, x_sem, xi_sem, go_sem,
-                st_s, st_r, u_s, u_r, p_s, p_r, g_s, g_r, cr_s, cr_r, xs_s, xs_r, ag_s, ag_r):
+                r_ref, bt_out, g_out, o_out, dt_out, x_out, xi_out,
+                norm_w, conv_b, dt_bias, d_skip, w_in, w_out, a_neg, ssm_buf, conv_buf, h_buf, u_own, z_buf, x_buf, low_buf, dt_buf, dtx_buf, b_bc, c_bc, o_buf, hx_buf,
+                st_send, st_recv, u_send, u_recv, p_own, p_send, p_recv, g_all, cr_send, cr_recv, xs_send, xs_recv,
+                in_sem, ssm_in_sem, conv_in_sem, dt_sem, x_sem, xi_sem, go_sem, o_sem,
+                st_s, st_r, u_s, u_r, p_s, p_r, g_s, g_r, cr_s, cr_r, xs_s, xs_r):
     n_layer, rows, d_loc, e_loc, n_state, n_rank, d_model = dims
     half = rows // 2
     n_chunk = N_CHUNK
     blk = half // n_chunk
     total = n_layer * n_chunk
+    n_tile = e_loc // 256
     tx = lax.axis_index("tx")
     ty = lax.axis_index("ty")
     core = lax.rem(ty, 2)
@@ -67,11 +68,11 @@
     def cr_copy(i):
         return remote(cr_send.at[i], cr_recv.at[i], cr_s.at[i], cr_r.at[i], core_peer)
 
-    def xs_copy(i):
-        return remote(xs_send.at[i], xs_recv.at[i], xs_s.at[i], xs_r.at[i], x_peer)
-
-    def ag_copy(i):
-        return remote(ag_send.at[i], ag_recv.at[i], ag_s.at[i], ag_r.at[i], core_peer)
+    def half_rows(h):
+        return pl.ds(pl.multiple_of(h * blk, blk), blk)
+
+    def xs_copy(i, q, h):
+        return remote(xs_send.at[i, half_rows(h)], xs_recv.at[i, half_rows(h)], xs_s.at[i, q], xs_r.at[i, h], (x_peer, d_peer)[q])
 
     def cache_rows(i):
         return pl.ds(pl.multiple_of(chunk_of(i) * blk, blk), blk)
@@ -93,6 +94,9 @@
     def xi_store(i):
         s = lax.rem(i, 2)
         return pltpu.make_async_copy(conv_buf.at[s, 3], xi_out.at[layer_of(i), cache_rows(i)], xi_sem.at[s])
+
+    def o_store(i):
+        return pltpu.make_async_copy(o_buf, o_out.at[cache_rows(i)], o_sem)
 
     def g_store(i):
         return pltpu.make_async_copy(g_all.at[i, pl.ds(0, blk)], g_out.at[cache_rows(i)], go_sem.at[chunk_of(i)])
@@ -138,21 +142,40 @@
                 val = r_ref[pl.ds(base + q * 16, 16), :]
                 h_buf[lo:lo + 16, :] = (val * col[lo:lo + 16] * nw).astype(BF)
 
+        src = lax.broadcasted_iota(jnp.int32, (128, 256), 0)
+        dst = lax.broadcasted_iota(jnp.int32, (128, 256), 1)
+        for k in range(2):
+            spread = jnp.where(dst == 2 * src + k, 1.0, 0.0).astype(BF)
+            for t in range(d_loc // 128):
+                wide = jnp.dot(h_buf[:, t * 128:(t + 1) * 128], spread, preferred_element_type=F32)
+                hx_buf[k * 2 * blk:(k + 1) * 2 * blk, t * 256:(t + 1) * 256] = wide.astype(BF)
+
         @pl.when(i >= 2)
         def _():
+            def done(k, carry):
+                u_copy(i - 2, k).wait_send()
+                return carry
+
+            lax.fori_loop(0, 2 * n_tile, done, 0)
+
+        w_rows = w_in.at[l].reshape(2 * d_loc, e_loc)
+
+        def tile(t, carry):
+            cols = pl.ds(pl.multiple_of(t * 256, 256), 256)
+            u = jnp.dot(hx_buf[...], w_rows[:, cols], preferred_element_type=F32)
             for k in range(2):
-                u_copy(i - 2, k).wait_send()
-
-        for k in range(2):
-            def tile(t, carry):
-                cols = pl.ds(pl.multiple_of(t * 256, 256), 256)
-                u = jnp.dot(h_buf[...], w_in[l, k, :, cols], preferred_element_type=F32)
-                u_own[s, k, :, cols] = u[:blk]
-                u_send[s, k, :, cols] = u[blk:].astype(BF)
-                return carry
-
-            lax.fori_loop(0, e_loc // 256, tile, 0)
-            u_copy(i, k).start()
+                u_own[s, k, :, cols] = u[2 * k * blk:(2 * k + 1) * blk]
+                u_send[s, k * n_tile + t] = u[(2 * k + 1) * blk:(2 * k + 2) * blk].astype(BF)
+            u_copy(i, t).start()
+            return carry
+
+        lax.fori_loop(0, n_tile, tile, 0)
+
+        def send_z(t, carry):
+            u_copy(i, n_tile + t).start()
+            return carry
+
+        lax.fori_loop(0, n_tile, send_z, 0)
 
     def phase_c(i):
         l = layer_of(i)
@@ -168,22 +191,21 @@
                 conv_load(i + 1).start()
 
         conv_load(i).wait()
-        u_copy(i, 0).wait_recv()
-        cb = conv_b[l]
-
-        def rows16(q, carry):
-            rws = pl.ds(pl.multiple_of(q * 16, 16), 16)
-            xi = (u_own[s, 0, rws, :] + u_recv[i, 0, rws, :].astype(F32)).astype(BF)
-            conv_buf[s, 3, rws, :] = xi
-            acc = conv_buf[s, 0, rws, :].astype(F32) * conv_w[l, 0:1, :]
-            acc = acc + conv_buf[s, 1, rws, :].astype(F32) * conv_w[l, 1:2, :]
-            acc = acc + conv_buf[s, 2, rws, :].astype(F32) * conv_w[l, 2:3, :]
-            acc = acc + xi.astype(F32) * conv_w[l, 3:4, :]
-            acc = acc + cb
-            x_buf[rws, :] = (acc * jax.nn.sigmoid(acc)).astype(BF)
-            return carry
-
-        lax.fori_loop(0, blk // 16, rows16, 0)
+
+        def conv_tile(t, carry):
+            u_copy(i, t).wait_recv()
+            cols = pl.ds(pl.multiple_of(t * 256, 256), 256)
+            xi = (u_own[s, 0, :, cols] + u_recv[i, t].astype(F32)).astype(BF)
+            conv_buf[s, 3, :, cols] = xi
+            acc = conv_buf[s, 0, :, cols].astype(F32) * conv_w[l, 0:1, cols]
+            acc = acc + conv_buf[s, 1, :, cols].astype(F32) * conv_w[l, 1:2, cols]
+            acc = acc + conv_buf[s, 2, :, cols].astype(F32) * conv_w[l, 2:3, cols]
+            acc = acc + xi.astype(F32) * conv_w[l, 3:4, cols]
+            acc = acc + conv_b[l, :, cols]
+            x_buf[:, cols] = (acc * jax.nn.sigmoid(acc)).astype(BF)
+            return carry
+
+        lax.fori_loop(0, n_tile, conv_tile, 0)
         xi_store(i).start()
         x_store(i).start()
 
@@ -199,19 +221,18 @@
         for q in range(3):
             p_copy(i, q).start()
 
-        u_copy(i, 1).wait_recv()
-
-        def zrows(q, carry):
-            rws = pl.ds(pl.multiple_of(q * 16, 16), 16)
-            z = (u_own[s, 1, rws, :] + u_recv[i, 1, rws, :].astype(F32)).astype(BF).astype(F32)
-            z_buf[rws, :] = z * jax.nn.sigmoid(z)
-            return carry
-
-        lax.fori_loop(0, blk // 16, zrows, 0)
-
     def phase_d(i):
         l = layer_of(i)
         s = lax.rem(i, 2)
+
+        def z_tile(t, carry):
+            u_copy(i, n_tile + t).wait_recv()
+            cols = pl.ds(pl.multiple_of(t * 256, 256), 256)
+            z = (u_own[s, 1, :, cols] + u_recv[i, n_tile + t].astype(F32)).astype(BF).astype(F32)
+            z_buf[:, cols] = z * jax.nn.sigmoid(z)
+            return carry
+
+        lax.fori_loop(0, n_tile, z_tile, 0)
         for q in range(3):
             p_copy(i, q).wait_recv()
         pt = p_own[...]
@@ -224,8 +245,7 @@
         low_buf[...] = jnp.transpose(unit(pt[:n_rank]))[:blk].astype(BF)
         bt = unit(pt[n_rank:n_rank + n_state])
         ct = unit(pt[n_rank + n_state:])
-        bt_out[i, 0] = bt
-        bt_out[i, 1] = pltpu.roll(bt, 2 * blk - blk // 2, 1)
+        bt_out[i] = bt
         for b in range(blk):
             b_bc[b] = jnp.broadcast_to(bt[:, b:b + 1], (n_state, 128))
             c_bc[b] = jnp.broadcast_to(ct[:, b:b + 1], (n_state, 128))
@@ -272,42 +292,42 @@
         def _():
             g_store(i).start()
 
+            @pl.when(i > total - n_chunk)
+            def _():
+                o_store(i - 1).wait()
+
+            def o_tile(t, carry):
+                cols = pl.ds(pl.multiple_of(t * 256, 256), 256)
+                o_buf[:, cols] = jnp.dot(g_all[i, pl.ds(0, blk)], w_out[l, :, cols], preferred_element_type=F32)
+                return carry
+
+            lax.fori_loop(0, d_loc // 256, o_tile, 0)
+            o_store(i).start()
+
     def phase_e(i):
         l = layer_of(i)
         g_copy(i).wait_recv()
 
         def tile(t, carry):
             cols = pl.ds(pl.multiple_of(t * 256, 256), 256)
-            o_buf[:, cols] = jnp.dot(g_all[i], w_out[l, :, cols], preferred_element_type=F32)
+            cr_send[i, :, cols] = jnp.dot(g_all[i], w_out[l, :, cols], preferred_element_type=F32).astype(BF)
             return carry
 
         lax.fori_loop(0, d_loc // 256, tile, 0)
-        other = pl.multiple_of((1 - core) * blk, blk)
-        cr_send[i] = o_buf[pl.ds(other, blk), :].astype(BF)
         cr_copy(i).start()
 
     def phase_f(i):
         cr_copy(i).wait_recv()
-        mine = pl.multiple_of(core * blk, blk)
-        xs_send[i] = (o_buf[pl.ds(mine, blk), :] + cr_recv[i].astype(F32)).astype(BF)
-        xs_copy(i).start()
+        xs_send[i] = (cr_send[i].astype(F32) + cr_recv[i].astype(F32)).astype(BF)
+        for q in range(2):
+            xs_copy(i, q, core).start()
 
     def phase_g(i):
-        xs_copy(i).wait_recv()
-        tot = (xs_send[i].astype(F32) + xs_recv[i].astype(F32)).astype(BF)
-        ag_send[i] = tot
-        ag_copy(i).start()
-        rws = pl.ds(part_rows(i, core), blk)
-        r_ref[rws, :] = r_ref[rws, :] + tot.astype(F32)
-
-    def phase_h(i):
-        ag_copy(i).wait_recv()
-        rws = pl.ds(part_rows(i, 1 - core), blk)
-        r_ref[rws, :] = r_ref[rws, :] + ag_recv[i].astype(F32)
-
-        @pl.when(i + n_chunk < total)
-        def _():
-            phase_a(i + n_chunk)
+        for h in range(2):
+            xs_copy(i, 0, h).wait_recv()
+            rws = pl.ds(part_rows(i, h), blk)
+            r_ref[rws, :] = r_ref[rws, :] + (xs_send[i, h * blk:(h + 1) * blk].astype(F32) + xs_recv[i, h * blk:(h + 1) * blk].astype(F32))
+        phase_a(i + n_chunk)
 
     for l in range(n_layer):
         for vec, src in ((norm_w, norm_w_in), (conv_b, conv_b_in), (dt_bias, dt_bias_in), (d_skip, d_skip_in)):
@@ -330,6 +350,16 @@
             phase(i)
 
     def step(s, carry):
+        last = total - n_chunk
+        run(phase_g, s - 4, last)
+
+        @pl.when((s >= 2) & (s < total))
+        def _():
+            ssm_load(s).start()
+
+        run(phase_c, s - 1)
+        run(phase_f, s - 3, last)
+
         @pl.when(s == n_chunk)
         def _():
             w_in_load[1].wait()
@@ -345,21 +375,13 @@
             w_out_load.start()
             w_in_load[1].start()
 
-        @pl.when((s >= 2) & (s < total))
-        def _():
-            ssm_load(s).start()
-
-        run(phase_c, s - 1)
+        run(phase_d, s - 1)
 
         @pl.when(s == 2)
         def _():
             w_out_load.wait()
 
-        run(phase_e, s - 2, total - n_chunk)
-        run(phase_g, s - 3, total - n_chunk)
-        run(phase_f, s - 2, total - n_chunk)
-        run(phase_h, s - 3, total - n_chunk)
-        run(phase_d, s - 1)
+        run(phase_e, s - 2, last)
         return carry
 
     lax.fori_loop(0, total + 1, step, 0)
@@ -367,8 +389,9 @@
     xi_store(total - 1).wait()
     x_store(total - 1).wait()
     dt_store(total - 1).wait()
+    o_store(total - 1).wait()
     for i in range(total - 2, total):
-        for k in range(2):
+        for k in range(2 * n_tile):
             u_copy(i, k).wait_send()
         for q in range(3):
             p_copy(i, q).wait_send()
@@ -378,8 +401,8 @@
         st_copy(i + n_chunk).wait_send()
         g_copy(i).wait_send()
         cr_copy(i).wait_send()
-        xs_copy(i).wait_send()
-        ag_copy(i).wait_send()
+        for q in range(2):
+            xs_copy(i, q, core).wait_send()
         g_store(i + total - n_chunk).wait()
         return carry
 
@@ -395,7 +418,7 @@
         a_neg[...] = jnp.exp(a_log[0]) * (-LOG2E)
 
     for b in range(blk):
-        b_bc[b] = jnp.broadcast_to(bt[0, 0, :, b:b + 1], (n_state, 128))
+        b_bc[b] = jnp.broadcast_to(bt[0, :, b:b + 1], (n_state, 128))
     conv_out[0, 0] = conv_in[0, 1]
     conv_out[0, 1] = conv_in[0, 2]
     conv_out[0, 2] = xi[0]
@@ -417,15 +440,14 @@
 
 def state_pass(l, ssm_t, dt, x, bt, a_log_t, conv_t, xi, carried):
     _, half, n_state, e_loc = ssm_t.shape
-    blk = 32
-    per = half // N_CHUNK // blk
+    blk = half // N_CHUNK
 
     def rows_spec(*tail):
         return pl.BlockSpec((1, blk) + tail, lambda g: (l, g) + (0,) * len(tail))
 
     conv_spec = pl.BlockSpec((1, 3, blk, e_loc), lambda g: (l, 0, g, 0))
     in_specs = [rows_spec(n_state, e_loc), rows_spec(e_loc), rows_spec(e_loc),
-                pl.BlockSpec((1, 1, n_state, 128), lambda g: (l * N_CHUNK + g // per, g % per, 0, 0)),
+                pl.BlockSpec((1, n_state, 128), lambda g: (l * N_CHUNK + g, 0, 0)),
                 pl.BlockSpec((1, n_state, e_loc), lambda g: (l, 0, 0)), conv_spec, rows_spec(e_loc)]
     in_specs += [pl.BlockSpec(memory_space=pl.ANY)] * len(carried)
     n_elem = half * n_state * e_loc
@@ -475,17 +497,16 @@
         total = n_layer * N_CHUNK
         blk = rows // 2 // N_CHUNK
         dims = (n_layer, rows, d_loc, e_loc, n_state, n_rank, d_model)
-        w_in_t = jnp.transpose(w_in, (0, 2, 1, 3))
         conv_t = jnp.transpose(conv_state, (0, 3, 1, 2))
         ssm_t = jnp.transpose(ssm_state, (0, 1, 3, 2))
         a_log_t = jnp.transpose(a_log, (0, 2, 1))
-        args = (residual, norm_w, w_in_t, jnp.transpose(conv_w, (0, 2, 1)), conv_b, jnp.transpose(w_x, (0, 2, 1)), w_dt, dt_bias, a_log_t, d_skip, w_out, conv_t, ssm_t)
+        args = (residual, norm_w, w_in, jnp.transpose(conv_w, (0, 2, 1)), conv_b, jnp.transpose(w_x, (0, 2, 1)), w_dt, dt_bias, a_log_t, d_skip, w_out, conv_t, ssm_t)
         hbm = pl.BlockSpec(memory_space=pl.ANY)
         vmem = pl.BlockSpec(memory_space=pltpu.VMEM)
         in_specs = [hbm, vmem, hbm, vmem, vmem, vmem, vmem, vmem, vmem, vmem, hbm, hbm, hbm]
         dma = pltpu.SemaphoreType.DMA
         scratch = [pltpu.VMEM((n_layer, 1, d_loc), F32)] + [pltpu.VMEM((n_layer, 1, e_loc), F32)] * 3 + [
-            pltpu.VMEM((n_layer, 2, d_loc, e_loc), BF),
+            pltpu.VMEM((n_layer, d_loc, 2, e_loc), BF),
             pltpu.VMEM((n_layer, e_loc, d_loc), BF),
             pltpu.VMEM((n_layer, n_state, e_loc), F32),
             pltpu.VMEM((2, blk, n_state, e_loc), F32),
@@ -499,27 +520,28 @@
             pltpu.VMEM((blk, e_loc), F32),
             pltpu.VMEM((blk, n_state, 128), F32),
             pltpu.VMEM((blk, n_state, 128), F32),
-            pltpu.VMEM((2 * blk, d_loc), F32),
+            pltpu.VMEM((blk, d_loc), F32),
+            pltpu.VMEM((4 * blk, 2 * d_loc), BF),
             pltpu.VMEM((total, 8, 2 * blk), F32),
             pltpu.VMEM((total, 8, 2 * blk), F32),
-            pltpu.VMEM((2, 2, blk, e_loc), BF),
-            pltpu.VMEM((total, 2, blk, e_loc), BF),
+            pltpu.VMEM((2, 2 * (e_loc // 256), blk, 256), BF),
+            pltpu.VMEM((total, 2 * (e_loc // 256), blk, 256), BF),
             pltpu.VMEM((n_proj, 2 * blk), F32),
             pltpu.VMEM((2, n_proj, 2 * blk), BF),
             pltpu.VMEM((total, 3, n_proj, 2 * blk), BF),
             pltpu.VMEM((total, 2 * blk, e_loc), BF),
-        ] + [pltpu.VMEM((total, blk, d_loc), BF)] * 6 + [
-            dma((2 + n_layer,)), dma((2,)), dma((2,)), dma(()), dma(()), dma((2,)), dma((N_CHUNK,)),
-            dma((total,)), dma((total,)), dma((2, 2)), dma((total, 2)), dma((2, 3)), dma((total, 3)),
-            dma((total,)), dma((total,)), dma((total,)), dma((total,)), dma((total,)), dma((total,)), dma((total,)), dma((total,)),
+        ] + [pltpu.VMEM((N_CHUNK, 2 * blk, d_loc), BF)] * 4 + [
+            dma((2 + n_layer,)), dma((2,)), dma((2,)), dma(()), dma(()), dma((2,)), dma((N_CHUNK,)), dma(()),
+            dma((total,)), dma((total,)), dma((2, 2 * (e_loc // 256))), dma((total, 2 * (e_loc // 256))), dma((2, 3)), dma((total, 3)),
+            dma((total,)), dma((total,)), dma((N_CHUNK,)), dma((N_CHUNK,)), dma((N_CHUNK, 2)), dma((N_CHUNK, 2)),
         ]
         half = rows // 2
-        r_mid, bt, g_own, dt, x_act, xi = pl.pallas_call(
+        r_mid, bt, g_own, o_own, dt, x_act, xi = pl.pallas_call(
             functools.partial(step_kernel, dims),
-            out_shape=(jax.ShapeDtypeStruct((rows, d_loc), F32), jax.ShapeDtypeStruct((total, 2, n_state, 128), F32), jax.ShapeDtypeStruct((half, e_loc), BF),
+            out_shape=(jax.ShapeDtypeStruct((rows, d_loc), F32), jax.ShapeDtypeStruct((total, n_state, 128), F32), jax.ShapeDtypeStruct((half, e_loc), BF), jax.ShapeDtypeStruct((half, d_loc), F32),
                        jax.ShapeDtypeStruct((n_layer, half, e_loc), F32), jax.ShapeDtypeStruct((n_layer, half, e_loc), BF), jax.ShapeDtypeStruct((n_layer, half, e_loc), BF)),
             in_specs=in_specs,
-            out_specs=(vmem, vmem, hbm, hbm, hbm, hbm),
+            out_specs=(vmem, vmem, hbm, hbm, hbm, hbm, hbm),
             scratch_shapes=scratch,
             compiler_params=pltpu.CompilerParams(collective_id=0, has_side_effects=True, vmem_limit_bytes=67043328),
             name="mamba_step",
@@ -530,7 +552,6 @@
         core_swap = [(0, 1), (1, 0), (2, 3), (3, 2)]
         g_peer = lax.ppermute(g_own, "tx", [(0, 1), (1, 0)])
         caches = state_pass(0, ssm_t, dt, x_act, bt, a_log_t, conv_t, xi, ())
-        o_own = out_proj(g_own, w_out, n_layer - 1)
         o_peer = out_proj(g_peer, w_out, n_layer - 1)
         kept = jnp.where(core == 0, o_own, o_peer)
         sent = jnp.where(core == 0, o_peer, o_own).astype(BF)

time: 207 us -> 193 us (0.932)
  local copies, waits for them, and re-layouts: 13.1 us -> 0.6 us
  Pallas kernels: 156 us -> 149 us
  waiting for transfers between devices: 30.1 us -> 35.2 us
    unnamed x7 -> x6, local copies, waits for them, and re-layouts: 13.1 us -> 0.6 us
    pallas_call x2, Pallas kernels: 39.1 us -> 34.1 us  [state_pass(): pl.pallas_call(functools.partial(state_kernel, len(carried), blk), grid=(...]
    ppermute x1, waiting for transfers between devices: 11.9 us -> 16.9 us  [local_step(): g_peer = lax.ppermute(g_own, 'tx', [(0, 1), (1, 0)])]
    pallas_call x2 -> x1, Pallas kernels: 9.81 us -> 4.91 us  [out_proj(): pl.pallas_call(out_kernel, grid=(1,), out_shape=jax.ShapeDtypeStruct((g.s...]
    pallas_call x1, Pallas kernels: 107 us -> 110 us  [local_step(): pl.pallas_call(functools.partial(step_kernel, dims), out_shape=(jax.Shape...]
  transfers between devices with their start and end apart: 4 -> 4, of which waited for: 3 -> 3; matrix products, arithmetic and copies ran while one was open for 0% -> 0% of each run, Pallas kernels for 21% -> 18%
where the time goes in v3:
time: 193 us
  Pallas kernels  149 us (77%)
  waiting for transfers between devices  35.2 us (18%)
  other arithmetic  6.06 us (3%)
    pallas_call x1, Pallas kernels, local_step(): pl.pallas_call(functools.partial(step_kernel, dims), out_shape=(jax.Shape...  110 us
    pallas_call x2, Pallas kernels, state_pass(): pl.pallas_call(functools.partial(state_kernel, len(carried), blk), grid=(...  34.1 us
    ppermute x1, waiting for transfers between devices, local_step(): g_peer = lax.ppermute(g_own, 'tx', [(0, 1), (1, 0)])  16.9 us
    ppermute x1, waiting for transfers between devices, local_step(): other = lax.ppermute(part, 'ty', [(0, 2), (2, 0), (1, 3), (3, 1)])  16.2 us
    pallas_call x1, Pallas kernels, out_proj(): pl.pallas_call(out_kernel, grid=(1,), out_shape=jax.ShapeDtypeStruct((g.s...  4.91 us
  transfers between devices with their start and end apart: 4, of which 3 were waited for; matrix products, arithmetic and copies ran while one was open for 0% of the time, Pallas kernels for 18%

profile of v3, /device:TPU:0, one launch (start us, length us, event | category | flops | bytes accessed | tf_op | source)
XLA Modules:
  0.0 193.0 jit_solution(13156999962229411647)
XLA Ops:
  0.6 110.4 %mamba_step.1 = (f32[512,1280]{1,0:T(8,128)}, f32[8,16,128]{2,1,0:T(8,128)}, bf16[256,1280]{1,0:T(8,128)(2,1)}, f32[256,1280]{1,0:T(8,128)}, f32[2,256,1280]{2,1...) custom-call(f32[512,1280]{1,0:T(8,128)} %res_hbm.1, f32[2,1280]{1,0:T(2,128)} %norm_w_in.1, ...), custom_call_target="tpu_custom_call" | custom-call | tf_op jit(solution)/shard_map/mamba_step/pallas_call | solution.py:539
  111.0 0.4 collective-permute-start
  111.5 16.9 %collective-permute-done.g_ref = bf16[256,1280]{1,0:T(8,128)(2,1)} collective-permute-done((bf16[256,1280]{1,0:T(8,128)(2,1)}, bf16[256,1280]{1,0:T(8,128)(2,1)}, u32[]{:S(2)}, u32[]{:S(2)}) %collective-permute-start) | collective-permute-done | bytes 655392 | tf_op jit(solution)/shard_map/ppermute | solution.py:553
  128.4 4.9 %out_proj.1 = f32[256,1280]{1,0:T(8,128)} custom-call(bf16[256,1280]{1,0:T(8,128)(2,1)} %collective-permute-done.g_ref, bf16[2,1280,1280]{2,1,0:T(8,128)(2,1)} %w_ref.1), custom_call_target="tpu_custom_call" | custom-call | tf_op jit(solution)/shard_map/out_proj/pallas_call | solution.py:477
  133.3 0.0 copy-start
  133.3 0.0 copy-start.1
  133.3 1.6 select_convert_fusion
  134.9 0.0 collective-permute-start.1
  134.9 2.1 %collective-permute-done.1 = bf16[256,1280]{1,0:T(8,128)(2,1)S(1)} collective-permute-done((bf16[256,1280]{1,0:T(8,128)(2,1)S(1)}, bf16[256,1280]{1,0:T(8,128)(2,1)S(1)}, u32[]{:S(2)}, u32[]{:S(2)}) %collective-permute-start.1) | collective-permute-done | bytes 655392 | tf_op jit(solution)/shard_map/ppermute | solution.py:558
  137.0 0.0 copy-done
  137.0 0.0 copy-done.1
  137.0 0.2 add_convert_fusion.1
  137.2 0.6 collective-permute-start.2
  137.8 16.2 %collective-permute-done.2 = bf16[256,1280]{1,0:T(8,128)(2,1)S(1)} collective-permute-done((bf16[256,1280]{1,0:T(8,128)(2,1)S(1)}, bf16[256,1280]{1,0:T(8,128)(2,1)S(1)}, u32[]{:S(2)}, u32[]{:S(2)}) %collective-permute-start.2) | collective-permute-done | bytes 655392 | tf_op jit(solution)/shard_map/ppermute | solution.py:559
  154.0 1.0 add_convert_fusion
  155.0 0.0 collective-permute-start.3
  155.0 17.1 %shard_map.148 = (f32[2,256,16,1280]{3,2,1,0:T(8,128)}, bf16[2,3,256,1280]{3,2,1,0:T(8,128)(2,1)}) custom-call(f32[2,256,16,1280]{3,2,1,0:T(8,128)} %bitcast.8, f32[2,256,1280]{2,1,0:T(8,128)} %get-tuple-element.17.dt, bf16[2,256,1280]{2,1,0:T(8,128)(2,1)} %get-tuple-element.18.x, f32[8,16,128]{2,1,0:T(8,128)} %get-tuple-element.19.bt, ...), custom_call_target="tpu_custom_call" | custom-call | flops 5242880000 | bytes 41943040 | tf_op jit(solution)/shard_map/pallas_call | solution.py:454
  172.1 17.1 %shard_map.149 = (f32[2,256,16,1280]{3,2,1,0:T(8,128)}, bf16[2,3,256,1280]{3,2,1,0:T(8,128)(2,1)}) custom-call(f32[2,256,16,1280]{3,2,1,0:T(8,128)} %bitcast.9, f32[2,256,1280]{2,1,0:T(8,128)} %get-tuple-element.17.dt, bf16[2,256,1280]{2,1,0:T(8,128)(2,1)} %get-tuple-element.18.x, ...), custom_call_target="tpu_custom_call", output_to_operand_aliasing={{0}: (7, {}), {1}: (8, {})} | custom-call | flops 5242880000 | bytes 41943040 | tf_op jit(solution)/shard_map/pallas_call | solution.py:454
  189.1 0.0 copy-start.2
  189.1 0.0 collective-permute-done.3
  189.1 1.5 broadcast_select_fusion.1
  190.7 0.6 copy-done.2
  191.2 1.7 convert_add_fusion
Async XLA Ops:
  111.0 17.3 %collective-permute-start = (bf16[256,1280]{1,0:T(8,128)(2,1)}, bf16[256,1280]{1,0:T(8,128)(2,1)}, u32[]{:S(2)}, u32[]{:S(2)}) collective-permute-start(bf16[256,1280]{1,0:T(8,128)(2,1)} %get-tuple-element.16), channel_id=1, source_target_pairs={{0,4},{4,0},{1,5},{5,1},{2,6},{6,2},{3,7},{7,3}} | collective-permute-start | bytes 1966088 | tf_op jit(solution)/shard_map/ppermute | solution.py:553
  133.3 3.7 %copy-start = (f32[256,1280]{1,0:T(8,128)S(1)}, f32[256,1280]{1,0:T(8,128)}, u32[]{:S(2)}) copy-start(f32[256,1280]{1,0:T(8,128)} %out_proj.1) | copy-start | bytes 3932164
  133.3 3.7 %copy-start.1 = (f32[256,1280]{1,0:T(8,128)S(1)}, f32[256,1280]{1,0:T(8,128)}, u32[]{:S(2)}) copy-start(f32[256,1280]{1,0:T(8,128)} %get-tuple-element.15) | copy-start | bytes 3932164
  134.9 2.1 %collective-permute-start.1 = (bf16[256,1280]{1,0:T(8,128)(2,1)S(1)}, bf16[256,1280]{1,0:T(8,128)(2,1)S(1)}, u32[]{:S(2)}, u32[]{:S(2)}) collective-permute-start(bf16[256,1280]{1,0:T(8,128)(2,1)S(1)} %select_convert_fusion), channel_id=1, source_target_pairs={{0,1},{1,0},{2,3},{3,2},{4,5},{5,4},{6,7},{7,6}} | collective-permute-start | bytes 1966088 | tf_op jit(solution)/shard_map/ppermute | solution.py:558
  137.2 16.8 %collective-permute-start.2 = (bf16[256,1280]{1,0:T(8,128)(2,1)S(1)}, bf16[256,1280]{1,0:T(8,128)(2,1)S(1)}, u32[]{:S(2)}, u32[]{:S(2)}) collective-permute-start(bf16[256,1280]{1,0:T(8,128)(2,1)S(1)} %add_convert_fusion.1), channel_id=1, source_target_pairs={{0,2},{2,0},{1,3},{3,1},{4,6},{6,4},{5,7},{7,5}} | collective-permute-start | bytes 1966088 | tf_op jit(solution)/shard_map/ppermute | solution.py:559
  155.0 34.1 %collective-permute-start.3 = (bf16[256,1280]{1,0:T(8,128)(2,1)}, bf16[256,1280]{1,0:T(8,128)(2,1)}, u32[]{:S(2)}, u32[]{:S(2)}) collective-permute-start(bf16[256,1280]{1,0:T(8,128)(2,1)} %add_convert_fusion), channel_id=1, source_target_pairs={{0,1},{1,0},{2,3},{3,2},{4,5},{5,4},{6,7},{7,6}} | collective-permute-start | bytes 1966088 | tf_op jit(solution)/shard_map/ppermute | solution.py:562
  189.1 2.1 %copy-start.2 = (f32[512,1280]{1,0:T(8,128)S(1)}, f32[512,1280]{1,0:T(8,128)}, u32[]{:S(2)}) copy-start(f32[512,1280]{1,0:T(8,128)} %get-tuple-element.14) | copy-start | bytes 7864324

commit v4 on v3

--- a/solution.py
+++ b/solution.py
@@ -16,12 +16,28 @@
 MESH = pl.DeviceIdType.MESH
 
 
+def fold_rows(parts):
+    sub = lax.broadcasted_iota(jnp.int32, (8, 128), 0)
+
+    def pair(a, b, shift):
+        low = (sub & shift) == 0
+        p = jnp.where(low, a, b)
+        q = jnp.where(low, b, a)
+        if shift == 4:
+            return p + pltpu.roll(q, 4, 0)
+        return p + jnp.where(low, pltpu.roll(q, 8 - shift, 0), pltpu.roll(q, shift, 0))
+
+    for shift in (4, 2, 1):
+        parts = [pair(parts[b], parts[b + shift], shift) for b in range(shift)]
+    return parts[0]
+
+
 def step_kernel(dims, res_hbm, norm_w_in, w_in_hbm, conv_w, conv_b_in, w_x, w_dt, dt_bias_in, a_log, d_skip_in, w_out_hbm, conv_hbm, ssm_hbm,
                 r_ref, bt_out, g_out, o_out, dt_out, x_out, xi_out,
                 norm_w, conv_b, dt_bias, d_skip, w_in, w_out, a_neg, ssm_buf, conv_buf, h_buf, u_own, z_buf, x_buf, low_buf, dt_buf, dtx_buf, b_bc, c_bc, o_buf, hx_buf,
                 st_send, st_recv, u_send, u_recv, p_own, p_send, p_recv, g_all, cr_send, cr_recv, xs_send, xs_recv,
                 in_sem, ssm_in_sem, conv_in_sem, dt_sem, x_sem, xi_sem, go_sem, o_sem,
-                st_s, st_r, u_s, u_r, p_s, p_r, g_s, g_r, cr_s, cr_r, xs_s, xs_r):
+                st_s, st_r, u_s, u_r, p_s, p_r, g_s, g_r, cr_s, cr_r, xs_s, xs_r, fw_s, fw_r):
     n_layer, rows, d_loc, e_loc, n_state, n_rank, d_model = dims
     half = rows // 2
     n_chunk = N_CHUNK
@@ -36,6 +52,7 @@
     core_peer = {"tx": tx, "ty": chip * 2 + (1 - core)}
     x_peer = {"tx": tx, "ty": (1 - chip) * 2 + core}
     d_peer = {"tx": tx, "ty": (1 - chip) * 2 + (1 - core)}
+    st_peer = {"tx": 1 - tx, "ty": (1 - chip) * 2 + core}
 
     def layer_of(i):
         return lax.div(i, n_chunk)
@@ -51,7 +68,7 @@
         return pltpu.make_async_remote_copy(src_ref=src, dst_ref=dst, send_sem=s_sem, recv_sem=r_sem, device_id=dev, device_id_type=MESH)
 
     def st_copy(i):
-        return remote(st_send.at[i], st_recv.at[i], st_s.at[i], st_r.at[i], y_peer)
+        return remote(st_send.at[i], st_recv.at[i], st_s.at[i], st_r.at[i], st_peer)
 
     def u_copy(i, k):
         s = lax.rem(i, 2)
@@ -71,8 +88,11 @@
     def half_rows(h):
         return pl.ds(pl.multiple_of(h * blk, blk), blk)
 
-    def xs_copy(i, q, h):
-        return remote(xs_send.at[i, half_rows(h)], xs_recv.at[i, half_rows(h)], xs_s.at[i, q], xs_r.at[i, h], (x_peer, d_peer)[q])
+    def xs_copy(i):
+        return remote(xs_send.at[i, half_rows(core)], xs_recv.at[i, half_rows(core)], xs_s.at[i], xs_r.at[i], x_peer)
+
+    def fw_copy(i):
+        return remote(xs_recv.at[i, half_rows(core)], xs_recv.at[i, half_rows(core)], fw_s.at[i], fw_r.at[i], core_peer)
 
     def cache_rows(i):
         return pl.ds(pl.multiple_of(chunk_of(i) * blk, blk), blk)
@@ -86,7 +106,8 @@
         return pltpu.make_async_copy(conv_hbm.at[layer_of(i), :, cache_rows(i)], conv_buf.at[s, pl.ds(0, 3)], conv_in_sem.at[s])
 
     def dt_store(i):
-        return pltpu.make_async_copy(dt_buf, dt_out.at[layer_of(i), cache_rows(i)], dt_sem)
+        n = blk // 8
+        return pltpu.make_async_copy(dt_buf, dt_out.at[layer_of(i), pl.ds(chunk_of(i) * n, n)], dt_sem)
 
     def x_store(i):
         return pltpu.make_async_copy(x_buf, x_out.at[layer_of(i), cache_rows(i)], x_sem)
@@ -109,9 +130,9 @@
     w_in_load[0].start()
 
     barrier = pltpu.get_barrier_semaphore()
-    for dev in (y_peer, core_peer, x_peer, d_peer):
+    for dev in (y_peer, core_peer, x_peer, d_peer, st_peer):
         pl.semaphore_signal(barrier, inc=1, device_id=dev, device_id_type=MESH)
-    pl.semaphore_wait(barrier, 4)
+    pl.semaphore_wait(barrier, 5)
 
     def eye():
         n = 2 * blk
@@ -169,7 +190,7 @@
             u_copy(i, t).start()
             return carry
 
-        lax.fori_loop(0, n_tile, tile, 0)
+        lax.fori_loop(0, n_tile, tile, 0, unroll=True)
 
         def send_z(t, carry):
             u_copy(i, n_tile + t).start()
@@ -205,7 +226,7 @@
             x_buf[:, cols] = (acc * jax.nn.sigmoid(acc)).astype(BF)
             return carry
 
-        lax.fori_loop(0, n_tile, conv_tile, 0)
+        lax.fori_loop(0, n_tile, conv_tile, 0, unroll=True)
         xi_store(i).start()
         x_store(i).start()
 
@@ -215,7 +236,7 @@
                 p_copy(i - 2, q).wait_send()
 
         pt = lax.dot_general(w_x[l], x_buf[...], (((1,), (1,)), ((), ())), preferred_element_type=F32)
-        pt = jnp.concatenate([pt, pt], axis=1)
+        pt = jnp.concatenate([pt[:pt.shape[0] // 2], pt[pt.shape[0] // 2:]], axis=1)
         p_own[...] = pt
         p_send[s] = pt.astype(BF)
         for q in range(3):
@@ -232,12 +253,13 @@
             z_buf[:, cols] = z * jax.nn.sigmoid(z)
             return carry
 
-        lax.fori_loop(0, n_tile, z_tile, 0)
+        lax.fori_loop(0, n_tile, z_tile, 0, unroll=True)
         for q in range(3):
             p_copy(i, q).wait_recv()
         pt = p_own[...]
         for q in range(3):
             pt = pt + p_recv[i, q].astype(F32)
+        pt = jnp.concatenate([pt, pltpu.roll(pt, blk, 1)], axis=0)
 
         def unit(v):
             return v * lax.rsqrt(jnp.mean(v * v, axis=0, keepdims=True) + INNER_EPS)
@@ -259,11 +281,11 @@
             v = jnp.dot(low_buf[...], w_dt[l, :, cols], preferred_element_type=F32)
             v = v + dt_bias[l, :, cols]
             dt = jnp.maximum(v, 0.0) + jnp.log1p(jnp.exp(-jnp.abs(v)))
-            dt_buf[:, cols] = dt
-            dtx_buf[:, cols] = dt * x_buf[:, cols].astype(F32)
+            dt_buf[:, :, cols] = dt.reshape(blk // 8, 8, 256)
+            dtx_buf[:, :, cols] = (dt * x_buf[:, cols].astype(F32)).reshape(blk // 8, 8, 256)
             return carry
 
-        lax.fori_loop(0, e_loc // 256, dt_tile, 0)
+        lax.fori_loop(0, e_loc // 256, dt_tile, 0, unroll=True)
         dt_store(i).start()
         ssm_load(i).wait()
 
@@ -273,10 +295,14 @@
                 a = a_neg[l, :, cols]
                 out = []
                 for p in range(2):
-                    rws = pl.ds(pl.multiple_of(g * 16 + p * 8, 8), 8)
-                    decay = jnp.exp2(dt_buf[rws, cols][:, None, :] * a[None])
-                    new = decay * ssm_buf[s, rws, :, cols] + dtx_buf[rws, cols][:, None, :] * b_bc[rws]
-                    out.append(jnp.sum(new * c_bc[rws], axis=1))
+                    parts = []
+                    for b in range(8):
+                        row = g * 16 + p * 8 + b
+                        decay = jnp.exp2(jnp.broadcast_to(dt_buf[g * 2 + p, b:b + 1, cols], (n_state, 128)) * a)
+                        new = decay * ssm_buf[s, row, :, cols] + jnp.broadcast_to(dtx_buf[g * 2 + p, b:b + 1, cols], (n_state, 128)) * b_bc[row]
+                        term = new * c_bc[row]
+                        parts.append(term[:8] + term[8:])
+                    out.append(fold_rows(parts))
                 rws = pl.ds(pl.multiple_of(g * 16, 16), 16)
                 y = jnp.concatenate(out, axis=0) + d_skip[l, :, cols] * x_buf[rws, cols].astype(F32)
                 g_all[i, rws, cols] = (y * z_buf[rws, cols]).astype(BF)
@@ -301,7 +327,7 @@
                 o_buf[:, cols] = jnp.dot(g_all[i, pl.ds(0, blk)], w_out[l, :, cols], preferred_element_type=F32)
                 return carry
 
-            lax.fori_loop(0, d_loc // 256, o_tile, 0)
+            lax.fori_loop(0, d_loc // 256, o_tile, 0, unroll=True)
             o_store(i).start()
 
     def phase_e(i):
@@ -313,20 +339,24 @@
             cr_send[i, :, cols] = jnp.dot(g_all[i], w_out[l, :, cols], preferred_element_type=F32).astype(BF)
             return carry
 
-        lax.fori_loop(0, d_loc // 256, tile, 0)
+        lax.fori_loop(0, d_loc // 256, tile, 0, unroll=True)
         cr_copy(i).start()
 
     def phase_f(i):
         cr_copy(i).wait_recv()
         xs_send[i] = (cr_send[i].astype(F32) + cr_recv[i].astype(F32)).astype(BF)
-        for q in range(2):
-            xs_copy(i, q, core).start()
+        xs_copy(i).start()
 
     def phase_g(i):
-        for h in range(2):
-            xs_copy(i, 0, h).wait_recv()
+        def add(h):
             rws = pl.ds(part_rows(i, h), blk)
-            r_ref[rws, :] = r_ref[rws, :] + (xs_send[i, h * blk:(h + 1) * blk].astype(F32) + xs_recv[i, h * blk:(h + 1) * blk].astype(F32))
+            r_ref[rws, :] = r_ref[rws, :] + (xs_send[i, half_rows(h), :].astype(F32) + xs_recv[i, half_rows(h), :].astype(F32))
+
+        xs_copy(i).wait_recv()
+        fw_copy(i).start()
+        add(core)
+        fw_copy(i).wait_recv()
+        add(1 - core)
         phase_a(i + n_chunk)
 
     for l in range(n_layer):
@@ -351,7 +381,6 @@
 
     def step(s, carry):
         last = total - n_chunk
-        run(phase_g, s - 4, last)
 
         @pl.when((s >= 2) & (s < total))
         def _():
@@ -381,6 +410,7 @@
         def _():
             w_out_load.wait()
 
+        run(phase_g, s - 3, last)
         run(phase_e, s - 2, last)
         return carry
 
@@ -401,8 +431,8 @@
         st_copy(i + n_chunk).wait_send()
         g_copy(i).wait_send()
         cr_copy(i).wait_send()
-        for q in range(2):
-            xs_copy(i, q, core).wait_send()
+        xs_copy(i).wait_send()
+        fw_copy(i).wait_send()
         g_store(i + total - n_chunk).wait()
         return carry
 
@@ -428,11 +458,13 @@
         for j in range(e_loc // 128):
             cols = slice(j * 128, (j + 1) * 128)
             a = a_neg[:, cols]
-            dtx = dt[0, rws16, cols] * x[0, rws16, cols].astype(F32)
+            x16 = x[0, rws16, cols].astype(F32)
             for p in range(2):
+                dt8 = dt[0, g * 2 + p, :, cols]
+                dtx = dt8 * x16[p * 8:p * 8 + 8]
                 rws = pl.ds(pl.multiple_of(g * 16 + p * 8, 8), 8)
-                decay = jnp.exp2(dt[0, rws, cols][:, None, :] * a[None])
-                ssm_out[0, rws, :, cols] = decay * ssm_in[0, rws, :, cols] + dtx[p * 8:p * 8 + 8][:, None, :] * b_bc[rws]
+                decay = jnp.exp2(dt8[:, None, :] * a[None])
+                ssm_out[0, rws, :, cols] = decay * ssm_in[0, rws, :, cols] + dtx[:, None, :] * b_bc[rws]
         return carry
 
     lax.fori_loop(0, blk // 16, group, 0)
@@ -446,7 +478,7 @@
         return pl.BlockSpec((1, blk) + tail, lambda g: (l, g) + (0,) * len(tail))
 
     conv_spec = pl.BlockSpec((1, 3, blk, e_loc), lambda g: (l, 0, g, 0))
-    in_specs = [rows_spec(n_state, e_loc), rows_spec(e_loc), rows_spec(e_loc),
+    in_specs = [rows_spec(n_state, e_loc), pl.BlockSpec((1, blk // 8, 8, e_loc), lambda g: (l, g, 0, 0)), rows_spec(e_loc),
                 pl.BlockSpec((1, n_state, 128), lambda g: (l * N_CHUNK + g, 0, 0)),
                 pl.BlockSpec((1, n_state, e_loc), lambda g: (l, 0, 0)), conv_spec, rows_spec(e_loc)]
     in_specs += [pl.BlockSpec(memory_space=pl.ANY)] * len(carried)
@@ -516,8 +548,8 @@
             pltpu.VMEM((blk, e_loc), F32),
             pltpu.VMEM((blk, e_loc), BF),
             pltpu.VMEM((blk, n_rank), BF),
-            pltpu.VMEM((blk, e_loc), F32),
-            pltpu.VMEM((blk, e_loc), F32),
+            pltpu.VMEM((blk // 8, 8, e_loc), F32),
+            pltpu.VMEM((blk // 8, 8, e_loc), F32),
             pltpu.VMEM((blk, n_state, 128), F32),
             pltpu.VMEM((blk, n_state, 128), F32),
             pltpu.VMEM((blk, d_loc), F32),
@@ -526,20 +558,20 @@
             pltpu.VMEM((total, 8, 2 * blk), F32),
             pltpu.VMEM((2, 2 * (e_loc // 256), blk, 256), BF),
             pltpu.VMEM((total, 2 * (e_loc // 256), blk, 256), BF),
-            pltpu.VMEM((n_proj, 2 * blk), F32),
-            pltpu.VMEM((2, n_proj, 2 * blk), BF),
-            pltpu.VMEM((total, 3, n_proj, 2 * blk), BF),
+            pltpu.VMEM((n_proj // 2, 2 * blk), F32),
+            pltpu.VMEM((2, n_proj // 2, 2 * blk), BF),
+            pltpu.VMEM((total, 3, n_proj // 2, 2 * blk), BF),
             pltpu.VMEM((total, 2 * blk, e_loc), BF),
         ] + [pltpu.VMEM((N_CHUNK, 2 * blk, d_loc), BF)] * 4 + [
             dma((2 + n_layer,)), dma((2,)), dma((2,)), dma(()), dma(()), dma((2,)), dma((N_CHUNK,)), dma(()),
             dma((total,)), dma((total,)), dma((2, 2 * (e_loc // 256))), dma((total, 2 * (e_loc // 256))), dma((2, 3)), dma((total, 3)),
-            dma((total,)), dma((total,)), dma((N_CHUNK,)), dma((N_CHUNK,)), dma((N_CHUNK, 2)), dma((N_CHUNK, 2)),
+            dma((total,)), dma((total,)), dma((N_CHUNK,)), dma((N_CHUNK,)), dma((N_CHUNK,)), dma((N_CHUNK,)), dma((N_CHUNK,)), dma((N_CHUNK,)),
         ]
         half = rows // 2
         r_mid, bt, g_own, o_own, dt, x_act, xi = pl.pallas_call(
             functools.partial(step_kernel, dims),
             out_shape=(jax.ShapeDtypeStruct((rows, d_loc), F32), jax.ShapeDtypeStruct((total, n_state, 128), F32), jax.ShapeDtypeStruct((half, e_loc), BF), jax.ShapeDtypeStruct((half, d_loc), F32),
-                       jax.ShapeDtypeStruct((n_layer, half, e_loc), F32), jax.ShapeDtypeStruct((n_layer, half, e_loc), BF), jax.ShapeDtypeStruct((n_layer, half, e_loc), BF)),
+                       jax.ShapeDtypeStruct((n_layer, half // 8, 8, e_loc), F32), jax.ShapeDtypeStruct((n_layer, half, e_loc), BF), jax.ShapeDtypeStruct((n_layer, half, e_loc), BF)),
             in_specs=in_specs,
             out_specs=(vmem, vmem, hbm, hbm, hbm, hbm, hbm),
             scratch_shapes=scratch,

time: 193 us -> 185 us (0.959)
  Pallas kernels: 149 us -> 141 us
    pallas_call x1, Pallas kernels: 110 us -> 102 us  [local_step(): pl.pallas_call(functools.partial(step_kernel, dims), out_shape=(jax.Shape...]
where the time goes in v4:
time: 185 us
  Pallas kernels  141 us (76%)
  waiting for transfers between devices  33.4 us (18%)
  other arithmetic  6.06 us (3%)
  starting transfers between devices  2.65 us (1%)
    pallas_call x1, Pallas kernels, local_step(): pl.pallas_call(functools.partial(step_kernel, dims), out_shape=(jax.Shape...  102 us
    pallas_call x2, Pallas kernels, state_pass(): pl.pallas_call(functools.partial(state_kernel, len(carried), blk), grid=(...  34.1 us
    ppermute x1, waiting for transfers between devices, local_step(): g_peer = lax.ppermute(g_own, 'tx', [(0, 1), (1, 0)])  16 us
    ppermute x1, waiting for transfers between devices, local_step(): other = lax.ppermute(part, 'ty', [(0, 2), (2, 0), (1, 3), (3, 1)])  15.3 us
    pallas_call x1, Pallas kernels, out_proj(): pl.pallas_call(out_kernel, grid=(1,), out_shape=jax.ShapeDtypeStruct((g.s...  4.91 us
  transfers between devices with their start and end apart: 4, of which 3 were waited for; matrix products, arithmetic and copies ran while one was open for 0% of the time, Pallas kernels for 18%

profile of v4, /device:TPU:0, one launch (start us, length us, event | category | flops | bytes accessed | tf_op | source)
XLA Modules:
  0.0 184.6 jit_solution(11665494413086329121)
XLA Ops:
  0.6 102.3 %mamba_step.1 = (f32[512,1280]{1,0:T(8,128)}, f32[8,16,128]{2,1,0:T(8,128)}, bf16[256,1280]{1,0:T(8,128)(2,1)}, f32[256,1280]{1,0:T(8,128)}, f32[2,32,8,1280]{3,...) custom-call(f32[512,1280]{1,0:T(8,128)} %res_hbm.1, f32[2,1280]{1,0:T(2,128)} %norm_w_in.1, ...), custom_call_target="tpu_custom_call" | custom-call | tf_op jit(solution)/shard_map/mamba_step/pallas_call | solution.py:571
  102.9 1.1 collective-permute-start
  104.0 16.0 %collective-permute-done.g_ref = bf16[256,1280]{1,0:T(8,128)(2,1)} collective-permute-done((bf16[256,1280]{1,0:T(8,128)(2,1)}, bf16[256,1280]{1,0:T(8,128)(2,1)}, u32[]{:S(2)}, u32[]{:S(2)}) %collective-permute-start) | collective-permute-done | bytes 655392 | tf_op jit(solution)/shard_map/ppermute | solution.py:585
  120.0 4.9 %out_proj.1 = f32[256,1280]{1,0:T(8,128)} custom-call(bf16[256,1280]{1,0:T(8,128)(2,1)} %collective-permute-done.g_ref, bf16[2,1280,1280]{2,1,0:T(8,128)(2,1)} %w_ref.1), custom_call_target="tpu_custom_call" | custom-call | tf_op jit(solution)/shard_map/out_proj/pallas_call | solution.py:509
  124.9 0.0 copy-start
  124.9 0.0 copy-start.1
  124.9 1.6 select_convert_fusion
  126.5 0.0 collective-permute-start.1
  126.5 2.1 %collective-permute-done.1 = bf16[256,1280]{1,0:T(8,128)(2,1)S(1)} collective-permute-done((bf16[256,1280]{1,0:T(8,128)(2,1)S(1)}, bf16[256,1280]{1,0:T(8,128)(2,1)S(1)}, u32[]{:S(2)}, u32[]{:S(2)}) %collective-permute-start.1) | collective-permute-done | bytes 655392 | tf_op jit(solution)/shard_map/ppermute | solution.py:590
  128.6 0.0 copy-done
  128.6 0.0 copy-done.1
  128.6 0.2 add_convert_fusion.1
  128.8 1.5 collective-permute-start.2
  130.3 15.3 %collective-permute-done.2 = bf16[256,1280]{1,0:T(8,128)(2,1)S(1)} collective-permute-done((bf16[256,1280]{1,0:T(8,128)(2,1)S(1)}, bf16[256,1280]{1,0:T(8,128)(2,1)S(1)}, u32[]{:S(2)}, u32[]{:S(2)}) %collective-permute-start.2) | collective-permute-done | bytes 655392 | tf_op jit(solution)/shard_map/ppermute | solution.py:591
  145.6 1.0 add_convert_fusion
  146.6 0.0 collective-permute-start.3
  146.6 17.0 %shard_map.148 = (f32[2,256,16,1280]{3,2,1,0:T(8,128)}, bf16[2,3,256,1280]{3,2,1,0:T(8,128)(2,1)}) custom-call(f32[2,256,16,1280]{3,2,1,0:T(8,128)} %bitcast.8, f32[2,32,8,1280]{3,2,1,0:T(8,128)} %get-tuple-element.17.dt, bf16[2,256,1280]{2,1,0:T(8,128)(2,1)} %get-tuple-element.18.x, f32[8,16,128]{2,1,0:T(8,128)} %get-tuple-element.19.bt, ...), custom_call_target="tpu_custom_call" | custom-call | flops 5242880000 | bytes 41943040 | tf_op jit(solution)/shard_map/pallas_call | solution.py:486
  163.7 17.0 %shard_map.149 = (f32[2,256,16,1280]{3,2,1,0:T(8,128)}, bf16[2,3,256,1280]{3,2,1,0:T(8,128)(2,1)}) custom-call(f32[2,256,16,1280]{3,2,1,0:T(8,128)} %bitcast.9, f32[2,32,8,1280]{3,2,1,0:T(8,128)} %get-tuple-element.17.dt, bf16[2,256,1280]{2,1,0:T(8,128)(2,1)} %get-tuple-element.18.x, ...), custom_call_target="tpu_custom_call", output_to_operand_aliasing={{0}: (7, {}), {1}: (8, {})} | custom-call | flops 5242880000 | bytes 41943040 | tf_op jit(solution)/shard_map/pallas_call | solution.py:486
  180.7 0.0 copy-start.2
  180.7 0.0 collective-permute-done.3
  180.7 1.5 broadcast_select_fusion.1
  182.3 0.6 copy-done.2
  182.9 1.7 convert_add_fusion
Async XLA Ops:
  102.9 17.1 %collective-permute-start = (bf16[256,1280]{1,0:T(8,128)(2,1)}, bf16[256,1280]{1,0:T(8,128)(2,1)}, u32[]{:S(2)}, u32[]{:S(2)}) collective-permute-start(bf16[256,1280]{1,0:T(8,128)(2,1)} %get-tuple-element.16), channel_id=1, source_target_pairs={{0,4},{4,0},{1,5},{5,1},{2,6},{6,2},{3,7},{7,3}} | collective-permute-start | bytes 1966088 | tf_op jit(solution)/shard_map/ppermute | solution.py:585
  124.9 3.7 %copy-start = (f32[256,1280]{1,0:T(8,128)S(1)}, f32[256,1280]{1,0:T(8,128)}, u32[]{:S(2)}) copy-start(f32[256,1280]{1,0:T(8,128)} %out_proj.1) | copy-start | bytes 3932164
  124.9 3.7 %copy-start.1 = (f32[256,1280]{1,0:T(8,128)S(1)}, f32[256,1280]{1,0:T(8,128)}, u32[]{:S(2)}) copy-start(f32[256,1280]{1,0:T(8,128)} %get-tuple-element.15) | copy-start | bytes 3932164
  126.5 2.1 %collective-permute-start.1 = (bf16[256,1280]{1,0:T(8,128)(2,1)S(1)}, bf16[256,1280]{1,0:T(8,128)(2,1)S(1)}, u32[]{:S(2)}, u32[]{:S(2)}) collective-permute-start(bf16[256,1280]{1,0:T(8,128)(2,1)S(1)} %select_convert_fusion), channel_id=1, source_target_pairs={{0,1},{1,0},{2,3},{3,2},{4,5},{5,4},{6,7},{7,6}} | collective-permute-start | bytes 1966088 | tf_op jit(solution)/shard_map/ppermute | solution.py:590
  128.8 16.8 %collective-permute-start.2 = (bf16[256,1280]{1,0:T(8,128)(2,1)S(1)}, bf16[256,1280]{1,0:T(8,128)(2,1)S(1)}, u32[]{:S(2)}, u32[]{:S(2)}) collective-permute-start(bf16[256,1280]{1,0:T(8,128)(2,1)S(1)} %add_convert_fusion.1), channel_id=1, source_target_pairs={{0,2},{2,0},{1,3},{3,1},{4,6},{6,4},{5,7},{7,5}} | collective-permute-start | bytes 1966088 | tf_op jit(solution)/shard_map/ppermute | solution.py:591
  146.6 34.1 %collective-permute-start.3 = (bf16[256,1280]{1,0:T(8,128)(2,1)}, bf16[256,1280]{1,0:T(8,128)(2,1)}, u32[]{:S(2)}, u32[]{:S(2)}) collective-permute-start(bf16[256,1280]{1,0:T(8,128)(2,1)} %add_convert_fusion), channel_id=1, source_target_pairs={{0,1},{1,0},{2,3},{3,2},{4,5},{5,4},{6,7},{7,6}} | collective-permute-start | bytes 1966088 | tf_op jit(solution)/shard_map/ppermute | solution.py:594
  180.7 2.1 %copy-start.2 = (f32[512,1280]{1,0:T(8,128)S(1)}, f32[512,1280]{1,0:T(8,128)}, u32[]{:S(2)}) copy-start(f32[512,1280]{1,0:T(8,128)} %get-tuple-element.14) | copy-start | bytes 7864324

commit v5 on v4

--- a/solution.py
+++ b/solution.py
@@ -11,6 +11,7 @@
 INNER_EPS = 1e-6
 LOG2E = 1.4426950408889634
 N_CHUNK = 4
+U_PARTS = ((0, 3), (3, 5), (5, 10))
 BF = jnp.bfloat16
 F32 = jnp.float32
 MESH = pl.DeviceIdType.MESH
@@ -32,9 +33,9 @@
     return parts[0]
 
 
-def step_kernel(dims, res_hbm, norm_w_in, w_in_hbm, conv_w, conv_b_in, w_x, w_dt, dt_bias_in, a_log, d_skip_in, w_out_hbm, conv_hbm, ssm_hbm,
-                r_ref, bt_out, g_out, o_out, dt_out, x_out, xi_out,
-                norm_w, conv_b, dt_bias, d_skip, w_in, w_out, a_neg, ssm_buf, conv_buf, h_buf, u_own, z_buf, x_buf, low_buf, dt_buf, dtx_buf, b_bc, c_bc, o_buf, hx_buf,
+def step_kernel(dims, res_hbm, norm_w_in, w_in_hbm, conv_w, conv_b_in, w_x_hbm, w_dt_hbm, dt_bias_in, a_log, d_skip_in, w_out_hbm, conv_hbm, ssm_hbm,
+                r_out, bt_out, g_out, o_out, dt_out, x_out, xi_out,
+                r_ref, w_x, w_dt, norm_w, conv_b, dt_bias, d_skip, w_in, w_out, a_neg, ssm_buf, conv_buf, h_buf, u_own, z_buf, x_buf, low_buf, dt_buf, dtx_buf, b_bc, c_bc, o_buf, hx_buf,
                 st_send, st_recv, u_send, u_recv, p_own, p_send, p_recv, g_all, cr_send, cr_recv, xs_send, xs_recv,
                 in_sem, ssm_in_sem, conv_in_sem, dt_sem, x_sem, xi_sem, go_sem, o_sem,
                 st_s, st_r, u_s, u_r, p_s, p_r, g_s, g_r, cr_s, cr_r, xs_s, xs_r, fw_s, fw_r):
@@ -72,7 +73,8 @@
 
     def u_copy(i, k):
         s = lax.rem(i, 2)
-        return remote(u_send.at[s, k], u_recv.at[i, k], u_s.at[s, k], u_r.at[i, k], y_peer)
+        part = pl.ds(U_PARTS[k][0], U_PARTS[k][1] - U_PARTS[k][0])
+        return remote(u_send.at[s, part], u_recv.at[i, part], u_s.at[s, k], u_r.at[i, k], y_peer)
 
     def p_copy(i, q):
         s = lax.rem(i, 2)
@@ -125,6 +127,9 @@
     res_load = pltpu.make_async_copy(res_hbm, r_ref, in_sem.at[0])
     w_in_load = [pltpu.make_async_copy(w_in_hbm.at[l], w_in.at[l], in_sem.at[1 + l]) for l in range(n_layer)]
     w_out_load = pltpu.make_async_copy(w_out_hbm, w_out, in_sem.at[1 + n_layer])
+    w_x_load = pltpu.make_async_copy(w_x_hbm, w_x, in_sem.at[2 + n_layer])
+    w_dt_load = pltpu.make_async_copy(w_dt_hbm, w_dt, in_sem.at[3 + n_layer])
+    r_store = pltpu.make_async_copy(r_ref, r_out, in_sem.at[4 + n_layer])
 
     res_load.start()
     w_in_load[0].start()
@@ -173,30 +178,20 @@
 
         @pl.when(i >= 2)
         def _():
-            def done(k, carry):
+            for k in range(len(U_PARTS)):
                 u_copy(i - 2, k).wait_send()
-                return carry
-
-            lax.fori_loop(0, 2 * n_tile, done, 0)
 
         w_rows = w_in.at[l].reshape(2 * d_loc, e_loc)
 
-        def tile(t, carry):
-            cols = pl.ds(pl.multiple_of(t * 256, 256), 256)
+        for t in range(n_tile):
+            cols = slice(t * 256, (t + 1) * 256)
             u = jnp.dot(hx_buf[...], w_rows[:, cols], preferred_element_type=F32)
             for k in range(2):
                 u_own[s, k, :, cols] = u[2 * k * blk:(2 * k + 1) * blk]
                 u_send[s, k * n_tile + t] = u[(2 * k + 1) * blk:(2 * k + 2) * blk].astype(BF)
-            u_copy(i, t).start()
-            return carry
-
-        lax.fori_loop(0, n_tile, tile, 0, unroll=True)
-
-        def send_z(t, carry):
-            u_copy(i, n_tile + t).start()
-            return carry
-
-        lax.fori_loop(0, n_tile, send_z, 0)
+            for k, (lo, hi) in enumerate(U_PARTS):
+                if (hi - 1 if hi <= n_tile else n_tile - 1) == t:
+                    u_copy(i, k).start()
 
     def phase_c(i):
         l = layer_of(i)
@@ -213,9 +208,11 @@
 
         conv_load(i).wait()
 
-        def conv_tile(t, carry):
-            u_copy(i, t).wait_recv()
-            cols = pl.ds(pl.multiple_of(t * 256, 256), 256)
+        for t in range(n_tile):
+            for k, (lo, hi) in enumerate(U_PARTS):
+                if lo == t:
+                    u_copy(i, k).wait_recv()
+            cols = slice(t * 256, (t + 1) * 256)
             xi = (u_own[s, 0, :, cols] + u_recv[i, t].astype(F32)).astype(BF)
             conv_buf[s, 3, :, cols] = xi
             acc = conv_buf[s, 0, :, cols].astype(F32) * conv_w[l, 0:1, cols]
@@ -224,9 +221,6 @@
             acc = acc + xi.astype(F32) * conv_w[l, 3:4, cols]
             acc = acc + conv_b[l, :, cols]
             x_buf[:, cols] = (acc * jax.nn.sigmoid(acc)).astype(BF)
-            return carry
-
-        lax.fori_loop(0, n_tile, conv_tile, 0, unroll=True)
         xi_store(i).start()
         x_store(i).start()
 
@@ -246,14 +240,13 @@
         l = layer_of(i)
         s = lax.rem(i, 2)
 
-        def z_tile(t, carry):
-            u_copy(i, n_tile + t).wait_recv()
-            cols = pl.ds(pl.multiple_of(t * 256, 256), 256)
+        for t in range(n_tile):
+            for k, (lo, hi) in enumerate(U_PARTS):
+                if lo == n_tile + t:
+                    u_copy(i, k).wait_recv()
+            cols = slice(t * 256, (t + 1) * 256)
             z = (u_own[s, 1, :, cols] + u_recv[i, n_tile + t].astype(F32)).astype(BF).astype(F32)
             z_buf[:, cols] = z * jax.nn.sigmoid(z)
-            return carry
-
-        lax.fori_loop(0, n_tile, z_tile, 0, unroll=True)
         for q in range(3):
             p_copy(i, q).wait_recv()
         pt = p_own[...]
@@ -386,6 +379,11 @@
         def _():
             ssm_load(s).start()
 
+        @pl.when(s == 1)
+        def _():
+            w_x_load.wait()
+            w_dt_load.wait()
+
         run(phase_c, s - 1)
         run(phase_f, s - 3, last)
 
@@ -398,6 +396,8 @@
         @pl.when(s == 0)
         def _():
             conv_load(0).start()
+            w_x_load.start()
+            w_dt_load.start()
             conv_load(1).start()
             ssm_load(0).start()
             ssm_load(1).start()
@@ -405,23 +405,28 @@
             w_in_load[1].start()
 
         run(phase_d, s - 1)
+        run(phase_g, s - 3, last)
+
+        @pl.when(s == n_chunk + 2)
+        def _():
+            r_store.start()
 
         @pl.when(s == 2)
         def _():
             w_out_load.wait()
 
-        run(phase_g, s - 3, last)
         run(phase_e, s - 2, last)
         return carry
 
     lax.fori_loop(0, total + 1, step, 0)
 
+    r_store.wait()
     xi_store(total - 1).wait()
     x_store(total - 1).wait()
     dt_store(total - 1).wait()
     o_store(total - 1).wait()
     for i in range(total - 2, total):
-        for k in range(2 * n_tile):
+        for k in range(len(U_PARTS)):
             u_copy(i, k).wait_send()
         for q in range(3):
             p_copy(i, q).wait_send()
@@ -496,25 +501,33 @@
     )(ssm_t, dt, x, bt, a_log_t, conv_t, xi, *carried)
 
 
-def out_kernel(g_ref, w_ref, o_ref):
-    def tile(t, carry):
-        cols = pl.ds(pl.multiple_of(t * 256, 256), 256)
-        o_ref[:, cols] = jnp.dot(g_ref[...], w_ref[0, :, cols], preferred_element_type=F32)
-        return carry
-
-    lax.fori_loop(0, w_ref.shape[2] // 256, tile, 0)
-
-
-def out_proj(g, w_out, l):
+def out_kernel(l, g_ref, w_hbm, own_ref, kept_ref, sent_ref, w_buf, sem):
+    first = lax.rem(lax.axis_index("ty"), 2) == 0
+    n_tile = own_ref.shape[1] // 256
+    loads = [pltpu.make_async_copy(w_hbm.at[l, :, pl.ds(t * 256, 256)], w_buf.at[t], sem.at[t]) for t in range(n_tile)]
+    for load in loads:
+        load.start()
+    for t in range(n_tile):
+        loads[t].wait()
+        cols = slice(t * 256, (t + 1) * 256)
+        peer = jnp.dot(g_ref[...], w_buf[t], preferred_element_type=F32)
+        own = own_ref[:, cols]
+        kept_ref[:, cols] = jnp.where(first, own, peer)
+        sent_ref[:, cols] = jnp.where(first, peer, own).astype(BF)
+
+
+def out_proj(g, w_out, own, l):
+    vmem = pl.BlockSpec(memory_space=pltpu.VMEM)
+    n_tile = own.shape[1] // 256
     return pl.pallas_call(
-        out_kernel,
-        grid=(1,),
-        out_shape=jax.ShapeDtypeStruct((g.shape[0], w_out.shape[2]), F32),
-        in_specs=[pl.BlockSpec(g.shape, lambda q: (0, 0)), pl.BlockSpec((1,) + w_out.shape[1:], lambda q: (l, 0, 0))],
-        out_specs=pl.BlockSpec((g.shape[0], w_out.shape[2]), lambda q: (0, 0)),
+        functools.partial(out_kernel, l),
+        out_shape=(jax.ShapeDtypeStruct(own.shape, F32), jax.ShapeDtypeStruct(own.shape, BF)),
+        in_specs=[vmem, pl.BlockSpec(memory_space=pl.ANY), vmem],
+        out_specs=(vmem, vmem),
+        scratch_shapes=[pltpu.VMEM((n_tile, w_out.shape[1], 256), BF), pltpu.SemaphoreType.DMA((n_tile,))],
         compiler_params=pltpu.CompilerParams(vmem_limit_bytes=67043328),
         name="out_proj",
-    )(g, w_out)
+    )(g, w_out, own)
 
 
 def solution(mesh):
@@ -535,9 +548,9 @@
         args = (residual, norm_w, w_in, jnp.transpose(conv_w, (0, 2, 1)), conv_b, jnp.transpose(w_x, (0, 2, 1)), w_dt, dt_bias, a_log_t, d_skip, w_out, conv_t, ssm_t)
         hbm = pl.BlockSpec(memory_space=pl.ANY)
         vmem = pl.BlockSpec(memory_space=pltpu.VMEM)
-        in_specs = [hbm, vmem, hbm, vmem, vmem, vmem, vmem, vmem, vmem, vmem, hbm, hbm, hbm]
+        in_specs = [hbm, vmem, hbm, vmem, vmem, hbm, hbm, vmem, vmem, vmem, hbm, hbm, hbm]
         dma = pltpu.SemaphoreType.DMA
-        scratch = [pltpu.VMEM((n_layer, 1, d_loc), F32)] + [pltpu.VMEM((n_layer, 1, e_loc), F32)] * 3 + [
+        scratch = [pltpu.VMEM((rows, d_loc), F32), pltpu.VMEM((n_layer, n_proj, e_loc), BF), pltpu.VMEM((n_layer, n_rank, e_loc), BF), pltpu.VMEM((n_layer, 1, d_loc), F32)] + [pltpu.VMEM((n_layer, 1, e_loc), F32)] * 3 + [
             pltpu.VMEM((n_layer, d_loc, 2, e_loc), BF),
             pltpu.VMEM((n_layer, e_loc, d_loc), BF),
             pltpu.VMEM((n_layer, n_state, e_loc), F32),
@@ -563,8 +576,8 @@
             pltpu.VMEM((total, 3, n_proj // 2, 2 * blk), BF),
             pltpu.VMEM((total, 2 * blk, e_loc), BF),
         ] + [pltpu.VMEM((N_CHUNK, 2 * blk, d_loc), BF)] * 4 + [
-            dma((2 + n_layer,)), dma((2,)), dma((2,)), dma(()), dma(()), dma((2,)), dma((N_CHUNK,)), dma(()),
-            dma((total,)), dma((total,)), dma((2, 2 * (e_loc // 256))), dma((total, 2 * (e_loc // 256))), dma((2, 3)), dma((total, 3)),
+            dma((5 + n_layer,)), dma((2,)), dma((2,)), dma(()), dma(()), dma((2,)), dma((N_CHUNK,)), dma(()),
+            dma((total,)), dma((total,)), dma((2, len(U_PARTS))), dma((total, len(U_PARTS))), dma((2, 3)), dma((total, 3)),
             dma((total,)), dma((total,)), dma((N_CHUNK,)), dma((N_CHUNK,)), dma((N_CHUNK,)), dma((N_CHUNK,)), dma((N_CHUNK,)), dma((N_CHUNK,)),
         ]
         half = rows // 2
@@ -573,7 +586,7 @@
             out_shape=(jax.ShapeDtypeStruct((rows, d_loc), F32), jax.ShapeDtypeStruct((total, n_state, 128), F32), jax.ShapeDtypeStruct((half, e_loc), BF), jax.ShapeDtypeStruct((half, d_loc), F32),
                        jax.ShapeDtypeStruct((n_layer, half // 8, 8, e_loc), F32), jax.ShapeDtypeStruct((n_layer, half, e_loc), BF), jax.ShapeDtypeStruct((n_layer, half, e_loc), BF)),
             in_specs=in_specs,
-            out_specs=(vmem, vmem, hbm, hbm, hbm, hbm, hbm),
+            out_specs=(hbm, vmem, hbm, hbm, hbm, hbm, hbm),
             scratch_shapes=scratch,
             compiler_params=pltpu.CompilerParams(collective_id=0, has_side_effects=True, vmem_limit_bytes=67043328),
             name="mamba_step",
@@ -584,17 +597,16 @@
         core_swap = [(0, 1), (1, 0), (2, 3), (3, 2)]
         g_peer = lax.ppermute(g_own, "tx", [(0, 1), (1, 0)])
         caches = state_pass(0, ssm_t, dt, x_act, bt, a_log_t, conv_t, xi, ())
-        o_peer = out_proj(g_peer, w_out, n_layer - 1)
-        kept = jnp.where(core == 0, o_own, o_peer)
-        sent = jnp.where(core == 0, o_peer, o_own).astype(BF)
+        kept, sent = out_proj(g_peer, w_out, o_own, n_layer - 1)
         part = (kept + lax.ppermute(sent, "ty", core_swap).astype(F32)).astype(BF)
         other = lax.ppermute(part, "ty", [(0, 2), (2, 0), (1, 3), (3, 1)])
+        part_peer = lax.ppermute(part, "ty", core_swap)
         caches = state_pass(1, ssm_t, dt, x_act, bt, a_log_t, conv_t, xi, caches)
-        tot = (part.astype(F32) + other.astype(F32)).astype(BF)
-        tot_peer = lax.ppermute(tot, "ty", core_swap)
-        first = jnp.where(core == tx, tot, tot_peer)
-        second = jnp.where(core == tx, tot_peer, tot)
-        r_out = r_mid + jnp.concatenate([first, second], axis=0).astype(F32)
+        other_peer = lax.ppermute(other, "ty", core_swap)
+        mine = part.astype(F32) + other.astype(F32)
+        theirs = part_peer.astype(F32) + other_peer.astype(F32)
+        same = core == tx
+        r_out = r_mid + jnp.concatenate([jnp.where(same, mine, theirs), jnp.where(same, theirs, mine)], axis=0)
         return r_out, jnp.transpose(caches[1], (0, 2, 3, 1)), jnp.transpose(caches[0], (0, 1, 3, 2))
 
     cache_spec = P(None, ("dp", "tx"), "ty", None)

time: 185 us -> 178 us (0.962)
  Pallas kernels: 141 us -> 134 us
    pallas_call x1, Pallas kernels: 102 us -> 93.7 us  [local_step(): pl.pallas_call(functools.partial(step_kernel, dims), out_shape=(jax.Shape...]
    convert_element_type x2 -> x0, other arithmetic: 2.59 us -> none  [the longest x1 1.59 us: local_step(): sent = jnp.where(core == 0, o_peer, o_own).astype(BF)]
    convert_element_type x1, other arithmetic: 0.21 us -> 2.36 us  [local_step(): part = (kept + lax.ppermute(sent, 'ty', core_swap).astype(F32)).astype(BF)]
  transfers between devices with their start and end apart: 4 -> 5, of which waited for: 3 -> 3; matrix products, arithmetic and copies ran while one was open for 0% -> 0% of each run, Pallas kernels for 18% -> 19%
where the time goes in v5:
time: 178 us
  Pallas kernels  134 us (75%)
  waiting for transfers between devices  34 us (19%)
  other arithmetic  6.33 us (4%)
  starting transfers between devices  2.53 us (1%)
    pallas_call x1, Pallas kernels, local_step(): pl.pallas_call(functools.partial(step_kernel, dims), out_shape=(jax.Shape...  93.7 us
    pallas_call x2, Pallas kernels, state_pass(): pl.pallas_call(functools.partial(state_kernel, len(carried), blk), grid=(...  34.1 us
    ppermute x1, waiting for transfers between devices, local_step(): g_peer = lax.ppermute(g_own, 'tx', [(0, 1), (1, 0)])  15.9 us
    ppermute x1, waiting for transfers between devices, local_step(): other = lax.ppermute(part, 'ty', [(0, 2), (2, 0), (1, 3), (3, 1)])  15.8 us
    pallas_call x1, Pallas kernels, out_proj(): pl.pallas_call(functools.partial(out_kernel, l), out_shape=(jax.ShapeDtyp...  6.22 us
  transfers between devices with their start and end apart: 5, of which 3 were waited for; matrix products, arithmetic and copies ran while one was open for 0% of the time, Pallas kernels for 19%

profile of v5, /device:TPU:0, one launch (start us, length us, event | category | flops | bytes accessed | tf_op | source)
XLA Modules:
  0.0 177.9 jit_solution(14609270508440838343)
XLA Ops:
  0.6 93.7 %mamba_step.1 = (f32[512,1280]{1,0:T(8,128)}, f32[8,16,128]{2,1,0:T(8,128)}, bf16[256,1280]{1,0:T(8,128)(2,1)}, f32[256,1280]{1,0:T(8,128)}, f32[2,32,8,1280]{3,...) custom-call(f32[512,1280]{1,0:T(8,128)} %res_hbm.1, f32[2,1280]{1,0:T(2,128)} %norm_w_in.1, ...), custom_call_target="tpu_custom_call" | custom-call | tf_op jit(solution)/shard_map/mamba_step/pallas_call | solution.py:584
  94.4 1.2 collective-permute-start
  95.6 15.9 %collective-permute-done.g_ref = bf16[256,1280]{1,0:T(8,128)(2,1)} collective-permute-done((bf16[256,1280]{1,0:T(8,128)(2,1)}, bf16[256,1280]{1,0:T(8,128)(2,1)}, u32[]{:S(2)}, u32[]{:S(2)}) %collective-permute-start) | collective-permute-done | bytes 655392 | tf_op jit(solution)/shard_map/ppermute | solution.py:598
  111.5 6.2 %out_proj.1 = (f32[256,1280]{1,0:T(8,128)}, bf16[256,1280]{1,0:T(8,128)(2,1)}) custom-call(bf16[256,1280]{1,0:T(8,128)(2,1)} %collective-permute-done.g_ref, bf16[2,1280,1280]{2,1,0:T(8,128)(2,1)} %w_hbm.1, f32[256,1280]{1,0:T(8,128)} %get-tuple-element.18.own_ref), custom_call_target="tpu_custom_call" | custom-call | tf_op jit(solution)/shard_map/out_proj/pallas_call | solution.py:522
  117.7 0.0 collective-permute-start.1
  117.7 2.3 %collective-permute-done.1 = bf16[256,1280]{1,0:T(8,128)(2,1)S(1)} collective-permute-done((bf16[256,1280]{1,0:T(8,128)(2,1)}, bf16[256,1280]{1,0:T(8,128)(2,1)S(1)}, u32[]{:S(2)}, u32[]{:S(2)}) %collective-permute-start.1) | collective-permute-done | bytes 655392 | tf_op jit(solution)/shard_map/ppermute | solution.py:601
  120.0 2.4 %add_convert_fusion = bf16[256,1280]{1,0:T(8,128)(2,1)} fusion(f32[256,1280]{1,0:T(8,128)} %get-tuple-element.19, bf16[256,1280]{1,0:T(8,128)(2,1)S(1)} %collective-permute-done.1), kind=kLoop, calls=%fused_computation.3 | loop fusion | flops 983040 | bytes 2621440 | tf_op jit(solution)/shard_map/convert_element_type | solution.py:601
  122.4 1.3 collective-permute-start.2
  123.7 0.0 collective-permute-start.3
  123.7 15.8 %collective-permute-done.2 = bf16[256,1280]{1,0:T(8,128)(2,1)} collective-permute-done((bf16[256,1280]{1,0:T(8,128)(2,1)}, bf16[256,1280]{1,0:T(8,128)(2,1)}, u32[]{:S(2)}, u32[]{:S(2)}) %collective-permute-start.2) | collective-permute-done | bytes 655392 | tf_op jit(solution)/shard_map/ppermute | solution.py:602
  139.5 0.0 collective-permute-start.4
  139.5 17.0 %shard_map.148 = (f32[2,256,16,1280]{3,2,1,0:T(8,128)}, bf16[2,3,256,1280]{3,2,1,0:T(8,128)(2,1)}) custom-call(f32[2,256,16,1280]{3,2,1,0:T(8,128)} %bitcast.8, f32[2,32,8,1280]{3,2,1,0:T(8,128)} %get-tuple-element.21.dt, bf16[2,256,1280]{2,1,0:T(8,128)(2,1)} %get-tuple-element.22.x, f32[8,16,128]{2,1,0:T(8,128)} %get-tuple-element.23.bt, ...), custom_call_target="tpu_custom_call" | custom-call | flops 5242880000 | bytes 41943040 | tf_op jit(solution)/shard_map/pallas_call | solution.py:491
  156.5 17.0 %shard_map.149 = (f32[2,256,16,1280]{3,2,1,0:T(8,128)}, bf16[2,3,256,1280]{3,2,1,0:T(8,128)(2,1)}) custom-call(f32[2,256,16,1280]{3,2,1,0:T(8,128)} %bitcast.9, f32[2,32,8,1280]{3,2,1,0:T(8,128)} %get-tuple-element.21.dt, bf16[2,256,1280]{2,1,0:T(8,128)(2,1)} %get-tuple-element.22.x, ...), custom_call_target="tpu_custom_call", output_to_operand_aliasing={{0}: (7, {}), {1}: (8, {})} | custom-call | flops 5242880000 | bytes 41943040 | tf_op jit(solution)/shard_map/pallas_call | solution.py:491
  173.6 0.0 collective-permute-done.3
  173.6 0.0 collective-permute-done.4
  173.6 0.0 copy-start
  173.6 2.2 %fusion.1 = (f32[256,1280]{1,0:T(8,128)S(1)}, f32[256,1280]{1,0:T(8,128)S(1)}) fusion(bf16[256,1280]{1,0:T(8,128)(2,1)} %collective-permute-done.2, bf16[256,1280]{1,0:T(8,128)(2,1)} %add_convert_fusion, bf16[256,1280]{1,0:T(8,128)(2,1)} %collective-permute-done.4, bf16[256,1280]{1,0:T(8,128)(2,1)} %collective-permute-done.3, pred[]{:T(512)S(6)} %eq.3), kind=kLoop, calls=%fused_computation.5 | loop fusion | flops 2621440 | bytes 5242881 | tf_op jit(solution)/shard_map/jit(_where)/select_n | solution.py:609
  175.8 0.3 copy-done
  176.1 1.8 %maximum_add_fusion = f32[512,1280]{1,0:T(8,128)} fusion(f32[512,1280]{1,0:T(8,128)S(1)} %copy-done, f32[256,1280]{1,0:T(8,128)S(1)} %get-tuple-element.30, f32[256,1280]{1,0:T(8,128)S(1)} %get-tuple-element.29), kind=kLoop, calls=%fused_computation | loop fusion | flops 1310720 | bytes 7864320 | tf_op jit(solution)/shard_map/add | solution.py:609
Async XLA Ops:
  94.4 17.1 %collective-permute-start = (bf16[256,1280]{1,0:T(8,128)(2,1)}, bf16[256,1280]{1,0:T(8,128)(2,1)}, u32[]{:S(2)}, u32[]{:S(2)}) collective-permute-start(bf16[256,1280]{1,0:T(8,128)(2,1)} %get-tuple-element.17), channel_id=1, source_target_pairs={{0,4},{4,0},{1,5},{5,1},{2,6},{6,2},{3,7},{7,3}} | collective-permute-start | bytes 1966088 | tf_op jit(solution)/shard_map/ppermute | solution.py:598
  117.7 2.3 %collective-permute-start.1 = (bf16[256,1280]{1,0:T(8,128)(2,1)}, bf16[256,1280]{1,0:T(8,128)(2,1)S(1)}, u32[]{:S(2)}, u32[]{:S(2)}) collective-permute-start(bf16[256,1280]{1,0:T(8,128)(2,1)} %get-tuple-element.20), channel_id=1, source_target_pairs={{0,1},{1,0},{2,3},{3,2},{4,5},{5,4},{6,7},{7,6}} | collective-permute-start | bytes 1966088 | tf_op jit(solution)/shard_map/ppermute | solution.py:601
  122.4 17.1 %collective-permute-start.2 = (bf16[256,1280]{1,0:T(8,128)(2,1)}, bf16[256,1280]{1,0:T(8,128)(2,1)}, u32[]{:S(2)}, u32[]{:S(2)}) collective-permute-start(bf16[256,1280]{1,0:T(8,128)(2,1)} %add_convert_fusion), channel_id=1, source_target_pairs={{0,2},{2,0},{1,3},{3,1},{4,6},{6,4},{5,7},{7,5}} | collective-permute-start | bytes 1966088 | tf_op jit(solution)/shard_map/ppermute | solution.py:602
  123.7 49.9 %collective-permute-start.3 = (bf16[256,1280]{1,0:T(8,128)(2,1)}, bf16[256,1280]{1,0:T(8,128)(2,1)}, u32[]{:S(2)}, u32[]{:S(2)}) collective-permute-start(bf16[256,1280]{1,0:T(8,128)(2,1)} %add_convert_fusion), channel_id=1, source_target_pairs={{0,1},{1,0},{2,3},{3,2},{4,5},{5,4},{6,7},{7,6}} | collective-permute-start | bytes 1966088 | tf_op jit(solution)/shard_map/ppermute | solution.py:603
  139.5 34.1 %collective-permute-start.4 = (bf16[256,1280]{1,0:T(8,128)(2,1)}, bf16[256,1280]{1,0:T(8,128)(2,1)}, u32[]{:S(2)}, u32[]{:S(2)}) collective-permute-start(bf16[256,1280]{1,0:T(8,128)(2,1)} %collective-permute-done.2), channel_id=1, source_target_pairs={{0,1},{1,0},{2,3},{3,2},{4,5},{5,4},{6,7},{7,6}} | collective-permute-start | bytes 1966088 | tf_op jit(solution)/shard_map/ppermute | solution.py:605
  173.6 2.5 %copy-start = (f32[512,1280]{1,0:T(8,128)S(1)}, f32[512,1280]{1,0:T(8,128)}, u32[]{:S(2)}) copy-start(f32[512,1280]{1,0:T(8,128)} %get-tuple-element.16) | copy-start | bytes 7864324

commit v6 on v5

--- a/solution.py
+++ b/solution.py
@@ -501,17 +501,20 @@
     )(ssm_t, dt, x, bt, a_log_t, conv_t, xi, *carried)
 
 
-def out_kernel(l, g_ref, w_hbm, own_ref, kept_ref, sent_ref, w_buf, sem):
+def out_kernel(l, g_ref, w_hbm, own_hbm, kept_ref, sent_ref, w_buf, own_buf, sem, own_sem):
     first = lax.rem(lax.axis_index("ty"), 2) == 0
-    n_tile = own_ref.shape[1] // 256
+    n_tile = kept_ref.shape[1] // 256
     loads = [pltpu.make_async_copy(w_hbm.at[l, :, pl.ds(t * 256, 256)], w_buf.at[t], sem.at[t]) for t in range(n_tile)]
-    for load in loads:
-        load.start()
+    own_loads = [pltpu.make_async_copy(own_hbm.at[:, pl.ds(t * 256, 256)], own_buf.at[t], own_sem.at[t]) for t in range(n_tile)]
+    for t in range(n_tile):
+        loads[t].start()
+        own_loads[t].start()
     for t in range(n_tile):
         loads[t].wait()
         cols = slice(t * 256, (t + 1) * 256)
         peer = jnp.dot(g_ref[...], w_buf[t], preferred_element_type=F32)
-        own = own_ref[:, cols]
+        own_loads[t].wait()
+        own = own_buf[t]
         kept_ref[:, cols] = jnp.where(first, own, peer)
         sent_ref[:, cols] = jnp.where(first, peer, own).astype(BF)
 
@@ -522,10 +525,10 @@
     return pl.pallas_call(
         functools.partial(out_kernel, l),
         out_shape=(jax.ShapeDtypeStruct(own.shape, F32), jax.ShapeDtypeStruct(own.shape, BF)),
-        in_specs=[vmem, pl.BlockSpec(memory_space=pl.ANY), vmem],
+        in_specs=[vmem, pl.BlockSpec(memory_space=pltpu.HBM), pl.BlockSpec(memory_space=pltpu.HBM)],
         out_specs=(vmem, vmem),
-        scratch_shapes=[pltpu.VMEM((n_tile, w_out.shape[1], 256), BF), pltpu.SemaphoreType.DMA((n_tile,))],
-        compiler_params=pltpu.CompilerParams(vmem_limit_bytes=67043328),
+        scratch_shapes=[pltpu.VMEM((n_tile, w_out.shape[1], 256), BF), pltpu.VMEM((n_tile, own.shape[0], 256), F32), pltpu.SemaphoreType.DMA((n_tile,)), pltpu.SemaphoreType.DMA((n_tile,))],
+        compiler_params=pltpu.CompilerParams(vmem_limit_bytes=24 * 2 ** 20),
         name="out_proj",
     )(g, w_out, own)
 
@@ -597,7 +600,7 @@
         core_swap = [(0, 1), (1, 0), (2, 3), (3, 2)]
         g_peer = lax.ppermute(g_own, "tx", [(0, 1), (1, 0)])
         caches = state_pass(0, ssm_t, dt, x_act, bt, a_log_t, conv_t, xi, ())
-        kept, sent = out_proj(g_peer, w_out, o_own, n_layer - 1)
+        kept, sent = out_proj(g_peer, pltpu.with_memory_space_constraint(w_out, pltpu.HBM), pltpu.with_memory_space_constraint(o_own, pltpu.HBM), n_layer - 1)
         part = (kept + lax.ppermute(sent, "ty", core_swap).astype(F32)).astype(BF)
         other = lax.ppermute(part, "ty", [(0, 2), (2, 0), (1, 3), (3, 1)])
         part_peer = lax.ppermute(part, "ty", core_swap)

time: 178 us -> 174 us (0.978)
  Pallas kernels: 134 us -> 131 us
    pallas_call x1, Pallas kernels: 6.22 us -> 3.65 us  [out_proj(): pl.pallas_call(functools.partial(out_kernel, l), out_shape=(jax.ShapeDtyp...]
  transfers between devices with their start and end apart: 5 -> 5, of which waited for: 3 -> 3; matrix products, arithmetic and copies ran while one was open for 0% -> 0% of each run, Pallas kernels for 19% -> 20%
where the time goes in v6:
time: 174 us
  Pallas kernels  131 us (75%)
  waiting for transfers between devices  33.7 us (19%)
  other arithmetic  4.92 us (3%)
  starting transfers between devices  2.53 us (1%)
    pallas_call x1, Pallas kernels, local_step(): pl.pallas_call(functools.partial(step_kernel, dims), out_shape=(jax.Shape...  93.7 us
    pallas_call x2, Pallas kernels, state_pass(): pl.pallas_call(functools.partial(state_kernel, len(carried), blk), grid=(...  34.1 us
    ppermute x1, waiting for transfers between devices, local_step(): g_peer = lax.ppermute(g_own, 'tx', [(0, 1), (1, 0)])  15.8 us
    ppermute x1, waiting for transfers between devices, local_step(): other = lax.ppermute(part, 'ty', [(0, 2), (2, 0), (1, 3), (3, 1)])  15.8 us
    pallas_call x1, Pallas kernels, out_proj(): pl.pallas_call(functools.partial(out_kernel, l), out_shape=(jax.ShapeDtyp...  3.65 us
  transfers between devices with their start and end apart: 5, of which 3 were waited for; matrix products, arithmetic and copies ran while one was open for 0% of the time, Pallas kernels for 20%

profile of v6, /device:TPU:0, one launch (start us, length us, event | category | flops | bytes accessed | tf_op | source)
XLA Modules:
  0.0 173.6 jit_solution(16632211546276725006)
XLA Ops:
  0.6 93.7 %mamba_step.1 = (f32[512,1280]{1,0:T(8,128)}, f32[8,16,128]{2,1,0:T(8,128)}, bf16[256,1280]{1,0:T(8,128)(2,1)}, f32[256,1280]{1,0:T(8,128)}, f32[2,32,8,1280]{3,...) custom-call(f32[512,1280]{1,0:T(8,128)} %res_hbm.1, f32[2,1280]{1,0:T(2,128)} %norm_w_in.1, ...), custom_call_target="tpu_custom_call" | custom-call | tf_op jit(solution)/shard_map/mamba_step/pallas_call | solution.py:587
  94.4 1.2 collective-permute-start
  95.6 15.8 %collective-permute-done.g_ref = bf16[256,1280]{1,0:T(8,128)(2,1)S(1)} collective-permute-done((bf16[256,1280]{1,0:T(8,128)(2,1)}, bf16[256,1280]{1,0:T(8,128)(2,1)S(1)}, u32[]{:S(2)}, u32[]{:S(2)}) %collective-permute-start) | collective-permute-done | bytes 655392 | tf_op jit(solution)/shard_map/ppermute | solution.py:601
  111.4 3.6 %out_proj.1 = (f32[256,1280]{1,0:T(8,128)S(1)}, bf16[256,1280]{1,0:T(8,128)(2,1)S(1)}) custom-call(bf16[256,1280]{1,0:T(8,128)(2,1)S(1)} %collective-permute-done.g_ref, bf16[2,1280,1280]{2,1,0:T(8,128)(2,1)} %w_hbm.1, f32[256,1280]{1,0:T(8,128)} %get-tuple-element.18.own_hbm), custom_call_target="tpu_custom_call" | custom-call | tf_op jit(solution)/shard_map/out_proj/pallas_call | solution.py:525
  115.0 0.0 collective-permute-start.1
  115.1 2.1 %collective-permute-done.1 = bf16[256,1280]{1,0:T(8,128)(2,1)S(1)} collective-permute-done((bf16[256,1280]{1,0:T(8,128)(2,1)S(1)}, bf16[256,1280]{1,0:T(8,128)(2,1)S(1)}, u32[]{:S(2)}, u32[]{:S(2)}) %collective-permute-start.1) | collective-permute-done | bytes 655392 | tf_op jit(solution)/shard_map/ppermute | solution.py:604
  117.1 0.9 add_convert_fusion
  118.1 1.3 collective-permute-start.2
  119.4 0.0 collective-permute-start.3
  119.4 15.8 %collective-permute-done.2 = bf16[256,1280]{1,0:T(8,128)(2,1)} collective-permute-done((bf16[256,1280]{1,0:T(8,128)(2,1)}, bf16[256,1280]{1,0:T(8,128)(2,1)}, u32[]{:S(2)}, u32[]{:S(2)}) %collective-permute-start.2) | collective-permute-done | bytes 655392 | tf_op jit(solution)/shard_map/ppermute | solution.py:605
  135.2 0.0 collective-permute-start.4
  135.2 17.0 %shard_map.148 = (f32[2,256,16,1280]{3,2,1,0:T(8,128)}, bf16[2,3,256,1280]{3,2,1,0:T(8,128)(2,1)}) custom-call(f32[2,256,16,1280]{3,2,1,0:T(8,128)} %bitcast.8, f32[2,32,8,1280]{3,2,1,0:T(8,128)} %get-tuple-element.21.dt, bf16[2,256,1280]{2,1,0:T(8,128)(2,1)} %get-tuple-element.22.x, f32[8,16,128]{2,1,0:T(8,128)} %get-tuple-element.23.bt, ...), custom_call_target="tpu_custom_call" | custom-call | flops 5242880000 | bytes 41943040 | tf_op jit(solution)/shard_map/pallas_call | solution.py:491
  152.2 17.0 %shard_map.149 = (f32[2,256,16,1280]{3,2,1,0:T(8,128)}, bf16[2,3,256,1280]{3,2,1,0:T(8,128)(2,1)}) custom-call(f32[2,256,16,1280]{3,2,1,0:T(8,128)} %bitcast.9, f32[2,32,8,1280]{3,2,1,0:T(8,128)} %get-tuple-element.21.dt, bf16[2,256,1280]{2,1,0:T(8,128)(2,1)} %get-tuple-element.22.x, ...), custom_call_target="tpu_custom_call", output_to_operand_aliasing={{0}: (7, {}), {1}: (8, {})} | custom-call | flops 5242880000 | bytes 41943040 | tf_op jit(solution)/shard_map/pallas_call | solution.py:491
  169.3 0.0 collective-permute-done.3
  169.3 0.0 collective-permute-done.4
  169.3 0.0 copy-start
  169.3 2.2 %fusion.1 = (f32[256,1280]{1,0:T(8,128)S(1)}, f32[256,1280]{1,0:T(8,128)S(1)}) fusion(bf16[256,1280]{1,0:T(8,128)(2,1)} %collective-permute-done.2, bf16[256,1280]{1,0:T(8,128)(2,1)} %add_convert_fusion, bf16[256,1280]{1,0:T(8,128)(2,1)} %collective-permute-done.4, bf16[256,1280]{1,0:T(8,128)(2,1)} %collective-permute-done.3, pred[]{:T(512)S(6)} %eq.3), kind=kLoop, calls=%fused_computation.5 | loop fusion | flops 2621440 | bytes 5242881 | tf_op jit(solution)/shard_map/jit(_where)/select_n | solution.py:612
  171.5 0.3 copy-done
  171.8 1.8 %maximum_add_fusion = f32[512,1280]{1,0:T(8,128)} fusion(f32[512,1280]{1,0:T(8,128)S(1)} %copy-done, f32[256,1280]{1,0:T(8,128)S(1)} %get-tuple-element.30, f32[256,1280]{1,0:T(8,128)S(1)} %get-tuple-element.29), kind=kLoop, calls=%fused_computation | loop fusion | flops 1310720 | bytes 7864320 | tf_op jit(solution)/shard_map/add | solution.py:612
Async XLA Ops:
  94.4 17.0 %collective-permute-start = (bf16[256,1280]{1,0:T(8,128)(2,1)}, bf16[256,1280]{1,0:T(8,128)(2,1)S(1)}, u32[]{:S(2)}, u32[]{:S(2)}) collective-permute-start(bf16[256,1280]{1,0:T(8,128)(2,1)} %get-tuple-element.17), channel_id=1, source_target_pairs={{0,4},{4,0},{1,5},{5,1},{2,6},{6,2},{3,7},{7,3}} | collective-permute-start | bytes 1966088 | tf_op jit(solution)/shard_map/ppermute | solution.py:601
  115.0 2.1 %collective-permute-start.1 = (bf16[256,1280]{1,0:T(8,128)(2,1)S(1)}, bf16[256,1280]{1,0:T(8,128)(2,1)S(1)}, u32[]{:S(2)}, u32[]{:S(2)}) collective-permute-start(bf16[256,1280]{1,0:T(8,128)(2,1)S(1)} %get-tuple-element.20), channel_id=1, source_target_pairs={{0,1},{1,0},{2,3},{3,2},{4,5},{5,4},{6,7},{7,6}} | collective-permute-start | bytes 1966088 | tf_op jit(solution)/shard_map/ppermute | solution.py:604
  118.1 17.1 %collective-permute-start.2 = (bf16[256,1280]{1,0:T(8,128)(2,1)}, bf16[256,1280]{1,0:T(8,128)(2,1)}, u32[]{:S(2)}, u32[]{:S(2)}) collective-permute-start(bf16[256,1280]{1,0:T(8,128)(2,1)} %add_convert_fusion), channel_id=1, source_target_pairs={{0,2},{2,0},{1,3},{3,1},{4,6},{6,4},{5,7},{7,5}} | collective-permute-start | bytes 1966088 | tf_op jit(solution)/shard_map/ppermute | solution.py:605
  119.4 49.9 %collective-permute-start.3 = (bf16[256,1280]{1,0:T(8,128)(2,1)}, bf16[256,1280]{1,0:T(8,128)(2,1)}, u32[]{:S(2)}, u32[]{:S(2)}) collective-permute-start(bf16[256,1280]{1,0:T(8,128)(2,1)} %add_convert_fusion), channel_id=1, source_target_pairs={{0,1},{1,0},{2,3},{3,2},{4,5},{5,4},{6,7},{7,6}} | collective-permute-start | bytes 1966088 | tf_op jit(solution)/shard_map/ppermute | solution.py:606
  135.2 34.1 %collective-permute-start.4 = (bf16[256,1280]{1,0:T(8,128)(2,1)}, bf16[256,1280]{1,0:T(8,128)(2,1)}, u32[]{:S(2)}, u32[]{:S(2)}) collective-permute-start(bf16[256,1280]{1,0:T(8,128)(2,1)} %collective-permute-done.2), channel_id=1, source_target_pairs={{0,1},{1,0},{2,3},{3,2},{4,5},{5,4},{6,7},{7,6}} | collective-permute-start | bytes 1966088 | tf_op jit(solution)/shard_map/ppermute | solution.py:608
  169.3 2.5 %copy-start = (f32[512,1280]{1,0:T(8,128)S(1)}, f32[512,1280]{1,0:T(8,128)}, u32[]{:S(2)}) copy-start(f32[512,1280]{1,0:T(8,128)} %get-tuple-element.16) | copy-start | bytes 7864324

commit v7 on v6

--- a/solution.py
+++ b/solution.py
@@ -34,10 +34,10 @@
 
 
 def step_kernel(dims, res_hbm, norm_w_in, w_in_hbm, conv_w, conv_b_in, w_x_hbm, w_dt_hbm, dt_bias_in, a_log, d_skip_in, w_out_hbm, conv_hbm, ssm_hbm,
-                r_out, bt_out, g_out, o_out, dt_out, x_out, xi_out,
-                r_ref, w_x, w_dt, norm_w, conv_b, dt_bias, d_skip, w_in, w_out, a_neg, ssm_buf, conv_buf, h_buf, u_own, z_buf, x_buf, low_buf, dt_buf, dtx_buf, b_bc, c_bc, o_buf, hx_buf,
+                r_out, bt_out, g_out, dt_out, x_out, xi_out,
+                r_ref, w_x, w_dt, norm_w, conv_b, dt_bias, d_skip, w_in, w_out, a_neg, ssm_buf, conv_buf, h_buf, u_own, z_buf, x_buf, low_buf, dt_buf, dtx_buf, b_bc, c_bc, hx_buf,
                 st_send, st_recv, u_send, u_recv, p_own, p_send, p_recv, g_all, cr_send, cr_recv, xs_send, xs_recv,
-                in_sem, ssm_in_sem, conv_in_sem, dt_sem, x_sem, xi_sem, go_sem, o_sem,
+                in_sem, ssm_in_sem, conv_in_sem, dt_sem, x_sem, xi_sem, go_sem,
                 st_s, st_r, u_s, u_r, p_s, p_r, g_s, g_r, cr_s, cr_r, xs_s, xs_r, fw_s, fw_r):
     n_layer, rows, d_loc, e_loc, n_state, n_rank, d_model = dims
     half = rows // 2
@@ -117,9 +117,6 @@
     def xi_store(i):
         s = lax.rem(i, 2)
         return pltpu.make_async_copy(conv_buf.at[s, 3], xi_out.at[layer_of(i), cache_rows(i)], xi_sem.at[s])
-
-    def o_store(i):
-        return pltpu.make_async_copy(o_buf, o_out.at[cache_rows(i)], o_sem)
 
     def g_store(i):
         return pltpu.make_async_copy(g_all.at[i, pl.ds(0, blk)], g_out.at[cache_rows(i)], go_sem.at[chunk_of(i)])
@@ -311,18 +308,6 @@
         def _():
             g_store(i).start()
 
-            @pl.when(i > total - n_chunk)
-            def _():
-                o_store(i - 1).wait()
-
-            def o_tile(t, carry):
-                cols = pl.ds(pl.multiple_of(t * 256, 256), 256)
-                o_buf[:, cols] = jnp.dot(g_all[i, pl.ds(0, blk)], w_out[l, :, cols], preferred_element_type=F32)
-                return carry
-
-            lax.fori_loop(0, d_loc // 256, o_tile, 0, unroll=True)
-            o_store(i).start()
-
     def phase_e(i):
         l = layer_of(i)
         g_copy(i).wait_recv()
@@ -424,7 +409,6 @@
     xi_store(total - 1).wait()
     x_store(total - 1).wait()
     dt_store(total - 1).wait()
-    o_store(total - 1).wait()
     for i in range(total - 2, total):
         for k in range(len(U_PARTS)):
             u_copy(i, k).wait_send()
@@ -505,32 +489,36 @@
     first = lax.rem(lax.axis_index("ty"), 2) == 0
     n_tile = kept_ref.shape[1] // 256
     loads = [pltpu.make_async_copy(w_hbm.at[l, :, pl.ds(t * 256, 256)], w_buf.at[t], sem.at[t]) for t in range(n_tile)]
-    own_loads = [pltpu.make_async_copy(own_hbm.at[:, pl.ds(t * 256, 256)], own_buf.at[t], own_sem.at[t]) for t in range(n_tile)]
-    for t in range(n_tile):
-        loads[t].start()
-        own_loads[t].start()
+    own_load = pltpu.make_async_copy(own_hbm, own_buf, own_sem)
+    loads[0].start()
+    own_load.start()
+    for load in loads[1:]:
+        load.start()
     for t in range(n_tile):
         loads[t].wait()
+        if t == 0:
+            own_load.wait()
         cols = slice(t * 256, (t + 1) * 256)
         peer = jnp.dot(g_ref[...], w_buf[t], preferred_element_type=F32)
-        own_loads[t].wait()
-        own = own_buf[t]
+        own = jnp.dot(own_buf[...], w_buf[t], preferred_element_type=F32)
         kept_ref[:, cols] = jnp.where(first, own, peer)
         sent_ref[:, cols] = jnp.where(first, peer, own).astype(BF)
 
 
-def out_proj(g, w_out, own, l):
+def out_proj(g, w_out, g_own, l):
     vmem = pl.BlockSpec(memory_space=pltpu.VMEM)
-    n_tile = own.shape[1] // 256
+    hbm = pl.BlockSpec(memory_space=pltpu.HBM)
+    n_rows, d_loc = g.shape[0], w_out.shape[2]
+    n_tile = d_loc // 256
     return pl.pallas_call(
         functools.partial(out_kernel, l),
-        out_shape=(jax.ShapeDtypeStruct(own.shape, F32), jax.ShapeDtypeStruct(own.shape, BF)),
-        in_specs=[vmem, pl.BlockSpec(memory_space=pltpu.HBM), pl.BlockSpec(memory_space=pltpu.HBM)],
+        out_shape=(jax.ShapeDtypeStruct((n_rows, d_loc), F32), jax.ShapeDtypeStruct((n_rows, d_loc), BF)),
+        in_specs=[vmem, hbm, hbm],
         out_specs=(vmem, vmem),
-        scratch_shapes=[pltpu.VMEM((n_tile, w_out.shape[1], 256), BF), pltpu.VMEM((n_tile, own.shape[0], 256), F32), pltpu.SemaphoreType.DMA((n_tile,)), pltpu.SemaphoreType.DMA((n_tile,))],
+        scratch_shapes=[pltpu.VMEM((n_tile, w_out.shape[1], 256), BF), pltpu.VMEM(g_own.shape, BF), pltpu.SemaphoreType.DMA((n_tile,)), pltpu.SemaphoreType.DMA],
         compiler_params=pltpu.CompilerParams(vmem_limit_bytes=24 * 2 ** 20),
         name="out_proj",
-    )(g, w_out, own)
+    )(g, w_out, g_own)
 
 
 def solution(mesh):
@@ -568,7 +556,6 @@
             pltpu.VMEM((blk // 8, 8, e_loc), F32),
             pltpu.VMEM((blk, n_state, 128), F32),
             pltpu.VMEM((blk, n_state, 128), F32),
-            pltpu.VMEM((blk, d_loc), F32),
             pltpu.VMEM((4 * blk, 2 * d_loc), BF),
             pltpu.VMEM((total, 8, 2 * blk), F32),
             pltpu.VMEM((total, 8, 2 * blk), F32),
@@ -579,17 +566,17 @@
             pltpu.VMEM((total, 3, n_proj // 2, 2 * blk), BF),
             pltpu.VMEM((total, 2 * blk, e_loc), BF),
         ] + [pltpu.VMEM((N_CHUNK, 2 * blk, d_loc), BF)] * 4 + [
-            dma((5 + n_layer,)), dma((2,)), dma((2,)), dma(()), dma(()), dma((2,)), dma((N_CHUNK,)), dma(()),
+            dma((5 + n_layer,)), dma((2,)), dma((2,)), dma(()), dma(()), dma((2,)), dma((N_CHUNK,)),
             dma((total,)), dma((total,)), dma((2, len(U_PARTS))), dma((total, len(U_PARTS))), dma((2, 3)), dma((total, 3)),
             dma((total,)), dma((total,)), dma((N_CHUNK,)), dma((N_CHUNK,)), dma((N_CHUNK,)), dma((N_CHUNK,)), dma((N_CHUNK,)), dma((N_CHUNK,)),
         ]
         half = rows // 2
-        r_mid, bt, g_own, o_own, dt, x_act, xi = pl.pallas_call(
+        r_mid, bt, g_own, dt, x_act, xi = pl.pallas_call(
             functools.partial(step_kernel, dims),
-            out_shape=(jax.ShapeDtypeStruct((rows, d_loc), F32), jax.ShapeDtypeStruct((total, n_state, 128), F32), jax.ShapeDtypeStruct((half, e_loc), BF), jax.ShapeDtypeStruct((half, d_loc), F32),
+            out_shape=(jax.ShapeDtypeStruct((rows, d_loc), F32), jax.ShapeDtypeStruct((total, n_state, 128), F32), jax.ShapeDtypeStruct((half, e_loc), BF),
                        jax.ShapeDtypeStruct((n_layer, half // 8, 8, e_loc), F32), jax.ShapeDtypeStruct((n_layer, half, e_loc), BF), jax.ShapeDtypeStruct((n_layer, half, e_loc), BF)),
             in_specs=in_specs,
-            out_specs=(hbm, vmem, hbm, hbm, hbm, hbm, hbm),
+            out_specs=(hbm, vmem, hbm, hbm, hbm, hbm),
             scratch_shapes=scratch,
             compiler_params=pltpu.CompilerParams(collective_id=0, has_side_effects=True, vmem_limit_bytes=67043328),
             name="mamba_step",
@@ -600,7 +587,7 @@
         core_swap = [(0, 1), (1, 0), (2, 3), (3, 2)]
         g_peer = lax.ppermute(g_own, "tx", [(0, 1), (1, 0)])
         caches = state_pass(0, ssm_t, dt, x_act, bt, a_log_t, conv_t, xi, ())
-        kept, sent = out_proj(g_peer, pltpu.with_memory_space_constraint(w_out, pltpu.HBM), pltpu.with_memory_space_constraint(o_own, pltpu.HBM), n_layer - 1)
+        kept, sent = out_proj(g_peer, pltpu.with_memory_space_constraint(w_out, pltpu.HBM), pltpu.with_memory_space_constraint(g_own, pltpu.HBM), n_layer - 1)
         part = (kept + lax.ppermute(sent, "ty", core_swap).astype(F32)).astype(BF)
         other = lax.ppermute(part, "ty", [(0, 2), (2, 0), (1, 3), (3, 1)])
         part_peer = lax.ppermute(part, "ty", core_swap)

time: 174 us -> 173 us (level)
    pallas_call x1, Pallas kernels: 93.7 us -> 91.7 us  [local_step(): pl.pallas_call(functools.partial(step_kernel, dims), out_shape=(jax.Shape...]
where the time goes in v7:
time: 173 us; the launch traced here: 172 us
  Pallas kernels  130 us (75%)
  waiting for transfers between devices  33.4 us (19%)
  other arithmetic  4.95 us (3%)
  starting transfers between devices  2.75 us (2%)
    pallas_call x1, Pallas kernels, local_step(): pl.pallas_call(functools.partial(step_kernel, dims), out_shape=(jax.Shape...  91.7 us
    pallas_call x2, Pallas kernels, state_pass(): pl.pallas_call(functools.partial(state_kernel, len(carried), blk), grid=(...  34.1 us
    ppermute x1, waiting for transfers between devices, local_step(): other = lax.ppermute(part, 'ty', [(0, 2), (2, 0), (1, 3), (3, 1)])  16 us
    ppermute x1, waiting for transfers between devices, local_step(): g_peer = lax.ppermute(g_own, 'tx', [(0, 1), (1, 0)])  15.4 us
    pallas_call x1, Pallas kernels, out_proj(): pl.pallas_call(functools.partial(out_kernel, l), out_shape=(jax.ShapeDtyp...  4.5 us
  transfers between devices with their start and end apart: 5, of which 3 were waited for; matrix products, arithmetic and copies ran while one was open for 0% of the time, Pallas kernels for 20%

profile of v7, /device:TPU:0, one launch (start us, length us, event | category | flops | bytes accessed | tf_op | source)
XLA Modules:
  0.0 172.5 jit_solution(17076759074472998220)
XLA Ops:
  0.6 91.7 %mamba_step.1 = (f32[512,1280]{1,0:T(8,128)}, f32[8,16,128]{2,1,0:T(8,128)}, bf16[256,1280]{1,0:T(8,128)(2,1)}, f32[2,32,8,1280]{3,2,1,0:T(8,128)}, bf16[2,256,1...) custom-call(f32[512,1280]{1,0:T(8,128)} %res_hbm.1, f32[2,1280]{1,0:T(2,128)} %norm_w_in.1, ...), custom_call_target="tpu_custom_call" | custom-call | tf_op jit(solution)/shard_map/mamba_step/pallas_call | solution.py:574
  92.4 1.6 collective-permute-start
  94.0 15.4 %collective-permute-done.g_ref = bf16[256,1280]{1,0:T(8,128)(2,1)S(1)} collective-permute-done((bf16[256,1280]{1,0:T(8,128)(2,1)}, bf16[256,1280]{1,0:T(8,128)(2,1)S(1)}, u32[]{:S(2)}, u32[]{:S(2)}) %collective-permute-start) | collective-permute-done | bytes 655392 | tf_op jit(solution)/shard_map/ppermute | solution.py:588
  109.3 4.5 %out_proj.1 = (f32[256,1280]{1,0:T(8,128)S(1)}, bf16[256,1280]{1,0:T(8,128)(2,1)S(1)}) custom-call(bf16[256,1280]{1,0:T(8,128)(2,1)S(1)} %collective-permute-done.g_ref, bf16[2,1280,1280]{2,1,0:T(8,128)(2,1)} %w_hbm.1, bf16[256,1280]{1,0:T(8,128)(2,1)} %get-tuple-element.16.own_hbm), custom_call_target="tpu_custom_call" | custom-call | tf_op jit(solution)/shard_map/out_proj/pallas_call | solution.py:513
  113.8 0.0 collective-permute-start.1
  113.9 2.1 %collective-permute-done.1 = bf16[256,1280]{1,0:T(8,128)(2,1)S(1)} collective-permute-done((bf16[256,1280]{1,0:T(8,128)(2,1)S(1)}, bf16[256,1280]{1,0:T(8,128)(2,1)S(1)}, u32[]{:S(2)}, u32[]{:S(2)}) %collective-permute-start.1) | collective-permute-done | bytes 655392 | tf_op jit(solution)/shard_map/ppermute | solution.py:591
  116.0 1.0 add_convert_fusion
  116.9 1.1 collective-permute-start.2
  118.1 0.0 collective-permute-start.3
  118.1 16.0 %collective-permute-done.2 = bf16[256,1280]{1,0:T(8,128)(2,1)} collective-permute-done((bf16[256,1280]{1,0:T(8,128)(2,1)}, bf16[256,1280]{1,0:T(8,128)(2,1)}, u32[]{:S(2)}, u32[]{:S(2)}) %collective-permute-start.2) | collective-permute-done | bytes 655392 | tf_op jit(solution)/shard_map/ppermute | solution.py:592
  134.0 0.0 collective-permute-start.4
  134.0 17.0 %shard_map.148 = (f32[2,256,16,1280]{3,2,1,0:T(8,128)}, bf16[2,3,256,1280]{3,2,1,0:T(8,128)(2,1)}) custom-call(f32[2,256,16,1280]{3,2,1,0:T(8,128)} %bitcast.8, f32[2,32,8,1280]{3,2,1,0:T(8,128)} %get-tuple-element.19.dt, bf16[2,256,1280]{2,1,0:T(8,128)(2,1)} %get-tuple-element.20.x, f32[8,16,128]{2,1,0:T(8,128)} %get-tuple-element.21.bt, ...), custom_call_target="tpu_custom_call" | custom-call | flops 5242880000 | bytes 41943040 | tf_op jit(solution)/shard_map/pallas_call | solution.py:475
  151.1 17.0 %shard_map.149 = (f32[2,256,16,1280]{3,2,1,0:T(8,128)}, bf16[2,3,256,1280]{3,2,1,0:T(8,128)(2,1)}) custom-call(f32[2,256,16,1280]{3,2,1,0:T(8,128)} %bitcast.9, f32[2,32,8,1280]{3,2,1,0:T(8,128)} %get-tuple-element.19.dt, bf16[2,256,1280]{2,1,0:T(8,128)(2,1)} %get-tuple-element.20.x, ...), custom_call_target="tpu_custom_call", output_to_operand_aliasing={{0}: (7, {}), {1}: (8, {})} | custom-call | flops 5242880000 | bytes 41943040 | tf_op jit(solution)/shard_map/pallas_call | solution.py:475
  168.1 0.0 collective-permute-done.3
  168.1 0.0 collective-permute-done.4
  168.1 0.0 copy-start
  168.2 2.2 %fusion.1 = (f32[256,1280]{1,0:T(8,128)S(1)}, f32[256,1280]{1,0:T(8,128)S(1)}) fusion(bf16[256,1280]{1,0:T(8,128)(2,1)} %collective-permute-done.2, bf16[256,1280]{1,0:T(8,128)(2,1)} %add_convert_fusion, bf16[256,1280]{1,0:T(8,128)(2,1)} %collective-permute-done.4, bf16[256,1280]{1,0:T(8,128)(2,1)} %collective-permute-done.3, pred[]{:T(512)S(6)} %eq.3), kind=kLoop, calls=%fused_computation.5 | loop fusion | flops 2621440 | bytes 5242881 | tf_op jit(solution)/shard_map/jit(_where)/select_n | solution.py:599
  170.3 0.3 copy-done
  170.7 1.8 %maximum_add_fusion = f32[512,1280]{1,0:T(8,128)} fusion(f32[512,1280]{1,0:T(8,128)S(1)} %copy-done, f32[256,1280]{1,0:T(8,128)S(1)} %get-tuple-element.28, f32[256,1280]{1,0:T(8,128)S(1)} %get-tuple-element.27), kind=kLoop, calls=%fused_computation | loop fusion | flops 1310720 | bytes 7864320 | tf_op jit(solution)/shard_map/add | solution.py:599
Async XLA Ops:
  92.4 17.0 %collective-permute-start = (bf16[256,1280]{1,0:T(8,128)(2,1)}, bf16[256,1280]{1,0:T(8,128)(2,1)S(1)}, u32[]{:S(2)}, u32[]{:S(2)}) collective-permute-start(bf16[256,1280]{1,0:T(8,128)(2,1)} %get-tuple-element.16.own_hbm), channel_id=1, source_target_pairs={{0,4},{4,0},{1,5},{5,1},{2,6},{6,2},{3,7},{7,3}} | collective-permute-start | bytes 1966088 | tf_op jit(solution)/shard_map/ppermute | solution.py:588
  113.8 2.1 %collective-permute-start.1 = (bf16[256,1280]{1,0:T(8,128)(2,1)S(1)}, bf16[256,1280]{1,0:T(8,128)(2,1)S(1)}, u32[]{:S(2)}, u32[]{:S(2)}) collective-permute-start(bf16[256,1280]{1,0:T(8,128)(2,1)S(1)} %get-tuple-element.18), channel_id=1, source_target_pairs={{0,1},{1,0},{2,3},{3,2},{4,5},{5,4},{6,7},{7,6}} | collective-permute-start | bytes 1966088 | tf_op jit(solution)/shard_map/ppermute | solution.py:591
  116.9 17.1 %collective-permute-start.2 = (bf16[256,1280]{1,0:T(8,128)(2,1)}, bf16[256,1280]{1,0:T(8,128)(2,1)}, u32[]{:S(2)}, u32[]{:S(2)}) collective-permute-start(bf16[256,1280]{1,0:T(8,128)(2,1)} %add_convert_fusion), channel_id=1, source_target_pairs={{0,2},{2,0},{1,3},{3,1},{4,6},{6,4},{5,7},{7,5}} | collective-permute-start | bytes 1966088 | tf_op jit(solution)/shard_map/ppermute | solution.py:592
  118.1 50.1 %collective-permute-start.3 = (bf16[256,1280]{1,0:T(8,128)(2,1)}, bf16[256,1280]{1,0:T(8,128)(2,1)}, u32[]{:S(2)}, u32[]{:S(2)}) collective-permute-start(bf16[256,1280]{1,0:T(8,128)(2,1)} %add_convert_fusion), channel_id=1, source_target_pairs={{0,1},{1,0},{2,3},{3,2},{4,5},{5,4},{6,7},{7,6}} | collective-permute-start | bytes 1966088 | tf_op jit(solution)/shard_map/ppermute | solution.py:593
  134.0 34.1 %collective-permute-start.4 = (bf16[256,1280]{1,0:T(8,128)(2,1)}, bf16[256,1280]{1,0:T(8,128)(2,1)}, u32[]{:S(2)}, u32[]{:S(2)}) collective-permute-start(bf16[256,1280]{1,0:T(8,128)(2,1)} %collective-permute-done.2), channel_id=1, source_target_pairs={{0,1},{1,0},{2,3},{3,2},{4,5},{5,4},{6,7},{7,6}} | collective-permute-start | bytes 1966088 | tf_op jit(solution)/shard_map/ppermute | solution.py:595
  168.1 2.5 %copy-start = (f32[512,1280]{1,0:T(8,128)S(1)}, f32[512,1280]{1,0:T(8,128)}, u32[]{:S(2)}) copy-start(f32[512,1280]{1,0:T(8,128)} %get-tuple-element.15) | copy-start | bytes 7864324

commit v8 on v7

--- a/solution.py
+++ b/solution.py
@@ -9,7 +9,6 @@
 
 NORM_EPS = 1e-5
 INNER_EPS = 1e-6
-LOG2E = 1.4426950408889634
 N_CHUNK = 4
 U_PARTS = ((0, 3), (3, 5), (5, 10))
 BF = jnp.bfloat16
@@ -288,7 +287,7 @@
                     parts = []
                     for b in range(8):
                         row = g * 16 + p * 8 + b
-                        decay = jnp.exp2(jnp.broadcast_to(dt_buf[g * 2 + p, b:b + 1, cols], (n_state, 128)) * a)
+                        decay = jnp.exp(jnp.broadcast_to(dt_buf[g * 2 + p, b:b + 1, cols], (n_state, 128)) * a)
                         new = decay * ssm_buf[s, row, :, cols] + jnp.broadcast_to(dtx_buf[g * 2 + p, b:b + 1, cols], (n_state, 128)) * b_bc[row]
                         term = new * c_bc[row]
                         parts.append(term[:8] + term[8:])
@@ -340,7 +339,7 @@
     for l in range(n_layer):
         for vec, src in ((norm_w, norm_w_in), (conv_b, conv_b_in), (dt_bias, dt_bias_in), (d_skip, d_skip_in)):
             vec[l] = src[l:l + 1, :]
-        a_neg[l] = jnp.exp(a_log[l]) * (-LOG2E)
+        a_neg[l] = -jnp.exp(a_log[l])
     res_load.wait()
 
     def first_a(i, carry):
@@ -434,7 +433,7 @@
 
     @pl.when(pl.program_id(0) == 0)
     def _():
-        a_neg[...] = jnp.exp(a_log[0]) * (-LOG2E)
+        a_neg[...] = -jnp.exp(a_log[0])
 
     for b in range(blk):
         b_bc[b] = jnp.broadcast_to(bt[0, :, b:b + 1], (n_state, 128))
@@ -452,7 +451,7 @@
                 dt8 = dt[0, g * 2 + p, :, cols]
                 dtx = dt8 * x16[p * 8:p * 8 + 8]
                 rws = pl.ds(pl.multiple_of(g * 16 + p * 8, 8), 8)
-                decay = jnp.exp2(dt8[:, None, :] * a[None])
+                decay = jnp.exp(dt8[:, None, :] * a[None])
                 ssm_out[0, rws, :, cols] = decay * ssm_in[0, rws, :, cols] + dtx[:, None, :] * b_bc[rws]
         return carry
 

time: 173 us -> 173 us (level)
  no operation moved by 1% of the time
where the time goes in v8:
time: 173 us
  Pallas kernels  131 us (76%)
  waiting for transfers between devices  33 us (19%)
  other arithmetic  4.95 us (3%)
  starting transfers between devices  3.21 us (2%)
    pallas_call x1, Pallas kernels, local_step(): pl.pallas_call(functools.partial(step_kernel, dims), out_shape=(jax.Shape...  91.9 us
    pallas_call x2, Pallas kernels, state_pass(): pl.pallas_call(functools.partial(state_kernel, len(carried), blk), grid=(...  34.8 us
    ppermute x1, waiting for transfers between devices, local_step(): other = lax.ppermute(part, 'ty', [(0, 2), (2, 0), (1, 3), (3, 1)])  15.7 us
    ppermute x1, waiting for transfers between devices, local_step(): g_peer = lax.ppermute(g_own, 'tx', [(0, 1), (1, 0)])  15.2 us
    pallas_call x1, Pallas kernels, out_proj(): pl.pallas_call(functools.partial(out_kernel, l), out_shape=(jax.ShapeDtyp...  4.5 us
  transfers between devices with their start and end apart: 5, of which 3 were waited for; matrix products, arithmetic and copies ran while one was open for 0% of the time, Pallas kernels for 20%

profile of v8, /device:TPU:0, one launch (start us, length us, event | category | flops | bytes accessed | tf_op | source)
XLA Modules:
  0.0 173.3 jit_solution(504064221463625390)
XLA Ops:
  0.6 91.9 %mamba_step.1 = (f32[512,1280]{1,0:T(8,128)}, f32[8,16,128]{2,1,0:T(8,128)}, bf16[256,1280]{1,0:T(8,128)(2,1)}, f32[2,32,8,1280]{3,2,1,0:T(8,128)}, bf16[2,256,1...) custom-call(f32[512,1280]{1,0:T(8,128)} %res_hbm.1, f32[2,1280]{1,0:T(2,128)} %norm_w_in.1, ...), custom_call_target="tpu_custom_call" | custom-call | tf_op jit(solution)/shard_map/mamba_step/pallas_call | solution.py:573
  92.5 1.8 %collective-permute-start = (bf16[256,1280]{1,0:T(8,128)(2,1)}, bf16[256,1280]{1,0:T(8,128)(2,1)S(1)}, u32[]{:S(2)}, u32[]{:S(2)}) collective-permute-start(bf16[256,1280]{1,0:T(8,128)(2,1)} %get-tuple-element.16.own_hbm), channel_id=1, source_target_pairs={{0,4},{4,0},{1,5},{5,1},{2,6},{6,2},{3,7},{7,3}} | collective-permute-start | bytes 1966088 | tf_op jit(solution)/shard_map/ppermute | solution.py:587
  94.3 15.2 %collective-permute-done.g_ref = bf16[256,1280]{1,0:T(8,128)(2,1)S(1)} collective-permute-done((bf16[256,1280]{1,0:T(8,128)(2,1)}, bf16[256,1280]{1,0:T(8,128)(2,1)S(1)}, u32[]{:S(2)}, u32[]{:S(2)}) %collective-permute-start) | collective-permute-done | bytes 655392 | tf_op jit(solution)/shard_map/ppermute | solution.py:587
  109.5 4.5 %out_proj.1 = (f32[256,1280]{1,0:T(8,128)S(1)}, bf16[256,1280]{1,0:T(8,128)(2,1)S(1)}) custom-call(bf16[256,1280]{1,0:T(8,128)(2,1)S(1)} %collective-permute-done.g_ref, bf16[2,1280,1280]{2,1,0:T(8,128)(2,1)} %w_hbm.1, bf16[256,1280]{1,0:T(8,128)(2,1)} %get-tuple-element.16.own_hbm), custom_call_target="tpu_custom_call" | custom-call | tf_op jit(solution)/shard_map/out_proj/pallas_call | solution.py:512
  114.0 0.0 collective-permute-start.1
  114.0 2.1 %collective-permute-done.1 = bf16[256,1280]{1,0:T(8,128)(2,1)S(1)} collective-permute-done((bf16[256,1280]{1,0:T(8,128)(2,1)S(1)}, bf16[256,1280]{1,0:T(8,128)(2,1)S(1)}, u32[]{:S(2)}, u32[]{:S(2)}) %collective-permute-start.1) | collective-permute-done | bytes 655392 | tf_op jit(solution)/shard_map/ppermute | solution.py:590
  116.1 1.0 add_convert_fusion
  117.1 1.4 collective-permute-start.2
  118.5 0.0 collective-permute-start.3
  118.5 15.7 %collective-permute-done.2 = bf16[256,1280]{1,0:T(8,128)(2,1)} collective-permute-done((bf16[256,1280]{1,0:T(8,128)(2,1)}, bf16[256,1280]{1,0:T(8,128)(2,1)}, u32[]{:S(2)}, u32[]{:S(2)}) %collective-permute-start.2) | collective-permute-done | bytes 655392 | tf_op jit(solution)/shard_map/ppermute | solution.py:591
  134.2 0.0 collective-permute-start.4
  134.2 17.4 %shard_map.148 = (f32[2,256,16,1280]{3,2,1,0:T(8,128)}, bf16[2,3,256,1280]{3,2,1,0:T(8,128)(2,1)}) custom-call(f32[2,256,16,1280]{3,2,1,0:T(8,128)} %bitcast.8, f32[2,32,8,1280]{3,2,1,0:T(8,128)} %get-tuple-element.19.dt, bf16[2,256,1280]{2,1,0:T(8,128)(2,1)} %get-tuple-element.20.x, f32[8,16,128]{2,1,0:T(8,128)} %get-tuple-element.21.bt, ...), custom_call_target="tpu_custom_call" | custom-call | flops 5242880000 | bytes 41943040 | tf_op jit(solution)/shard_map/pallas_call | solution.py:474
  151.6 17.4 %shard_map.149 = (f32[2,256,16,1280]{3,2,1,0:T(8,128)}, bf16[2,3,256,1280]{3,2,1,0:T(8,128)(2,1)}) custom-call(f32[2,256,16,1280]{3,2,1,0:T(8,128)} %bitcast.9, f32[2,32,8,1280]{3,2,1,0:T(8,128)} %get-tuple-element.19.dt, bf16[2,256,1280]{2,1,0:T(8,128)(2,1)} %get-tuple-element.20.x, ...), custom_call_target="tpu_custom_call", output_to_operand_aliasing={{0}: (7, {}), {1}: (8, {})} | custom-call | flops 5242880000 | bytes 41943040 | tf_op jit(solution)/shard_map/pallas_call | solution.py:474
  169.0 0.0 collective-permute-done.3
  169.0 0.0 collective-permute-done.4
  169.0 0.0 copy-start
  169.0 2.2 %fusion.1 = (f32[256,1280]{1,0:T(8,128)S(1)}, f32[256,1280]{1,0:T(8,128)S(1)}) fusion(bf16[256,1280]{1,0:T(8,128)(2,1)} %collective-permute-done.2, bf16[256,1280]{1,0:T(8,128)(2,1)} %add_convert_fusion, bf16[256,1280]{1,0:T(8,128)(2,1)} %collective-permute-done.4, bf16[256,1280]{1,0:T(8,128)(2,1)} %collective-permute-done.3, pred[]{:T(512)S(6)} %eq.3), kind=kLoop, calls=%fused_computation.5 | loop fusion | flops 2621440 | bytes 5242881 | tf_op jit(solution)/shard_map/jit(_where)/select_n | solution.py:598
  171.2 0.3 copy-done
  171.5 1.8 %maximum_add_fusion = f32[512,1280]{1,0:T(8,128)} fusion(f32[512,1280]{1,0:T(8,128)S(1)} %copy-done, f32[256,1280]{1,0:T(8,128)S(1)} %get-tuple-element.28, f32[256,1280]{1,0:T(8,128)S(1)} %get-tuple-element.27), kind=kLoop, calls=%fused_computation | loop fusion | flops 1310720 | bytes 7864320 | tf_op jit(solution)/shard_map/add | solution.py:598
Async XLA Ops:
  92.5 17.0 %collective-permute-start = (bf16[256,1280]{1,0:T(8,128)(2,1)}, bf16[256,1280]{1,0:T(8,128)(2,1)S(1)}, u32[]{:S(2)}, u32[]{:S(2)}) collective-permute-start(bf16[256,1280]{1,0:T(8,128)(2,1)} %get-tuple-element.16.own_hbm), channel_id=1, source_target_pairs={{0,4},{4,0},{1,5},{5,1},{2,6},{6,2},{3,7},{7,3}} | collective-permute-start | bytes 1966088 | tf_op jit(solution)/shard_map/ppermute | solution.py:587
  114.0 2.1 %collective-permute-start.1 = (bf16[256,1280]{1,0:T(8,128)(2,1)S(1)}, bf16[256,1280]{1,0:T(8,128)(2,1)S(1)}, u32[]{:S(2)}, u32[]{:S(2)}) collective-permute-start(bf16[256,1280]{1,0:T(8,128)(2,1)S(1)} %get-tuple-element.18), channel_id=1, source_target_pairs={{0,1},{1,0},{2,3},{3,2},{4,5},{5,4},{6,7},{7,6}} | collective-permute-start | bytes 1966088 | tf_op jit(solution)/shard_map/ppermute | solution.py:590
  117.1 17.1 %collective-permute-start.2 = (bf16[256,1280]{1,0:T(8,128)(2,1)}, bf16[256,1280]{1,0:T(8,128)(2,1)}, u32[]{:S(2)}, u32[]{:S(2)}) collective-permute-start(bf16[256,1280]{1,0:T(8,128)(2,1)} %add_convert_fusion), channel_id=1, source_target_pairs={{0,2},{2,0},{1,3},{3,1},{4,6},{6,4},{5,7},{7,5}} | collective-permute-start | bytes 1966088 | tf_op jit(solution)/shard_map/ppermute | solution.py:591
  118.5 50.5 %collective-permute-start.3 = (bf16[256,1280]{1,0:T(8,128)(2,1)}, bf16[256,1280]{1,0:T(8,128)(2,1)}, u32[]{:S(2)}, u32[]{:S(2)}) collective-permute-start(bf16[256,1280]{1,0:T(8,128)(2,1)} %add_convert_fusion), channel_id=1, source_target_pairs={{0,1},{1,0},{2,3},{3,2},{4,5},{5,4},{6,7},{7,6}} | collective-permute-start | bytes 1966088 | tf_op jit(solution)/shard_map/ppermute | solution.py:592
  134.2 34.8 %collective-permute-start.4 = (bf16[256,1280]{1,0:T(8,128)(2,1)}, bf16[256,1280]{1,0:T(8,128)(2,1)}, u32[]{:S(2)}, u32[]{:S(2)}) collective-permute-start(bf16[256,1280]{1,0:T(8,128)(2,1)} %collective-permute-done.2), channel_id=1, source_target_pairs={{0,1},{1,0},{2,3},{3,2},{4,5},{5,4},{6,7},{7,6}} | collective-permute-start | bytes 1966088 | tf_op jit(solution)/shard_map/ppermute | solution.py:594
  169.0 2.5 %copy-start = (f32[512,1280]{1,0:T(8,128)S(1)}, f32[512,1280]{1,0:T(8,128)}, u32[]{:S(2)}) copy-start(f32[512,1280]{1,0:T(8,128)} %get-tuple-element.15) | copy-start | bytes 7864324
